TPU v7x, 32 devices: a whole 2x2x4 slice. The times are simulated.
32 devices in a mesh: dp: 4 (over x, core), fsdp: 8 (over z, y).
Axes of the slice: x: 2, y: 2, z: 4, core: 2. Of those that a mesh axis runs over, the one named last changes fastest.
Arguments:
- inputs: bfloat16 [2, 4, 16, 192, 768], P(None, 'dp', 'fsdp'), may hold values from -6 to 6
- space_in: bfloat16 [768, 2304], P('fsdp'), may hold values from -0.21875 to 0.21875
- space_out: bfloat16 [768, 768], P('fsdp'), may hold values from -1.5 to 1.5
- time_in: bfloat16 [768, 2304], P('fsdp'), may hold values from -0.21875 to 0.21875
- time_out: bfloat16 [768, 768], P('fsdp'), may hold values from -0.4375 to 0.4375
- hidden_in: bfloat16 [768, 3072], P('fsdp'), may hold values from -0.21875 to 0.21875
- hidden_out: bfloat16 [3072, 768], P('fsdp'), may hold values from -0.109375 to 0.109375
- norm_gains: bfloat16 [3, 768], P(None, 'fsdp'), may hold values from 0.5 to 1.5
- cotangent: bfloat16 [2, 4, 16, 192, 768], P(None, 'dp', 'fsdp'), may hold values from -6 to 6
Outputs:
- result: float32 [2, 4, 16, 192, 768], P(None, 'dp', 'fsdp')
- input_grad: float32 [2, 4, 16, 192, 768], P(None, 'dp', 'fsdp')
- grad_space_in: float32 [768, 2304], P('fsdp')
- grad_space_out: float32 [768, 768], P('fsdp')
- grad_time_in: float32 [768, 2304], P('fsdp')
- grad_time_out: float32 [768, 768], P('fsdp')
- grad_hidden_in: float32 [768, 3072], P('fsdp')
- grad_hidden_out: float32 [3072, 768], P('fsdp')
- grad_norm_gains: float32 [3, 768], P(None, 'fsdp')
All inputs are finite; a program needn't handle non-finite values.
Results may differ from a plain program's by a relative error of at most 0.025.
Values may be sent and summed in bfloat16 or wider, within the bound.
A program may use at most 192 MiB of HBM per device.

v0:
```python
import jax
import jax.numpy as jnp
from jax import lax
from jax.sharding import Mesh
from jax.sharding import PartitionSpec as P


D = 768
HEADS = 12
HEAD_DIM = 64
GAIN_COLS = 128

EPS = 1e-06

MEMBERS = ("fsdp", "core")


def layer_norm(values, scales):
    average = jnp.mean(values, axis=-1, keepdims=True)
    centred = values - average
    spread = jnp.mean(centred * centred, axis=-1, keepdims=True)
    return centred * lax.rsqrt(spread + EPS) * scales


def norm_back(values, scales, incoming):
    _, pullback = jax.vjp(layer_norm, values, scales)
    return pullback(incoming)


def flat_dot(left, right):
    flat = left.reshape(-1, left.shape[-1])
    product = jnp.dot(flat, right, preferred_element_type=jnp.float32)
    return product.reshape(left.shape[:-1] + (right.shape[1],))


def back_dot(left, right):
    flat = left.reshape(-1, left.shape[-1])
    product = lax.dot_general(
        flat, right, (((1,), (1,)), ((), ())), preferred_element_type=jnp.float32
    )
    return product.reshape(left.shape[:-1] + (right.shape[0],))


def token_sum(left, right):
    left_rows = left.reshape(-1, left.shape[-1])
    right_rows = right.reshape(-1, right.shape[-1])
    return lax.dot_general(
        left_rows, right_rows, (((0,), (0,)), ((), ())), preferred_element_type=jnp.float32
    )


def split_join(joined):
    split_heads = joined.reshape(joined.shape[:-1] + (3, HEADS, HEAD_DIM))
    return (split_heads[..., 0, :, :], split_heads[..., 1, :, :], split_heads[..., 2, :, :])


def attend_core(normed, weight_in, token_form, key_form, score_form):
    joined = flat_dot(normed, weight_in).astype(jnp.bfloat16)
    queries, keyset, valueset = split_join(joined)
    factor = HEAD_DIM ** (-0.5)
    scores = (
        jnp.einsum(
            token_form + "hd," + key_form + "hd->" + score_form,
            queries,
            keyset,
            preferred_element_type=jnp.float32,
        )
        * factor
    )
    totals = jax.nn.logsumexp(scores, axis=-1, keepdims=True)
    weighting = jnp.exp(scores - totals).astype(jnp.bfloat16)
    context = jnp.einsum(
        score_form + "," + key_form + "hd->" + token_form + "hd",
        weighting,
        valueset,
        preferred_element_type=jnp.float32,
    )
    context = context.reshape(normed.shape[:-1] + (D,)).astype(jnp.bfloat16)
    return (joined, totals, context)


def attend_back(joined, totals, back_context, token_form, key_form, score_form):
    queries, keyset, valueset = split_join(joined)
    back_heads = back_context.reshape(back_context.shape[:-1] + (HEADS, HEAD_DIM))
    factor = HEAD_DIM ** (-0.5)
    scores = (
        jnp.einsum(
            token_form + "hd," + key_form + "hd->" + score_form,
            queries,
            keyset,
            preferred_element_type=jnp.float32,
        )
        * factor
    )
    weighting = jnp.exp(scores - totals)
    back_weight = jnp.einsum(
        token_form + "hd," + key_form + "hd->" + score_form,
        back_heads,
        valueset,
        preferred_element_type=jnp.float32,
    )
    back_weight = back_weight.astype(jnp.bfloat16).astype(jnp.float32)
    inner_sum = jnp.sum(weighting * back_weight, axis=-1, keepdims=True)
    back_scores = (weighting * (back_weight - inner_sum)).astype(jnp.bfloat16)
    back_query = (
        jnp.einsum(
            score_form + "," + key_form + "hd->" + token_form + "hd",
            back_scores,
            keyset,
            preferred_element_type=jnp.float32,
        )
        * factor
    )
    back_keys = (
        jnp.einsum(
            score_form + "," + token_form + "hd->" + key_form + "hd",
            back_scores,
            queries,
            preferred_element_type=jnp.float32,
        )
        * factor
    )
    back_values = jnp.einsum(
        score_form + "," + token_form + "hd->" + key_form + "hd",
        weighting.astype(jnp.bfloat16),
        back_heads,
        preferred_element_type=jnp.float32,
    )
    shape = back_context.shape[:-1] + (D,)
    return tuple(
        part.reshape(shape).astype(jnp.bfloat16) for part in (back_query, back_keys, back_values)
    )


def join_sum(normed, parts):
    return jnp.concatenate([token_sum(normed, part) for part in parts], axis=1)


def join_back(parts, weight_in):
    total = None
    for index, part in enumerate(parts):
        term = back_dot(part, weight_in[:, index * D:(index + 1) * D])
        total = term if total is None else total + term
    return total


SQRT_HALF = 0.5 ** 0.5


def gelu_parts(hidden):
    tail = lax.erfc(-hidden * SQRT_HALF)
    return 0.5 * hidden * tail, tail


def gelu_back(hidden, tail, incoming):
    slope = 0.5 * tail + hidden * (SQRT_HALF / jnp.sqrt(jnp.pi)) * jnp.exp(-0.5 * hidden * hidden)
    return incoming * slope


def to_member(array, kind, part, half):
    if kind == "gains":
        gain_part = lax.dynamic_slice_in_dim(array, part * half, half, axis=1).T
        return jnp.pad(gain_part, ((0, 0), (0, GAIN_COLS - gain_part.shape[1])))
    if kind == "grouped":
        rows = lax.dynamic_slice_in_dim(array, part * 4 * half, 4 * half, axis=0)
        return jnp.concatenate([rows[q * half:(q + 1) * half] for q in range(4)], axis=1)
    return lax.dynamic_slice_in_dim(array, part * half, half, axis=0)


def width_of(array, kind):
    return {"gains": GAIN_COLS, "grouped": 4 * D}.get(kind, array.shape[-1])


def from_members(block, kinds, widths, half):
    members = block.shape[0] // half
    outs = []
    offset = 0
    for kind, width in zip(kinds, widths):
        part = block[:, offset:offset + width]
        offset += width
        if kind == "gains":
            outs.append(part[:, :3].T)
        elif kind == "grouped":
            grouped = part.reshape(members, half, 4 * D)
            outs.append(
                jnp.concatenate([grouped[:, :, q * D:(q + 1) * D] for q in range(4)], axis=1).reshape(
                    members * 4 * half, D
                )
            )
        else:
            outs.append(part)
    return outs


def to_members_full(array, kind, members, half):
    array = array.astype(jnp.bfloat16)
    if kind == "gains":
        cols = array.T
        return jnp.pad(cols, ((0, 0), (0, GAIN_COLS - cols.shape[1])))
    if kind == "grouped":
        grouped = array.reshape(members, 4 * half, D)
        return jnp.concatenate(
            [grouped[:, q * half:(q + 1) * half, :] for q in range(4)], axis=2
        ).reshape(members * half, 4 * D)
    return array


def gather_group(arrays, kinds, part, half):
    block = jnp.concatenate([to_member(a, k, part, half) for a, k in zip(arrays, kinds)], axis=1)
    widths = [width_of(a, k) for a, k in zip(arrays, kinds)]
    gathered = lax.all_gather(block, MEMBERS, axis=0, tiled=True)
    return from_members(gathered, kinds, widths, half)


def pair_sum(values, axis):
    if lax.axis_size(axis) == 2:
        return values + lax.ppermute(values, axis, [(0, 1), (1, 0)])
    return lax.psum(values, axis)


def core_gather(values):
    if lax.axis_size("core") == 2:
        other = lax.ppermute(values, "core", [(0, 1), (1, 0)])
        first = lax.axis_index("core") == 0
        return jnp.concatenate(
            [jnp.where(first, values, other), jnp.where(first, other, values)], axis=0
        )
    return lax.all_gather(values, "core", axis=0, tiled=True)


def pack_group(grads, kinds, members, half):
    return jnp.concatenate(
        [to_members_full(g, k, members, half) for g, k in zip(grads, kinds)], axis=1
    )


def reduce_group(packed, grads, kinds, half):
    widths = [width_of(g, k) for g, k in zip(grads, kinds)]
    owned = lax.psum_scatter(packed, MEMBERS, scatter_dimension=0, tiled=True)
    owned = core_gather(pair_sum(owned, "dpo"))
    return [part.astype(jnp.float32) for part in from_members(owned, kinds, widths, half)]


def layer(
    inputs, space_in, space_out, time_in, time_out, hidden_in, hidden_out, norm_gains, cotangent
):
    fsdp_size = lax.axis_size("fsdp")
    core_size = lax.axis_size("core")
    members = fsdp_size * core_size
    half = space_in.shape[0] // core_size
    core = lax.axis_index("core")

    s_in, s_out, gains = gather_group(
        (space_in, space_out, norm_gains), ("plain", "plain", "gains"), core, half
    )
    t_in, t_out = gather_group((time_in, time_out), ("plain", "plain"), core, half)
    h_in, h_out = gather_group((hidden_in, hidden_out), ("plain", "grouped"), core, half)
    gain_rows = gains.astype(jnp.float32)

    micro = inputs.shape[0]
    spatial = ("gl", "gm", "ghlm")
    temporal = ("lg", "mg", "ghlm")

    saved = []
    results = []
    for index in range(micro):
        frames_in = inputs[index, 0].astype(jnp.float32)
        normed_one = layer_norm(frames_in, gain_rows[0]).astype(jnp.bfloat16)
        join_space, total_space, context_space = attend_core(normed_one, s_in, *spatial)
        mixed_one = frames_in + flat_dot(context_space, s_out)
        normed_two = layer_norm(mixed_one, gain_rows[1]).astype(jnp.bfloat16)
        placed = lax.all_to_all(normed_two, "fsdp", split_axis=1, concat_axis=0, tiled=True)
        join_time, total_time, context_placed = attend_core(placed, t_in, *temporal)
        context_time = lax.all_to_all(
            context_placed, "fsdp", split_axis=0, concat_axis=1, tiled=True
        )
        mixed_two = mixed_one + flat_dot(context_time, t_out)
        normed_three = layer_norm(mixed_two, gain_rows[2]).astype(jnp.bfloat16)
        hidden = flat_dot(normed_three, h_in)
        activated, tail = gelu_parts(hidden)
        activated = activated.astype(jnp.bfloat16)
        results.append(mixed_two + flat_dot(activated, h_out))
        saved.append(
            dict(
                frames_in=frames_in,
                normed_one=normed_one,
                join_space=join_space,
                total_space=total_space,
                context_space=context_space,
                mixed_one=mixed_one,
                placed=placed,
                join_time=join_time,
                total_time=total_time,
                context_time=context_time,
                mixed_two=mixed_two,
                normed_three=normed_three,
                hidden=hidden,
                tail=tail,
                activated=activated,
            )
        )

    def summed(terms):
        total = terms[0]
        for term in terms[1:]:
            total = total + term
        return total

    upstreams = []
    back_threes = []
    gain_two_terms = []
    hidden_out_terms = []
    hidden_in_terms = []
    for index in range(micro):
        s = saved[index]
        upstream = cotangent[index, 0].astype(jnp.float32)
        rounded = upstream.astype(jnp.bfloat16)
        hidden_out_terms.append(token_sum(s["activated"], rounded))
        back_active = back_dot(rounded, h_out).astype(jnp.bfloat16)
        back_hidden = gelu_back(
            s["hidden"], s["tail"], back_active.astype(jnp.float32)
        ).astype(jnp.bfloat16)
        hidden_in_terms.append(token_sum(s["normed_three"], back_hidden))
        back_threes.append(back_dot(back_hidden, h_in).astype(jnp.bfloat16))
        upstreams.append(upstream)
    ffn_grads = (summed(hidden_in_terms), summed(hidden_out_terms))
    ffn_kinds = ("plain", "grouped")
    packed_ffn, back_threes[-1] = lax.optimization_barrier(
        (pack_group(ffn_grads, ffn_kinds, members, half), back_threes[-1])
    )
    grad_ffn = reduce_group(packed_ffn, ffn_grads, ffn_kinds, half)

    back_twos_placed = []
    time_out_terms = []
    time_in_terms = []
    for index in range(micro):
        s = saved[index]
        back_mixed, gain_grad = norm_back(
            s["mixed_two"], gain_rows[2], back_threes[index].astype(jnp.float32)
        )
        gain_two_terms.append(gain_grad)
        upstream = upstreams[index] + back_mixed
        upstreams[index] = upstream
        rounded = upstream.astype(jnp.bfloat16)
        time_out_terms.append(token_sum(s["context_time"], rounded))
        back_context = back_dot(rounded, t_out).astype(jnp.bfloat16)
        back_placed = lax.all_to_all(back_context, "fsdp", split_axis=1, concat_axis=0, tiled=True)
        back_join = attend_back(s["join_time"], s["total_time"], back_placed, *temporal)
        time_in_terms.append(join_sum(s["placed"], back_join))
        back_twos_placed.append(join_back(back_join, t_in).astype(jnp.bfloat16))
    time_grads = (summed(time_in_terms), summed(time_out_terms))
    time_kinds = ("plain", "plain")
    packed_time, back_twos_placed[-1] = lax.optimization_barrier(
        (pack_group(time_grads, time_kinds, members, half), back_twos_placed[-1])
    )
    grad_time = reduce_group(packed_time, time_grads, time_kinds, half)

    input_grads = []
    gain_one_terms = []
    gain_zero_terms = []
    space_out_terms = []
    space_in_terms = []
    for index in range(micro):
        s = saved[index]
        back_two = lax.all_to_all(
            back_twos_placed[index], "fsdp", split_axis=0, concat_axis=1, tiled=True
        )
        back_mixed, gain_grad = norm_back(s["mixed_one"], gain_rows[1], back_two.astype(jnp.float32))
        gain_one_terms.append(gain_grad)
        upstream = upstreams[index] + back_mixed
        rounded = upstream.astype(jnp.bfloat16)
        space_out_terms.append(token_sum(s["context_space"], rounded))
        back_context = back_dot(rounded, s_out).astype(jnp.bfloat16)
        back_join = attend_back(s["join_space"], s["total_space"], back_context, *spatial)
        space_in_terms.append(join_sum(s["normed_one"], back_join))
        back_one = join_back(back_join, s_in).astype(jnp.bfloat16)
        back_mixed, gain_grad = norm_back(
            s["frames_in"], gain_rows[0], back_one.astype(jnp.float32)
        )
        gain_zero_terms.append(gain_grad)
        input_grads.append(upstream + back_mixed)
    grad_space_in = summed(space_in_terms)
    grad_space_out = summed(space_out_terms)
    gain_grad_zero = summed(gain_zero_terms)
    gain_grad_one = summed(gain_one_terms)
    gain_grad_two = summed(gain_two_terms)
    result = jnp.stack(results)
    input_grad = jnp.stack(input_grads)

    gain_grads = jnp.stack((gain_grad_zero, gain_grad_one, gain_grad_two))
    space_grads = (grad_space_in, grad_space_out, gain_grads)
    space_kinds = ("plain", "plain", "gains")
    grad_space = reduce_group(
        pack_group(space_grads, space_kinds, members, half), space_grads, space_kinds, half
    )
    return (
        result[:, None],
        input_grad[:, None],
        grad_space[0],
        grad_space[1],
        grad_time[0],
        grad_time[1],
        grad_ffn[0],
        grad_ffn[1],
        grad_space[2],
    )


def solution(mesh):
    dp_size, fsdp_size = mesh.devices.shape
    split = Mesh(mesh.devices.reshape(dp_size // 2, 2, fsdp_size), ("dpo", "core", "fsdp"))
    tokens = P(None, ("dpo", "core"), "fsdp", None, None)
    rows = P("fsdp", None)
    return jax.shard_map(
        layer,
        mesh=split,
        in_specs=(tokens, rows, rows, rows, rows, rows, rows, P(None, "fsdp"), tokens),
        out_specs=(tokens, tokens, rows, rows, rows, rows, rows, rows, P(None, "fsdp")),
        check_vma=False,
    )
```

profile of v0, /device:TPU:0, one launch (start us, length us, event | category | flops | bytes accessed | tf_op | source)
XLA Modules:
  0.0 765.4 jit_solution(16595435303153086460)
XLA Ops:
  15.0 52.6 %all-gather.4.cloned.1.call-done = bf16[768,3200]{1,0:T(8,128)(2,1)} async-done(((bf16[48,3200]{1,0:T(8,128)(2,1)}), bf16[768,3200]{1,0:T(8,128)(2,1)}) %all-gather.4.cloned.1.call-update) | async-done | bytes 4915216 | tf_op jit(solution)/shard_map/all_gather | solution.py:211
  75.6 5.0 convolution_convert_fusion.5
  104.5 25.9 %all-to-all-done.2 = bf16[2,192,768]{2,0,1:T(2,128)(2,1)S(1)} async-done(((bf16[2,192,768]{2,0,1:T(2,128)(2,1)}), bf16[2,192,768]{2,0,1:T(2,128)(2,1)S(1)}, u32[]{:S(2)}, u32[]{:S(2)}) %all-to-all-start.2) | async-done | bytes 589856 | tf_op jit(solution)/shard_map/all_to_all | solution.py:272
  155.4 5.2 all-to-all-done
  165.1 5.0 convolution_convert_fusion.4
  170.0 6.4 reshape.653
  188.9 6.2 all-to-all-start.1
  198.1 29.7 %all-to-all-done.1 = bf16[16,24,768]{2,1,0:T(8,128)(2,1)} async-done(((bf16[16,24,768]{2,1,0:T(8,128)(2,1)}), bf16[16,24,768]{2,1,0:T(8,128)(2,1)}, u32[]{:S(2)}, u32[]{:S(2)}) %all-to-all-start.1) | async-done | bytes 589856 | tf_op jit(solution)/shard_map/all_to_all | solution.py:274
  249.3 13.4 %fusion.22 = (bf16[2,192,3072]{2,1,0:T(8,128)(2,1)S(1)}, f32[2,192,3072]{2,1,0:T(8,128)S(1)}) fusion(f32[2,192,3072]{2,1,0:T(8,128)} %bitcast.522, f32[2,192,3072]{2,1,0:T(8,128)S(1)} %get-tuple-element.142, u8[192,3072]{1,0:T(8,128)(4,1)S(1)} %get-tuple-element.65, u8[192,3072]{1,0:T(8,128)(4,1)S(1)} %get-tuple-element.64), kind=kLoop, calls=%fused_computation.36 | loop fusion | flops 88473600 | bytes 17694720 | tf_op jit(solution)/shard_map/convert_element_type | solution.py:322
  272.2 12.6 %fusion.17 = (bf16[2,192,3072]{2,1,0:T(8,128)(2,1)}, f32[2,192,3072]{2,1,0:T(8,128)S(1)}) fusion(f32[2,192,3072]{2,1,0:T(8,128)S(1)} %bitcast.523, f32[2,192,3072]{2,1,0:T(8,128)S(1)} %get-tuple-element.147, u8[192,3072]{1,0:T(8,128)(4,1)S(1)} %get-tuple-element.63, u8[192,3072]{1,0:T(8,128)(4,1)S(1)} %get-tuple-element.62), kind=kLoop, calls=%fused_computation.31 | loop fusion | flops 88473600 | bytes 17694720 | tf_op jit(solution)/shard_map/convert_element_type | solution.py:322
  293.3 5.5 fusion.166
  298.9 5.5 fusion.1
  309.1 5.2 fusion.87
  338.6 9.5 %all-to-all-done.4 = bf16[2,192,768]{2,0,1:T(2,128)(2,1)} async-done(((bf16[2,192,768]{2,0,1:T(2,128)(2,1)}), bf16[2,192,768]{2,0,1:T(2,128)(2,1)}, u32[]{:S(2)}, u32[]{:S(2)}) %all-to-all-start.4) | async-done | bytes 589856 | tf_op jit(solution)/shard_map/all_to_all | solution.py:347
  357.3 6.4 fusion.39
  430.1 6.2 all-to-all-start.5
  451.5 6.0 all-to-all-start.7
  458.1 6.7 copy.447
  467.0 4.9 all-to-all-done.7
  540.2 7.5 copy.445
  548.3 5.2 fusion.80
  578.7 43.6 %reduce-scatter.10.cloned.1.call-done = bf16[48,3200]{1,0:T(8,128)(2,1)} async-done(((bf16[768,3200]{1,0:T(8,128)(2,1)}), bf16[48,3200]{1,0:T(8,128)(2,1)}) %reduce-scatter.10.cloned.1.call-update) | async-done | bytes 307216 | tf_op jit(solution)/shard_map/reduce_scatter | solution.py:239
  640.8 95.5 %reduce-scatter.8.cloned.1.call-done = bf16[48,6144]{1,0:T(8,128)(2,1)} async-done(((bf16[768,6144]{1,0:T(8,128)(2,1)}), bf16[48,6144]{1,0:T(8,128)(2,1)}) %reduce-scatter.8.cloned.1.call-update) | async-done | bytes 589840 | tf_op jit(solution)/shard_map/reduce_scatter | solution.py:239
  737.9 13.4 %collective-permute-done.4 = bf16[48,6144]{1,0:T(8,128)(2,1)S(1)} collective-permute-done((bf16[48,6144]{1,0:T(8,128)(2,1)}, bf16[48,6144]{1,0:T(8,128)(2,1)S(1)}, u32[]{:S(2)}, u32[]{:S(2)}) %collective-permute-start.4) | collective-permute-done | bytes 589856 | tf_op jit(solution)/shard_map/ppermute | solution.py:217
  (625 shorter events, 365.3 us)
Async XLA Ops:
  7.2 60.4 %all-gather.4.cloned.1.call-start = ((), (), s32[]{:S(2)}) async-start(), calls=%async_computation.11 | async-start | bytes 5222400 | tf_op jit(solution)/shard_map/all_gather | solution.py:211
  9.9 125.4 %all-gather.6.cloned.1.call-start = ((), (), s32[]{:S(2)}) async-start(), calls=%async_computation.12 | async-start | bytes 5013504 | tf_op jit(solution)/shard_map/all_gather | solution.py:211
  12.6 223.5 %all-gather.8.cloned.1.call-start = ((), (), s32[]{:S(2)}) async-start(), calls=%async_computation.13 | async-start | bytes 10027008 | tf_op jit(solution)/shard_map/all_gather | solution.py:211
  13.9 59.0 %copy-start.130 = (f32[2,192]{1,0:T(2,128)}, f32[2,192]{1,0:T(2,128)S(1)}, u32[]{:S(2)}) copy-start(f32[2,192]{1,0:T(2,128)S(1)} %get-tuple-element.159) | copy-start | bytes 4612
  13.9 61.7 %copy-start.132 = (f32[2,192]{1,0:T(2,128)}, f32[2,192]{1,0:T(2,128)S(1)}, u32[]{:S(2)}) copy-start(f32[2,192]{1,0:T(2,128)S(1)} %get-tuple-element.160) | copy-start | bytes 4612
  15.0 60.6 %copy-start.141 = (f32[2,192]{1,0:T(2,128)}, f32[2,192]{1,0:T(2,128)S(1)}, u32[]{:S(2)}) copy-start(f32[2,192]{1,0:T(2,128)S(1)} %fusion.171) | copy-start | bytes 4612
  99.5 30.9 %all-to-all-start.2 = ((bf16[2,192,768]{2,0,1:T(2,128)(2,1)}), bf16[2,192,768]{2,0,1:T(2,128)(2,1)S(1)}, u32[]{:S(2)}, u32[]{:S(2)}) async-start(bf16[2,192,768]{2,0,1:T(2,128)(2,1)} %copy.342), calls=%async_computation.2 | async-start | bytes 1179648 | tf_op jit(solution)/shard_map/all_to_all | solution.py:272
  130.4 30.2 %all-to-all-start = ((bf16[2,192,768]{2,0,1:T(2,128)(2,1)}), bf16[2,192,768]{2,0,1:T(2,128)(2,1)S(1)}, u32[]{:S(2)}, u32[]{:S(2)}) async-start(bf16[2,192,768]{2,0,1:T(2,128)(2,1)} %copy.327), calls=%async_computation | async-start | bytes 1179648 | tf_op jit(solution)/shard_map/all_to_all | solution.py:272
  160.6 28.3 %all-to-all-start.3 = ((bf16[16,24,768]{2,1,0:T(8,128)(2,1)}), bf16[16,24,768]{2,1,0:T(8,128)(2,1)}, u32[]{:S(2)}, u32[]{:S(2)}) async-start(bf16[16,24,768]{2,1,0:T(8,128)(2,1)} %convert_element_type.549), calls=%async_computation.3 | async-start | bytes 1179648 | tf_op jit(solution)/shard_map/all_to_all | solution.py:274
  188.9 38.9 %all-to-all-start.1 = ((bf16[16,24,768]{2,1,0:T(8,128)(2,1)}), bf16[16,24,768]{2,1,0:T(8,128)(2,1)}, u32[]{:S(2)}, u32[]{:S(2)}) async-start(bf16[16,24,768]{2,1,0:T(8,128)(2,1)} %convert_element_type.533), calls=%async_computation.1 | async-start | bytes 1179648 | tf_op jit(solution)/shard_map/all_to_all | solution.py:274
  236.0 85.9 %copy-start.117 = (f32[2,192]{1,0:T(2,128)}, f32[2,192]{1,0:T(2,128)S(1)}, u32[]{:S(2)}) copy-start(f32[2,192]{1,0:T(2,128)S(1)} %fusion.173) | copy-start | bytes 4612
  327.9 20.2 %all-to-all-start.4 = ((bf16[2,192,768]{2,0,1:T(2,128)(2,1)}), bf16[2,192,768]{2,0,1:T(2,128)(2,1)}, u32[]{:S(2)}, u32[]{:S(2)}) async-start(bf16[2,192,768]{2,0,1:T(2,128)(2,1)} %copy.351), calls=%async_computation.4 | async-start | bytes 1179648 | tf_op jit(solution)/shard_map/all_to_all | solution.py:347
  348.1 46.2 %all-to-all-start.6 = ((bf16[2,192,768]{2,0,1:T(2,128)(2,1)}), bf16[2,192,768]{2,0,1:T(2,128)(2,1)}, u32[]{:S(2)}, u32[]{:S(2)}) async-start(bf16[2,192,768]{2,0,1:T(2,128)(2,1)} %copy.372), calls=%async_computation.6 | async-start | bytes 1179648 | tf_op jit(solution)/shard_map/all_to_all | solution.py:347
  430.1 21.4 %all-to-all-start.5 = ((bf16[16,24,768]{2,1,0:T(8,128)(2,1)}), bf16[16,24,768]{2,1,0:T(8,128)(2,1)}, u32[]{:S(2)}, u32[]{:S(2)}) async-start(bf16[16,24,768]{2,1,0:T(8,128)(2,1)} %fusion.82), calls=%async_computation.5 | async-start | bytes 1179648 | tf_op jit(solution)/shard_map/all_to_all | solution.py:365
  451.5 20.5 %all-to-all-start.7 = ((bf16[16,24,768]{2,1,0:T(8,128)(2,1)}), bf16[16,24,768]{2,1,0:T(8,128)(2,1)S(1)}, u32[]{:S(2)}, u32[]{:S(2)}) async-start(bf16[16,24,768]{2,1,0:T(8,128)(2,1)} %fusion.83), calls=%async_computation.7 | async-start | bytes 1179648 | tf_op jit(solution)/shard_map/all_to_all | solution.py:365
  457.5 102.4 %reduce-scatter.12.cloned.1.call-start = ((), (), s32[]{:S(2)}) async-start(), calls=%async_computation.16 | async-start | bytes 5013504 | tf_op jit(solution)/shard_map/reduce_scatter | solution.py:239
  464.8 157.5 %reduce-scatter.10.cloned.1.call-start = ((), (), s32[]{:S(2)}) async-start(), calls=%async_computation.15 | async-start | bytes 5222400 | tf_op jit(solution)/shard_map/reduce_scatter | solution.py:239
  547.7 188.6 %reduce-scatter.8.cloned.1.call-start = ((), (), s32[]{:S(2)}) async-start(), calls=%async_computation.14 | async-start | bytes 10027008 | tf_op jit(solution)/shard_map/reduce_scatter | solution.py:239
  559.8 7.0 collective-permute-start.2
  573.6 3.8 collective-permute-start.3
  622.3 8.0 %collective-permute-start = (bf16[48,3200]{1,0:T(8,128)(2,1)}, bf16[48,3200]{1,0:T(8,128)(2,1)}, u32[]{:S(2)}, u32[]{:S(2)}) collective-permute-start(bf16[48,3200]{1,0:T(8,128)(2,1)} %reduce-scatter.10.cloned.1.call-done), channel_id=1, source_target_pairs={{0,16},{16,0},{1,17},{17,1},{2,18},{18,2},{3,19},{19,3},{4,20},{20... | collective-permute-start | bytes 921608 | tf_op jit(solution)/shard_map/ppermute | solution.py:217
  635.3 5.0 collective-permute-start.1
  736.3 15.0 %collective-permute-start.4 = (bf16[48,6144]{1,0:T(8,128)(2,1)}, bf16[48,6144]{1,0:T(8,128)(2,1)S(1)}, u32[]{:S(2)}, u32[]{:S(2)}) collective-permute-start(bf16[48,6144]{1,0:T(8,128)(2,1)} %reduce-scatter.8.cloned.1.call-done), channel_id=1, source_target_pairs={{0,16},{16,0},{1,17},{17,1},{2,18},{18,2},{3,19},{19,3},{4,20},{20... | collective-permute-start | bytes 1769480 | tf_op jit(solution)/shard_map/ppermute | solution.py:217
  751.5 3.3 collective-permute-start.5
  (171 other events, 771.0 us)
Sparse Core Ops, SparseCore 0:
  10.8 56.8 all-gather.3
  70.5 62.2 all-gather.5
  135.6 99.8 all-gather.7
  465.0 76.9 reduce-scatter.11
  547.8 74.4 reduce-scatter.9
  626.3 110.0 reduce-scatter.7
where the time goes:
time: 772 us; the launch traced here: 765 us
  waiting for transfers between devices  288 us (37%)
  matrix products  171 us (22%)
  local copies, waits for them, and re-layouts  159 us (21%)
  other arithmetic  85.9 us (11%)
  starting transfers between devices  44.3 us (6%)
  between operations  17.1 us (2%)
    reduce_scatter x3, waiting for transfers between devices, reduce_group(): owned = lax.psum_scatter(packed, MEMBERS, scatter_dimension=0, tiled=True)  139 us
    all_gather x3, waiting for transfers between devices, gather_group(): gathered = lax.all_gather(block, MEMBERS, axis=0, tiled=True)  52.7 us
    unnamed x361, local copies, waits for them, and re-layouts  49 us
    dot_general x20, matrix products, back_dot(): lax.dot_general(flat, right, (((1,), (1,)), ((), ())), preferred_element_...  47.2 us
    dot_general x12, matrix products, flat_dot(): product = jnp.dot(flat, right, preferred_element_type=jnp.float32)  43 us
    convert_element_type x18, local copies, waits for them, and re-layouts, attend_back(): part.reshape(shape).astype(jnp.bfloat16)  35.2 us
    dot_general x20, matrix products, token_sum(): lax.dot_general(left_rows, right_rows, (((0,), (0,)), ((), ())), preferre...  34.8 us
    all_to_all x2, waiting for transfers between devices, layer(): lax.all_to_all(normed_two, 'fsdp', split_axis=1, concat_axis=0, tiled=True)  31.1 us
  transfers between devices with their start and end apart: 20, of which 11 were waited for; matrix products, arithmetic and copies ran while one was open for 34% of the time, Pallas kernels for 0%

commit v1 on v0

--- a/solution.py
+++ b/solution.py
@@ -1,3 +1,5 @@
+from functools import partial
+
 import jax
 import jax.numpy as jnp
 from jax import lax
@@ -126,35 +128,8 @@
         back_heads,
         preferred_element_type=jnp.float32,
     )
-    shape = back_context.shape[:-1] + (D,)
-    return tuple(
-        part.reshape(shape).astype(jnp.bfloat16) for part in (back_query, back_keys, back_values)
-    )
-
-
-def join_sum(normed, parts):
-    return jnp.concatenate([token_sum(normed, part) for part in parts], axis=1)
-
-
-def join_back(parts, weight_in):
-    total = None
-    for index, part in enumerate(parts):
-        term = back_dot(part, weight_in[:, index * D:(index + 1) * D])
-        total = term if total is None else total + term
-    return total
-
-
-SQRT_HALF = 0.5 ** 0.5
-
-
-def gelu_parts(hidden):
-    tail = lax.erfc(-hidden * SQRT_HALF)
-    return 0.5 * hidden * tail, tail
-
-
-def gelu_back(hidden, tail, incoming):
-    slope = 0.5 * tail + hidden * (SQRT_HALF / jnp.sqrt(jnp.pi)) * jnp.exp(-0.5 * hidden * hidden)
-    return incoming * slope
+    stacked = jnp.stack((back_query, back_keys, back_values), axis=-3)
+    return stacked.reshape(back_context.shape[:-1] + (3 * D,)).astype(jnp.bfloat16)
 
 
 def to_member(array, kind, part, half):
@@ -277,8 +252,7 @@
         mixed_two = mixed_one + flat_dot(context_time, t_out)
         normed_three = layer_norm(mixed_two, gain_rows[2]).astype(jnp.bfloat16)
         hidden = flat_dot(normed_three, h_in)
-        activated, tail = gelu_parts(hidden)
-        activated = activated.astype(jnp.bfloat16)
+        activated = jax.nn.gelu(hidden, approximate=False).astype(jnp.bfloat16)
         results.append(mixed_two + flat_dot(activated, h_out))
         saved.append(
             dict(
@@ -295,7 +269,6 @@
                 mixed_two=mixed_two,
                 normed_three=normed_three,
                 hidden=hidden,
-                tail=tail,
                 activated=activated,
             )
         )
@@ -317,9 +290,8 @@
         rounded = upstream.astype(jnp.bfloat16)
         hidden_out_terms.append(token_sum(s["activated"], rounded))
         back_active = back_dot(rounded, h_out).astype(jnp.bfloat16)
-        back_hidden = gelu_back(
-            s["hidden"], s["tail"], back_active.astype(jnp.float32)
-        ).astype(jnp.bfloat16)
+        _, gelu_pull = jax.vjp(partial(jax.nn.gelu, approximate=False), s["hidden"])
+        back_hidden = gelu_pull(back_active.astype(jnp.float32))[0].astype(jnp.bfloat16)
         hidden_in_terms.append(token_sum(s["normed_three"], back_hidden))
         back_threes.append(back_dot(back_hidden, h_in).astype(jnp.bfloat16))
         upstreams.append(upstream)
@@ -346,8 +318,8 @@
         back_context = back_dot(rounded, t_out).astype(jnp.bfloat16)
         back_placed = lax.all_to_all(back_context, "fsdp", split_axis=1, concat_axis=0, tiled=True)
         back_join = attend_back(s["join_time"], s["total_time"], back_placed, *temporal)
-        time_in_terms.append(join_sum(s["placed"], back_join))
-        back_twos_placed.append(join_back(back_join, t_in).astype(jnp.bfloat16))
+        time_in_terms.append(token_sum(s["placed"], back_join))
+        back_twos_placed.append(back_dot(back_join, t_in).astype(jnp.bfloat16))
     time_grads = (summed(time_in_terms), summed(time_out_terms))
     time_kinds = ("plain", "plain")
     packed_time, back_twos_placed[-1] = lax.optimization_barrier(
@@ -365,6 +337,8 @@
         back_two = lax.all_to_all(
             back_twos_placed[index], "fsdp", split_axis=0, concat_axis=1, tiled=True
         )
+        if index == micro - 1:
+            back_two, grad_ffn = lax.optimization_barrier((back_two, grad_ffn))
         back_mixed, gain_grad = norm_back(s["mixed_one"], gain_rows[1], back_two.astype(jnp.float32))
         gain_one_terms.append(gain_grad)
         upstream = upstreams[index] + back_mixed
@@ -372,8 +346,8 @@
         space_out_terms.append(token_sum(s["context_space"], rounded))
         back_context = back_dot(rounded, s_out).astype(jnp.bfloat16)
         back_join = attend_back(s["join_space"], s["total_space"], back_context, *spatial)
-        space_in_terms.append(join_sum(s["normed_one"], back_join))
-        back_one = join_back(back_join, s_in).astype(jnp.bfloat16)
+        space_in_terms.append(token_sum(s["normed_one"], back_join))
+        back_one = back_dot(back_join, s_in).astype(jnp.bfloat16)
         back_mixed, gain_grad = norm_back(
             s["frames_in"], gain_rows[0], back_one.astype(jnp.float32)
         )

time: 772 us -> 652 us (0.84)
  waiting for transfers between devices: 288 us -> 220 us
  local copies, waits for them, and re-layouts: 159 us -> 125 us
  matrix products: 171 us -> 160 us
    reduce_scatter x3, waiting for transfers between devices: 139 us -> 77.6 us  [reduce_group(): owned = lax.psum_scatter(packed, MEMBERS, scatter_dimension=0, tiled=True)]
    unnamed x361 -> x268, local copies, waits for them, and re-layouts: 49 us -> 24 us
    ppermute x3, waiting for transfers between devices: 20.2 us -> 9.92 us  [pair_sum(): return values + lax.ppermute(values, axis, [(0, 1), (1, 0)])]
    dot_general x20 -> x12, matrix products: 34.8 us -> 31.2 us  [token_sum(): lax.dot_general(left_rows, right_rows, (((0,), (0,)), ((), ())), preferre...]
    convert_element_type x6 -> x8, other arithmetic: 31.3 us -> 33.6 us  [the longest x2 27.2 us: layer(): gelu_pull(back_active.astype(jnp.float32))[0].astype(jnp.bfloat16)]
    dot_general x20 -> x12, matrix products: 47.2 us -> 46 us  [back_dot(): lax.dot_general(flat, right, (((1,), (1,)), ((), ())), preferred_element_...]
    convert_element_type x18 -> x8, local copies, waits for them, and re-layouts: 35.2 us -> 34.8 us  [attend_back(): stacked.reshape(back_context.shape[:-1] + (3 * D,)).astype(jnp.bfloat16)]
  transfers between devices with their start and end apart: 20 -> 20, of which waited for: 11 -> 12; matrix products, arithmetic and copies ran while one was open for 34% -> 41% of each run, Pallas kernels for 0% -> 0%
where the time goes in v1:
time: 652 us; the launch traced here: 646 us
  waiting for transfers between devices  220 us (34%)
  matrix products  160 us (25%)
  local copies, waits for them, and re-layouts  125 us (19%)
  other arithmetic  82.6 us (13%)
  starting transfers between devices  41.9 us (6%)
  between operations  16.6 us (3%)
    reduce_scatter x3, waiting for transfers between devices, reduce_group(): owned = lax.psum_scatter(packed, MEMBERS, scatter_dimension=0, tiled=True)  77.6 us
    all_gather x3, waiting for transfers between devices, gather_group(): gathered = lax.all_gather(block, MEMBERS, axis=0, tiled=True)  52.6 us
    dot_general x12, matrix products, back_dot(): lax.dot_general(flat, right, (((1,), (1,)), ((), ())), preferred_element_...  46 us
    dot_general x12, matrix products, flat_dot(): product = jnp.dot(flat, right, preferred_element_type=jnp.float32)  42.6 us
    convert_element_type x8, local copies, waits for them, and re-layouts, attend_back(): stacked.reshape(back_context.shape[:-1] + (3 * D,)).astype(jnp.bfloat16)  34.8 us
    all_to_all x2, waiting for transfers between devices, layer(): lax.all_to_all(normed_two, 'fsdp', split_axis=1, concat_axis=0, tiled=True)  31.7 us
    dot_general x12, matrix products, token_sum(): lax.dot_general(left_rows, right_rows, (((0,), (0,)), ((), ())), preferre...  31.2 us
    all_to_all x2, waiting for transfers between devices, layer(): lax.all_to_all(context_placed, 'fsdp', split_axis=0, concat_axis=1, tiled...  29.3 us
  transfers between devices with their start and end apart: 20, of which 12 were waited for; matrix products, arithmetic and copies ran while one was open for 41% of the time, Pallas kernels for 0%

profile of v1, /device:TPU:0, one launch (start us, length us, event | category | flops | bytes accessed | tf_op | source)
XLA Modules:
  0.0 645.6 jit_solution(15507972799474495034)
XLA Ops:
  15.0 52.6 %all-gather.4.cloned.1.call-done = bf16[768,3200]{1,0:T(8,128)(2,1)} async-done(((bf16[48,3200]{1,0:T(8,128)(2,1)}), bf16[768,3200]{1,0:T(8,128)(2,1)}) %all-gather.4.cloned.1.call-update) | async-done | bytes 4915216 | tf_op jit(solution)/shard_map/all_gather | solution.py:186
  75.5 5.0 convolution_convert_fusion.5
  103.8 26.6 %all-to-all-done.2 = bf16[2,192,768]{2,0,1:T(2,128)(2,1)S(1)} async-done(((bf16[2,192,768]{2,0,1:T(2,128)(2,1)}), bf16[2,192,768]{2,0,1:T(2,128)(2,1)S(1)}, u32[]{:S(2)}, u32[]{:S(2)}) %all-to-all-start.2) | async-done | bytes 589856 | tf_op jit(solution)/shard_map/all_to_all | solution.py:247
  155.1 5.1 all-to-all-done
  171.9 6.5 %reshape.589 = bf16[16,24,3,12,64]{4,3,2,1,0:T(8,128)(2,1)} reshape(bf16[16,24,2304]{2,1,0:T(8,128)(2,1)} %convolution_convert_fusion.4) | data formatting | bytes 3538944 | tf_op jit(solution)/shard_map/reshape | solution.py:55
  190.7 5.9 all-to-all-start.1
  200.1 29.3 %all-to-all-done.1 = bf16[16,24,768]{2,1,0:T(8,128)(2,1)} async-done(((bf16[16,24,768]{2,1,0:T(8,128)(2,1)}), bf16[16,24,768]{2,1,0:T(8,128)(2,1)}, u32[]{:S(2)}, u32[]{:S(2)}) %all-to-all-start.1) | async-done | bytes 589856 | tf_op jit(solution)/shard_map/all_to_all | solution.py:249
  250.6 13.5 %add_convert_fusion.2 = (bf16[2,192,3072]{2,1,0:T(8,128)(2,1)}, f32[2,192,3072]{2,1,0:T(8,128)S(1)}) fusion(f32[2,192,3072]{2,1,0:T(8,128)} %bitcast.473, f32[2,192,3072]{2,1,0:T(8,128)S(1)} %get-tuple-element.148, u8[192,3072]{1,0:T(8,128)(4,1)S(1)} %get-tuple-element.71, u8[192,3072]{1,0:T(8,128)(4,1)S(1)} %get-tuple-element.70), kind=kLoop, calls=%fused_computation.41 | loop fusion | flops 90832896 | bytes 17694720 | tf_op jit(solution)/shard_map/convert_element_type | solution.py:294
  265.2 7.4 %fusion.23 = f32[3072,384]{0,1:T(8,128)} fusion(bf16[3072,768]{1,0:T(8,128)(2,1)} %bitcast.470, bf16[384,768]{1,0:T(8,128)(2,1)S(1)} %bitcast.485), kind=kOutput, calls=%fused_computation.76 | convolution fusion | flops 1814298624 | bytes 10027008 | tf_op jit(solution)/shard_map/dot_general | solution.py:40
  275.8 13.7 %add_convert_fusion.3 = (bf16[2,192,3072]{2,1,0:T(8,128)(2,1)}, f32[2,192,3072]{2,1,0:T(8,128)S(1)}) fusion(f32[2,192,3072]{2,1,0:T(8,128)} %bitcast.474, f32[2,192,3072]{2,1,0:T(8,128)S(1)} %get-tuple-element.153, u8[192,3072]{1,0:T(8,128)(4,1)S(1)} %get-tuple-element.69, u8[192,3072]{1,0:T(8,128)(4,1)S(1)} %get-tuple-element.68), kind=kLoop, calls=%fused_computation.42 | loop fusion | flops 90832896 | bytes 17694720 | tf_op jit(solution)/shard_map/convert_element_type | solution.py:294
  311.9 5.2 fusion.66
  317.2 5.8 fusion.71
  341.6 8.1 %all-to-all-done.4 = bf16[2,192,768]{2,0,1:T(2,128)(2,1)} async-done(((bf16[2,192,768]{2,0,1:T(2,128)(2,1)}), bf16[2,192,768]{2,0,1:T(2,128)(2,1)}, u32[]{:S(2)}, u32[]{:S(2)}) %all-to-all-start.4) | async-done | bytes 589856 | tf_op jit(solution)/shard_map/all_to_all | solution.py:319
  373.3 6.6 %convert_element_type.446 = bf16[16,24,2304]{2,1,0:T(8,128)(2,1)} reshape(bf16[16,24,3,12,64]{4,3,2,1,0:T(8,128)(2,1)} %copy.303) | data formatting | bytes 3538944 | tf_op jit(solution)/shard_map/convert_element_type | solution.py:132
  379.9 6.6 %convert_element_type.472 = bf16[384,2304]{1,0:T(8,128)(2,1)} reshape(bf16[16,24,3,12,64]{4,3,2,1,0:T(8,128)(2,1)} %copy.303) | data formatting | bytes 3538944 | tf_op jit(solution)/shard_map/convert_element_type | solution.py:132
  405.1 6.6 %convert_element_type.479 = bf16[384,2304]{1,0:T(8,128)(2,1)} reshape(bf16[16,24,3,12,64]{4,3,2,1,0:T(8,128)(2,1)} %copy.319) | data formatting | bytes 3538944 | tf_op jit(solution)/shard_map/convert_element_type | solution.py:132
  411.7 6.6 %convert_element_type.482 = bf16[16,24,2304]{2,1,0:T(8,128)(2,1)} reshape(bf16[16,24,3,12,64]{4,3,2,1,0:T(8,128)(2,1)} %copy.319) | data formatting | bytes 3538944 | tf_op jit(solution)/shard_map/convert_element_type | solution.py:132
  418.2 5.5 convolution_convert_fusion.20
  423.8 6.5 %all-to-all-start.5 = ((bf16[16,24,768]{2,1,0:T(8,128)(2,1)}), bf16[16,24,768]{2,1,0:T(8,128)(2,1)}, u32[]{:S(2)}, u32[]{:S(2)}) async-start(bf16[16,24,768]{2,1,0:T(8,128)(2,1)} %convolution_convert_fusion.20), calls=%async_computation.5 | async-start | bytes 1179648 | tf_op jit(solution)/shard_map/all_to_all | solution.py:337
  440.9 12.9 %reduce-scatter.4.cloned.1.call-done = bf16[48,6144]{1,0:T(8,128)(2,1)} async-done(((bf16[768,6144]{1,0:T(8,128)(2,1)}), bf16[48,6144]{1,0:T(8,128)(2,1)}) %reduce-scatter.4.cloned.1.call-update) | async-done | bytes 589840 | tf_op jit(solution)/shard_map/reduce_scatter | solution.py:214
  469.9 10.1 %all-to-all-done.7 = bf16[16,24,768]{2,1,0:T(8,128)(2,1)S(1)} async-done(((bf16[16,24,768]{2,1,0:T(8,128)(2,1)}), bf16[16,24,768]{2,1,0:T(8,128)(2,1)S(1)}, u32[]{:S(2)}, u32[]{:S(2)}) %all-to-all-start.7) | async-done | bytes 589856 | tf_op jit(solution)/shard_map/all_to_all | solution.py:337
  546.4 5.2 fusion.63
  560.3 63.5 %reduce-scatter.6.cloned.1.call-done = bf16[48,3200]{1,0:T(8,128)(2,1)} async-done(((bf16[768,3200]{1,0:T(8,128)(2,1)}), bf16[48,3200]{1,0:T(8,128)(2,1)}) %reduce-scatter.6.cloned.1.call-update) | async-done | bytes 307216 | tf_op jit(solution)/shard_map/reduce_scatter | solution.py:214
  625.2 6.0 collective-permute-done.2
  (500 shorter events, 308.2 us)
Async XLA Ops:
  7.2 60.4 %all-gather.4.cloned.1.call-start = ((), (), s32[]{:S(2)}) async-start(), calls=%async_computation.11 | async-start | bytes 5222400 | tf_op jit(solution)/shard_map/all_gather | solution.py:186
  9.9 125.1 %all-gather.6.cloned.1.call-start = ((), (), s32[]{:S(2)}) async-start(), calls=%async_computation.12 | async-start | bytes 5013504 | tf_op jit(solution)/shard_map/all_gather | solution.py:186
  12.6 224.5 %all-gather.8.cloned.1.call-start = ((), (), s32[]{:S(2)}) async-start(), calls=%async_computation.13 | async-start | bytes 10027008 | tf_op jit(solution)/shard_map/all_gather | solution.py:186
  13.9 61.6 %copy-start.106 = (f32[2,192]{1,0:T(2,128)}, f32[2,192]{1,0:T(2,128)S(1)}, u32[]{:S(2)}) copy-start(f32[2,192]{1,0:T(2,128)S(1)} %get-tuple-element.166) | copy-start | bytes 4612
  15.0 60.5 %copy-start.112 = (f32[2,192]{1,0:T(2,128)}, f32[2,192]{1,0:T(2,128)S(1)}, u32[]{:S(2)}) copy-start(f32[2,192]{1,0:T(2,128)S(1)} %fusion.154) | copy-start | bytes 4612
  98.9 31.6 %all-to-all-start.2 = ((bf16[2,192,768]{2,0,1:T(2,128)(2,1)}), bf16[2,192,768]{2,0,1:T(2,128)(2,1)S(1)}, u32[]{:S(2)}, u32[]{:S(2)}) async-start(bf16[2,192,768]{2,0,1:T(2,128)(2,1)} %copy.289), calls=%async_computation.2 | async-start | bytes 1179648 | tf_op jit(solution)/shard_map/all_to_all | solution.py:247
  130.5 29.7 %all-to-all-start = ((bf16[2,192,768]{2,0,1:T(2,128)(2,1)}), bf16[2,192,768]{2,0,1:T(2,128)(2,1)S(1)}, u32[]{:S(2)}, u32[]{:S(2)}) async-start(bf16[2,192,768]{2,0,1:T(2,128)(2,1)} %copy.274), calls=%async_computation | async-start | bytes 1179648 | tf_op jit(solution)/shard_map/all_to_all | solution.py:247
  161.0 29.7 %all-to-all-start.3 = ((bf16[16,24,768]{2,1,0:T(8,128)(2,1)}), bf16[16,24,768]{2,1,0:T(8,128)(2,1)S(1)}, u32[]{:S(2)}, u32[]{:S(2)}) async-start(bf16[16,24,768]{2,1,0:T(8,128)(2,1)} %convert_element_type.428), calls=%async_computation.3 | async-start | bytes 1179648 | tf_op jit(solution)/shard_map/all_to_all | solution.py:249
  190.7 38.7 %all-to-all-start.1 = ((bf16[16,24,768]{2,1,0:T(8,128)(2,1)}), bf16[16,24,768]{2,1,0:T(8,128)(2,1)}, u32[]{:S(2)}, u32[]{:S(2)}) async-start(bf16[16,24,768]{2,1,0:T(8,128)(2,1)} %convert_element_type.412), calls=%async_computation.1 | async-start | bytes 1179648 | tf_op jit(solution)/shard_map/all_to_all | solution.py:249
  196.6 257.2 %reduce-scatter.4.cloned.1.call-start = ((), (), s32[]{:S(2)}) async-start(), calls=%async_computation.14 | async-start | bytes 10027008 | tf_op jit(solution)/shard_map/reduce_scatter | solution.py:214
  330.7 18.9 %all-to-all-start.4 = ((bf16[2,192,768]{2,0,1:T(2,128)(2,1)}), bf16[2,192,768]{2,0,1:T(2,128)(2,1)}, u32[]{:S(2)}, u32[]{:S(2)}) async-start(bf16[2,192,768]{2,0,1:T(2,128)(2,1)} %copy.298), calls=%async_computation.4 | async-start | bytes 1179648 | tf_op jit(solution)/shard_map/all_to_all | solution.py:319
  349.7 36.8 %all-to-all-start.6 = ((bf16[2,192,768]{2,0,1:T(2,128)(2,1)}), bf16[2,192,768]{2,0,1:T(2,128)(2,1)}, u32[]{:S(2)}, u32[]{:S(2)}) async-start(bf16[2,192,768]{2,0,1:T(2,128)(2,1)} %copy.314), calls=%async_computation.6 | async-start | bytes 1179648 | tf_op jit(solution)/shard_map/all_to_all | solution.py:319
  423.8 36.4 %all-to-all-start.5 = ((bf16[16,24,768]{2,1,0:T(8,128)(2,1)}), bf16[16,24,768]{2,1,0:T(8,128)(2,1)}, u32[]{:S(2)}, u32[]{:S(2)}) async-start(bf16[16,24,768]{2,1,0:T(8,128)(2,1)} %convolution_convert_fusion.20), calls=%async_computation.5 | async-start | bytes 1179648 | tf_op jit(solution)/shard_map/all_to_all | solution.py:337
  453.8 13.6 %collective-permute-start = (bf16[48,6144]{1,0:T(8,128)(2,1)}, bf16[48,6144]{1,0:T(8,128)(2,1)S(1)}, u32[]{:S(2)}, u32[]{:S(2)}) collective-permute-start(bf16[48,6144]{1,0:T(8,128)(2,1)} %reduce-scatter.4.cloned.1.call-done), channel_id=1, source_target_pairs={{0,16},{16,0},{1,17},{17,1},{2,18},{18,2},{3,19},{19,3},{4,20},{20... | collective-permute-start | bytes 1769480 | tf_op jit(solution)/shard_map/ppermute | solution.py:192
  460.1 19.9 %all-to-all-start.7 = ((bf16[16,24,768]{2,1,0:T(8,128)(2,1)}), bf16[16,24,768]{2,1,0:T(8,128)(2,1)S(1)}, u32[]{:S(2)}, u32[]{:S(2)}) async-start(bf16[16,24,768]{2,1,0:T(8,128)(2,1)} %convolution_convert_fusion.16), calls=%async_computation.7 | async-start | bytes 1179648 | tf_op jit(solution)/shard_map/all_to_all | solution.py:337
  464.1 80.8 %reduce-scatter.8.cloned.1.call-start = ((), (), s32[]{:S(2)}) async-start(), calls=%async_computation.16 | async-start | bytes 5013504 | tf_op jit(solution)/shard_map/reduce_scatter | solution.py:214
  467.5 12.5 %collective-permute-start.1 = (bf16[48,6144]{1,0:T(8,128)(2,1)S(1)}, bf16[48,6144]{1,0:T(8,128)(2,1)S(1)}, u32[]{:S(2)}, u32[]{:S(2)}) collective-permute-start(bf16[48,6144]{1,0:T(8,128)(2,1)S(1)} %add.247), channel_id=1, source_target_pairs={{0,8},{8,0},{1,9},{9,1},{2,10},{10,2},{3,11},{11,3},{4,12},{12,4},... | collective-permute-start | bytes 1769480 | tf_op jit(solution)/shard_map/ppermute | solution.py:198
  467.7 156.1 %reduce-scatter.6.cloned.1.call-start = ((), (), s32[]{:S(2)}) async-start(), calls=%async_computation.15 | async-start | bytes 5222400 | tf_op jit(solution)/shard_map/reduce_scatter | solution.py:214
  544.9 7.3 %collective-permute-start.4 = (bf16[48,3072]{1,0:T(8,128)(2,1)}, bf16[48,3072]{1,0:T(8,128)(2,1)S(1)}, u32[]{:S(2)}, u32[]{:S(2)}) collective-permute-start(bf16[48,3072]{1,0:T(8,128)(2,1)} %reduce-scatter.8.cloned.1.call-done), channel_id=1, source_target_pairs={{0,16},{16,0},{1,17},{17,1},{2,18},{18,2},{3,19},{19,3},{4,20},{20... | collective-permute-start | bytes 884744 | tf_op jit(solution)/shard_map/ppermute | solution.py:192
  552.3 6.2 collective-permute-start.5
  558.5 73.9 %copy-start.28 = (bf16[2,1,2,192,768]{4,3,2,1,0:T(8,128)(2,1)S(1)}, bf16[2,1,2,192,768]{4,3,2,1,0:T(8,128)(2,1)}, u32[]{:S(2)}) copy-start(bf16[2,1,2,192,768]{4,3,2,1,0:T(8,128)(2,1)} %param.9) | copy-start | bytes 3538948
  558.5 73.9 %copy-start.32 = (f32[2,192,768]{2,1,0:T(8,128)S(1)}, f32[2,192,768]{2,1,0:T(8,128)}, u32[]{:S(2)}) copy-start(f32[2,192,768]{2,1,0:T(8,128)} %copy-done.31) | copy-start | bytes 3538948
  623.8 7.5 %collective-permute-start.2 = (bf16[48,3200]{1,0:T(8,128)(2,1)}, bf16[48,3200]{1,0:T(8,128)(2,1)S(1)}, u32[]{:S(2)}, u32[]{:S(2)}) collective-permute-start(bf16[48,3200]{1,0:T(8,128)(2,1)} %reduce-scatter.6.cloned.1.call-done), channel_id=1, source_target_pairs={{0,16},{16,0},{1,17},{17,1},{2,18},{18,2},{3,19},{19,3},{4,20},{20... | collective-permute-start | bytes 921608 | tf_op jit(solution)/shard_map/ppermute | solution.py:192
  632.3 3.8 collective-permute-start.3
  (128 other events, 677.2 us)
Sparse Core Ops, SparseCore 0:
  10.8 56.8 all-gather.3
  70.5 62.2 all-gather.5
  135.6 99.5 all-gather.7
  317.3 136.4 reduce-scatter.3
  468.5 76.3 reduce-scatter.7
  548.7 74.9 reduce-scatter.5

commit v2 on v1

--- a/solution.py
+++ b/solution.py
@@ -1,5 +1,3 @@
-from functools import partial
-
 import jax
 import jax.numpy as jnp
 from jax import lax
@@ -130,6 +128,10 @@
     )
     stacked = jnp.stack((back_query, back_keys, back_values), axis=-3)
     return stacked.reshape(back_context.shape[:-1] + (3 * D,)).astype(jnp.bfloat16)
+
+
+def gelu(values):
+    return 0.5 * values * (1.0 + lax.erf(values * (0.5 ** 0.5)))
 
 
 def to_member(array, kind, part, half):
@@ -252,7 +254,7 @@
         mixed_two = mixed_one + flat_dot(context_time, t_out)
         normed_three = layer_norm(mixed_two, gain_rows[2]).astype(jnp.bfloat16)
         hidden = flat_dot(normed_three, h_in)
-        activated = jax.nn.gelu(hidden, approximate=False).astype(jnp.bfloat16)
+        activated = gelu(hidden).astype(jnp.bfloat16)
         results.append(mixed_two + flat_dot(activated, h_out))
         saved.append(
             dict(
@@ -290,7 +292,7 @@
         rounded = upstream.astype(jnp.bfloat16)
         hidden_out_terms.append(token_sum(s["activated"], rounded))
         back_active = back_dot(rounded, h_out).astype(jnp.bfloat16)
-        _, gelu_pull = jax.vjp(partial(jax.nn.gelu, approximate=False), s["hidden"])
+        _, gelu_pull = jax.vjp(gelu, s["hidden"])
         back_hidden = gelu_pull(back_active.astype(jnp.float32))[0].astype(jnp.bfloat16)
         hidden_in_terms.append(token_sum(s["normed_three"], back_hidden))
         back_threes.append(back_dot(back_hidden, h_in).astype(jnp.bfloat16))
@@ -337,8 +339,6 @@
         back_two = lax.all_to_all(
             back_twos_placed[index], "fsdp", split_axis=0, concat_axis=1, tiled=True
         )
-        if index == micro - 1:
-            back_two, grad_ffn = lax.optimization_barrier((back_two, grad_ffn))
         back_mixed, gain_grad = norm_back(s["mixed_one"], gain_rows[1], back_two.astype(jnp.float32))
         gain_one_terms.append(gain_grad)
         upstream = upstreams[index] + back_mixed

time: 652 us -> 741 us (1.14)
  waiting for transfers between devices: 220 us -> 342 us
  other arithmetic: 82.6 us -> 54.7 us
    reduce_scatter x3, waiting for transfers between devices: 77.6 us -> 163 us  [reduce_group(): owned = lax.psum_scatter(packed, MEMBERS, scatter_dimension=0, tiled=True)]
    convert_element_type x4 -> x0, other arithmetic: 30.7 us -> none  [the longest x2 27.2 us: layer(): gelu_pull(back_active.astype(jnp.float32))[0].astype(jnp.bfloat16)]
    all_to_all x2, waiting for transfers between devices: 31.7 us -> 51.9 us  [layer(): lax.all_to_all(normed_two, 'fsdp', split_axis=1, concat_axis=0, tiled=True)]
    ppermute x3, waiting for transfers between devices: 9.92 us -> 23.1 us  [pair_sum(): return values + lax.ppermute(values, axis, [(0, 1), (1, 0)])]
    unnamed x268 -> x292, local copies, waits for them, and re-layouts: 24 us -> 24.4 us
  transfers between devices with their start and end apart: 20 -> 20, of which waited for: 12 -> 12; matrix products, arithmetic and copies ran while one was open for 41% -> 28% of each run, Pallas kernels for 0% -> 0%
where the time goes in v2:
time: 741 us; the launch traced here: 735 us
  waiting for transfers between devices  342 us (46%)
  matrix products  160 us (22%)
  local copies, waits for them, and re-layouts  120 us (16%)
  other arithmetic  54.7 us (7%)
  starting transfers between devices  42.6 us (6%)
  between operations  16.7 us (2%)
    reduce_scatter x3, waiting for transfers between devices, reduce_group(): owned = lax.psum_scatter(packed, MEMBERS, scatter_dimension=0, tiled=True)  163 us
    all_gather x3, waiting for transfers between devices, gather_group(): gathered = lax.all_gather(block, MEMBERS, axis=0, tiled=True)  54.4 us
    all_to_all x2, waiting for transfers between devices, layer(): lax.all_to_all(normed_two, 'fsdp', split_axis=1, concat_axis=0, tiled=True)  51.9 us
    dot_general x12, matrix products, flat_dot(): product = jnp.dot(flat, right, preferred_element_type=jnp.float32)  43.6 us
    dot_general x12, matrix products, back_dot(): lax.dot_general(flat, right, (((1,), (1,)), ((), ())), preferred_element_...  38.6 us
    dot_general x12, matrix products, token_sum(): lax.dot_general(left_rows, right_rows, (((0,), (0,)), ((), ())), preferre...  33.5 us
    convert_element_type x8, local copies, waits for them, and re-layouts, attend_back(): stacked.reshape(back_context.shape[:-1] + (3 * D,)).astype(jnp.bfloat16)  32.7 us
    unnamed x292, local copies, waits for them, and re-layouts  24.4 us
  transfers between devices with their start and end apart: 20, of which 12 were waited for; matrix products, arithmetic and copies ran while one was open for 28% of the time, Pallas kernels for 0%

profile of v2, /device:TPU:0, one launch (start us, length us, event | category | flops | bytes accessed | tf_op | source)
XLA Modules:
  0.0 735.2 jit_solution(12045179089398057539)
XLA Ops:
  13.3 54.4 %all-gather.4.cloned.1.call-done = bf16[768,3200]{1,0:T(8,128)(2,1)} async-done(((bf16[48,3200]{1,0:T(8,128)(2,1)}), bf16[768,3200]{1,0:T(8,128)(2,1)}) %all-gather.4.cloned.1.call-update) | async-done | bytes 4915216 | tf_op jit(solution)/shard_map/all_gather | solution.py:188
  75.5 5.0 convolution_convert_fusion.5
  103.8 26.7 %all-to-all-done = bf16[2,192,768]{2,0,1:T(2,128)(2,1)S(1)} async-done(((bf16[2,192,768]{2,0,1:T(2,128)(2,1)}), bf16[2,192,768]{2,0,1:T(2,128)(2,1)S(1)}, u32[]{:S(2)}, u32[]{:S(2)}) %all-to-all-start) | async-done | bytes 589856 | tf_op jit(solution)/shard_map/all_to_all | solution.py:249
  135.0 25.2 %all-to-all-done.2 = bf16[2,192,768]{2,0,1:T(2,128)(2,1)S(1)} async-done(((bf16[2,192,768]{2,0,1:T(2,128)(2,1)}), bf16[2,192,768]{2,0,1:T(2,128)(2,1)S(1)}, u32[]{:S(2)}, u32[]{:S(2)}) %all-to-all-start.2) | async-done | bytes 589856 | tf_op jit(solution)/shard_map/all_to_all | solution.py:249
  189.6 6.5 reshape.597
  208.2 8.7 %all-to-all-done.1 = bf16[16,24,768]{2,1,0:T(8,128)(2,1)} async-done(((bf16[16,24,768]{2,1,0:T(8,128)(2,1)}), bf16[16,24,768]{2,1,0:T(8,128)(2,1)}, u32[]{:S(2)}, u32[]{:S(2)}) %all-to-all-start.1) | async-done | bytes 589856 | tf_op jit(solution)/shard_map/all_to_all | solution.py:251
  225.6 15.1 %all-to-all-done.3 = bf16[16,24,768]{2,1,0:T(8,128)(2,1)S(1)} async-done(((bf16[16,24,768]{2,1,0:T(8,128)(2,1)}), bf16[16,24,768]{2,1,0:T(8,128)(2,1)S(1)}, u32[]{:S(2)}, u32[]{:S(2)}) %all-to-all-start.3) | async-done | bytes 589856 | tf_op jit(solution)/shard_map/all_to_all | solution.py:251
  265.3 5.6 fusion.126
  276.5 6.0 add_convert_fusion.2
  286.1 5.6 fusion.1
  296.6 5.2 fusion.52
  320.7 9.4 %all-to-all-done.4 = bf16[2,192,768]{2,0,1:T(2,128)(2,1)} async-done(((bf16[2,192,768]{2,0,1:T(2,128)(2,1)}), bf16[2,192,768]{2,0,1:T(2,128)(2,1)}, u32[]{:S(2)}, u32[]{:S(2)}) %all-to-all-start.4) | async-done | bytes 589856 | tf_op jit(solution)/shard_map/all_to_all | solution.py:321
  369.9 5.5 convert_element_type.481
  375.4 6.6 convert_element_type.455
  392.0 6.4 all-to-all-start.5
  398.5 6.6 convert_element_type.488
  411.2 6.7 convert_element_type.491
  427.6 6.0 all-to-all-start.7
  434.3 14.3 %all-to-all-done.7 = bf16[16,24,768]{2,1,0:T(8,128)(2,1)S(1)} async-done(((bf16[16,24,768]{2,1,0:T(8,128)(2,1)}), bf16[16,24,768]{2,1,0:T(8,128)(2,1)S(1)}, u32[]{:S(2)}, u32[]{:S(2)}) %all-to-all-start.7) | async-done | bytes 589856 | tf_op jit(solution)/shard_map/all_to_all | solution.py:339
  515.0 5.2 fusion.50
  525.6 5.2 collective-permute-done.2
  535.8 58.3 %reduce-scatter.4.cloned.1.call-done = bf16[48,3200]{1,0:T(8,128)(2,1)} async-done(((bf16[768,3200]{1,0:T(8,128)(2,1)}), bf16[48,3200]{1,0:T(8,128)(2,1)}) %reduce-scatter.4.cloned.1.call-update) | async-done | bytes 307216 | tf_op jit(solution)/shard_map/reduce_scatter | solution.py:216
  602.9 105.2 %reduce-scatter.8.cloned.1.call-done = bf16[48,6144]{1,0:T(8,128)(2,1)} async-done(((bf16[768,6144]{1,0:T(8,128)(2,1)}), bf16[48,6144]{1,0:T(8,128)(2,1)}) %reduce-scatter.8.cloned.1.call-update) | async-done | bytes 589840 | tf_op jit(solution)/shard_map/reduce_scatter | solution.py:216
  709.6 13.5 %collective-permute-done.4 = bf16[48,6144]{1,0:T(8,128)(2,1)S(1)} collective-permute-done((bf16[48,6144]{1,0:T(8,128)(2,1)}, bf16[48,6144]{1,0:T(8,128)(2,1)S(1)}, u32[]{:S(2)}, u32[]{:S(2)}) %collective-permute-start.4) | collective-permute-done | bytes 589856 | tf_op jit(solution)/shard_map/ppermute | solution.py:194
  (522 shorter events, 305.7 us)
Async XLA Ops:
  7.2 60.4 %all-gather.4.cloned.1.call-start = ((), (), s32[]{:S(2)}) async-start(), calls=%async_computation.11 | async-start | bytes 5222400 | tf_op jit(solution)/shard_map/all_gather | solution.py:188
  9.9 150.4 %all-gather.6.cloned.1.call-start = ((), (), s32[]{:S(2)}) async-start(), calls=%async_computation.12 | async-start | bytes 5013504 | tf_op jit(solution)/shard_map/all_gather | solution.py:188
  10.8 239.4 %all-gather.8.cloned.1.call-start = ((), (), s32[]{:S(2)}) async-start(), calls=%async_computation.13 | async-start | bytes 10027008 | tf_op jit(solution)/shard_map/all_gather | solution.py:188
  12.2 60.7 %copy-start.115 = (f32[2,192]{1,0:T(2,128)}, f32[2,192]{1,0:T(2,128)S(1)}, u32[]{:S(2)}) copy-start(f32[2,192]{1,0:T(2,128)S(1)} %get-tuple-element.153) | copy-start | bytes 4612
  12.2 63.3 %copy-start.117 = (f32[2,192]{1,0:T(2,128)}, f32[2,192]{1,0:T(2,128)S(1)}, u32[]{:S(2)}) copy-start(f32[2,192]{1,0:T(2,128)S(1)} %get-tuple-element.154) | copy-start | bytes 4612
  13.3 62.2 %copy-start.119 = (f32[2,192]{1,0:T(2,128)}, f32[2,192]{1,0:T(2,128)S(1)}, u32[]{:S(2)}) copy-start(f32[2,192]{1,0:T(2,128)S(1)} %fusion.135) | copy-start | bytes 4612
  98.8 31.7 %all-to-all-start = ((bf16[2,192,768]{2,0,1:T(2,128)(2,1)}), bf16[2,192,768]{2,0,1:T(2,128)(2,1)S(1)}, u32[]{:S(2)}, u32[]{:S(2)}) async-start(bf16[2,192,768]{2,0,1:T(2,128)(2,1)} %copy.274), calls=%async_computation | async-start | bytes 1179648 | tf_op jit(solution)/shard_map/all_to_all | solution.py:249
  130.5 29.7 %all-to-all-start.2 = ((bf16[2,192,768]{2,0,1:T(2,128)(2,1)}), bf16[2,192,768]{2,0,1:T(2,128)(2,1)S(1)}, u32[]{:S(2)}, u32[]{:S(2)}) async-start(bf16[2,192,768]{2,0,1:T(2,128)(2,1)} %copy.289), calls=%async_computation.2 | async-start | bytes 1179648 | tf_op jit(solution)/shard_map/all_to_all | solution.py:249
  180.3 36.6 %all-to-all-start.1 = ((bf16[16,24,768]{2,1,0:T(8,128)(2,1)}), bf16[16,24,768]{2,1,0:T(8,128)(2,1)}, u32[]{:S(2)}, u32[]{:S(2)}) async-start(bf16[16,24,768]{2,1,0:T(8,128)(2,1)} %convert_element_type.421), calls=%async_computation.1 | async-start | bytes 1179648 | tf_op jit(solution)/shard_map/all_to_all | solution.py:251
  216.9 23.8 %all-to-all-start.3 = ((bf16[16,24,768]{2,1,0:T(8,128)(2,1)}), bf16[16,24,768]{2,1,0:T(8,128)(2,1)S(1)}, u32[]{:S(2)}, u32[]{:S(2)}) async-start(bf16[16,24,768]{2,1,0:T(8,128)(2,1)} %convert_element_type.437), calls=%async_computation.3 | async-start | bytes 1179648 | tf_op jit(solution)/shard_map/all_to_all | solution.py:251
  309.9 20.3 %all-to-all-start.4 = ((bf16[2,192,768]{2,0,1:T(2,128)(2,1)}), bf16[2,192,768]{2,0,1:T(2,128)(2,1)}, u32[]{:S(2)}, u32[]{:S(2)}) async-start(bf16[2,192,768]{2,0,1:T(2,128)(2,1)} %copy.298), calls=%async_computation.4 | async-start | bytes 1179648 | tf_op jit(solution)/shard_map/all_to_all | solution.py:321
  330.2 20.3 %all-to-all-start.6 = ((bf16[2,192,768]{2,0,1:T(2,128)(2,1)}), bf16[2,192,768]{2,0,1:T(2,128)(2,1)S(1)}, u32[]{:S(2)}, u32[]{:S(2)}) async-start(bf16[2,192,768]{2,0,1:T(2,128)(2,1)} %copy.314), calls=%async_computation.6 | async-start | bytes 1179648 | tf_op jit(solution)/shard_map/all_to_all | solution.py:321
  392.0 35.6 %all-to-all-start.5 = ((bf16[16,24,768]{2,1,0:T(8,128)(2,1)}), bf16[16,24,768]{2,1,0:T(8,128)(2,1)S(1)}, u32[]{:S(2)}, u32[]{:S(2)}) async-start(bf16[16,24,768]{2,1,0:T(8,128)(2,1)} %convolution_convert_fusion.20), calls=%async_computation.5 | async-start | bytes 1179648 | tf_op jit(solution)/shard_map/all_to_all | solution.py:339
  427.6 21.0 %all-to-all-start.7 = ((bf16[16,24,768]{2,1,0:T(8,128)(2,1)}), bf16[16,24,768]{2,1,0:T(8,128)(2,1)S(1)}, u32[]{:S(2)}, u32[]{:S(2)}) async-start(bf16[16,24,768]{2,1,0:T(8,128)(2,1)} %convolution_convert_fusion.16), calls=%async_computation.7 | async-start | bytes 1179648 | tf_op jit(solution)/shard_map/all_to_all | solution.py:339
  433.6 90.3 %reduce-scatter.6.cloned.1.call-start = ((), (), s32[]{:S(2)}) async-start(), calls=%async_computation.15 | async-start | bytes 5013504 | tf_op jit(solution)/shard_map/reduce_scatter | solution.py:216
  434.2 159.8 %reduce-scatter.4.cloned.1.call-start = ((), (), s32[]{:S(2)}) async-start(), calls=%async_computation.14 | async-start | bytes 5222400 | tf_op jit(solution)/shard_map/reduce_scatter | solution.py:216
  514.4 193.6 %reduce-scatter.8.cloned.1.call-start = ((), (), s32[]{:S(2)}) async-start(), calls=%async_computation.16 | async-start | bytes 10027008 | tf_op jit(solution)/shard_map/reduce_scatter | solution.py:216
  523.9 6.9 collective-permute-start.2
  531.9 63.6 %collective-permute-start.3 = (bf16[48,3072]{1,0:T(8,128)(2,1)S(1)}, bf16[48,3072]{1,0:T(8,128)(2,1)}, u32[]{:S(2)}, u32[]{:S(2)}) collective-permute-start(bf16[48,3072]{1,0:T(8,128)(2,1)S(1)} %add.268), channel_id=1, source_target_pairs={{0,8},{8,0},{1,9},{9,1},{2,10},{10,2},{3,11},{11,3},{4,12},{12,4},... | collective-permute-start | bytes 884744 | tf_op jit(solution)/shard_map/ppermute | solution.py:200
  534.2 61.3 %copy-start.92 = (bf16[48,3072]{1,0:T(8,128)(2,1)S(1)}, bf16[48,3072]{1,0:T(8,128)(2,1)}, u32[]{:S(2)}) copy-start(bf16[48,3072]{1,0:T(8,128)(2,1)} %copy-done.91) | copy-start | bytes 884740
  594.0 7.7 %collective-permute-start = (bf16[48,3200]{1,0:T(8,128)(2,1)}, bf16[48,3200]{1,0:T(8,128)(2,1)S(1)}, u32[]{:S(2)}, u32[]{:S(2)}) collective-permute-start(bf16[48,3200]{1,0:T(8,128)(2,1)} %reduce-scatter.4.cloned.1.call-done), channel_id=1, source_target_pairs={{0,16},{16,0},{1,17},{17,1},{2,18},{18,2},{3,19},{19,3},{4,20},{20... | collective-permute-start | bytes 921608 | tf_op jit(solution)/shard_map/ppermute | solution.py:194
  601.8 107.7 %collective-permute-start.1 = (bf16[48,3200]{1,0:T(8,128)(2,1)S(1)}, bf16[48,3200]{1,0:T(8,128)(2,1)S(1)}, u32[]{:S(2)}, u32[]{:S(2)}) collective-permute-start(bf16[48,3200]{1,0:T(8,128)(2,1)S(1)} %add.267), channel_id=1, source_target_pairs={{0,8},{8,0},{1,9},{9,1},{2,10},{10,2},{3,11},{11,3},{4,12},{12,4},... | collective-permute-start | bytes 921608 | tf_op jit(solution)/shard_map/ppermute | solution.py:200
  708.1 15.0 %collective-permute-start.4 = (bf16[48,6144]{1,0:T(8,128)(2,1)}, bf16[48,6144]{1,0:T(8,128)(2,1)S(1)}, u32[]{:S(2)}, u32[]{:S(2)}) collective-permute-start(bf16[48,6144]{1,0:T(8,128)(2,1)} %reduce-scatter.8.cloned.1.call-done), channel_id=1, source_target_pairs={{0,16},{16,0},{1,17},{17,1},{2,18},{18,2},{3,19},{19,3},{4,20},{20... | collective-permute-start | bytes 1769480 | tf_op jit(solution)/shard_map/ppermute | solution.py:194
  723.2 2.5 collective-permute-start.5
  (140 other events, 660.2 us)
Sparse Core Ops, SparseCore 0:
  10.8 56.8 all-gather.3
  70.5 62.2 all-gather.5
  135.6 103.9 all-gather.7
  438.0 76.9 reduce-scatter.5
  518.8 75.1 reduce-scatter.3
  598.0 110.0 reduce-scatter.7

commit v3 on v2

--- a/solution.py
+++ b/solution.py
@@ -132,6 +132,22 @@
 
 def gelu(values):
     return 0.5 * values * (1.0 + lax.erf(values * (0.5 ** 0.5)))
+
+
+def to_places(frames_major):
+    peers = lax.axis_size("fsdp")
+    frames, places, width = frames_major.shape
+    blocks = frames_major.reshape(frames, peers, places // peers, width).transpose(1, 0, 2, 3)
+    blocks = lax.all_to_all(blocks, "fsdp", split_axis=0, concat_axis=0, tiled=True)
+    return blocks.reshape(peers * frames, places // peers, width)
+
+
+def to_frames(places_major):
+    peers = lax.axis_size("fsdp")
+    all_frames, places, width = places_major.shape
+    blocks = places_major.reshape(peers, all_frames // peers, places, width)
+    blocks = lax.all_to_all(blocks, "fsdp", split_axis=0, concat_axis=0, tiled=True)
+    return blocks.transpose(1, 0, 2, 3).reshape(all_frames // peers, peers * places, width)
 
 
 def to_member(array, kind, part, half):
@@ -246,11 +262,9 @@
         join_space, total_space, context_space = attend_core(normed_one, s_in, *spatial)
         mixed_one = frames_in + flat_dot(context_space, s_out)
         normed_two = layer_norm(mixed_one, gain_rows[1]).astype(jnp.bfloat16)
-        placed = lax.all_to_all(normed_two, "fsdp", split_axis=1, concat_axis=0, tiled=True)
+        placed = to_places(normed_two)
         join_time, total_time, context_placed = attend_core(placed, t_in, *temporal)
-        context_time = lax.all_to_all(
-            context_placed, "fsdp", split_axis=0, concat_axis=1, tiled=True
-        )
+        context_time = to_frames(context_placed)
         mixed_two = mixed_one + flat_dot(context_time, t_out)
         normed_three = layer_norm(mixed_two, gain_rows[2]).astype(jnp.bfloat16)
         hidden = flat_dot(normed_three, h_in)
@@ -275,6 +289,11 @@
             )
         )
 
+    def pooled(pairs):
+        lefts = [left.reshape(-1, left.shape[-1]) for left, _ in pairs]
+        rights = [right.reshape(-1, right.shape[-1]) for _, right in pairs]
+        return token_sum(jnp.concatenate(lefts, axis=0), jnp.concatenate(rights, axis=0))
+
     def summed(terms):
         total = terms[0]
         for term in terms[1:]:
@@ -290,14 +309,14 @@
         s = saved[index]
         upstream = cotangent[index, 0].astype(jnp.float32)
         rounded = upstream.astype(jnp.bfloat16)
-        hidden_out_terms.append(token_sum(s["activated"], rounded))
+        hidden_out_terms.append((s["activated"], rounded))
         back_active = back_dot(rounded, h_out).astype(jnp.bfloat16)
         _, gelu_pull = jax.vjp(gelu, s["hidden"])
         back_hidden = gelu_pull(back_active.astype(jnp.float32))[0].astype(jnp.bfloat16)
-        hidden_in_terms.append(token_sum(s["normed_three"], back_hidden))
+        hidden_in_terms.append((s["normed_three"], back_hidden))
         back_threes.append(back_dot(back_hidden, h_in).astype(jnp.bfloat16))
         upstreams.append(upstream)
-    ffn_grads = (summed(hidden_in_terms), summed(hidden_out_terms))
+    ffn_grads = (pooled(hidden_in_terms), pooled(hidden_out_terms))
     ffn_kinds = ("plain", "grouped")
     packed_ffn, back_threes[-1] = lax.optimization_barrier(
         (pack_group(ffn_grads, ffn_kinds, members, half), back_threes[-1])
@@ -316,13 +335,13 @@
         upstream = upstreams[index] + back_mixed
         upstreams[index] = upstream
         rounded = upstream.astype(jnp.bfloat16)
-        time_out_terms.append(token_sum(s["context_time"], rounded))
+        time_out_terms.append((s["context_time"], rounded))
         back_context = back_dot(rounded, t_out).astype(jnp.bfloat16)
-        back_placed = lax.all_to_all(back_context, "fsdp", split_axis=1, concat_axis=0, tiled=True)
+        back_placed = to_places(back_context)
         back_join = attend_back(s["join_time"], s["total_time"], back_placed, *temporal)
-        time_in_terms.append(token_sum(s["placed"], back_join))
+        time_in_terms.append((s["placed"], back_join))
         back_twos_placed.append(back_dot(back_join, t_in).astype(jnp.bfloat16))
-    time_grads = (summed(time_in_terms), summed(time_out_terms))
+    time_grads = (pooled(time_in_terms), pooled(time_out_terms))
     time_kinds = ("plain", "plain")
     packed_time, back_twos_placed[-1] = lax.optimization_barrier(
         (pack_group(time_grads, time_kinds, members, half), back_twos_placed[-1])
@@ -336,25 +355,23 @@
     space_in_terms = []
     for index in range(micro):
         s = saved[index]
-        back_two = lax.all_to_all(
-            back_twos_placed[index], "fsdp", split_axis=0, concat_axis=1, tiled=True
-        )
+        back_two = to_frames(back_twos_placed[index])
         back_mixed, gain_grad = norm_back(s["mixed_one"], gain_rows[1], back_two.astype(jnp.float32))
         gain_one_terms.append(gain_grad)
         upstream = upstreams[index] + back_mixed
         rounded = upstream.astype(jnp.bfloat16)
-        space_out_terms.append(token_sum(s["context_space"], rounded))
+        space_out_terms.append((s["context_space"], rounded))
         back_context = back_dot(rounded, s_out).astype(jnp.bfloat16)
         back_join = attend_back(s["join_space"], s["total_space"], back_context, *spatial)
-        space_in_terms.append(token_sum(s["normed_one"], back_join))
+        space_in_terms.append((s["normed_one"], back_join))
         back_one = back_dot(back_join, s_in).astype(jnp.bfloat16)
         back_mixed, gain_grad = norm_back(
             s["frames_in"], gain_rows[0], back_one.astype(jnp.float32)
         )
         gain_zero_terms.append(gain_grad)
         input_grads.append(upstream + back_mixed)
-    grad_space_in = summed(space_in_terms)
-    grad_space_out = summed(space_out_terms)
+    grad_space_in = pooled(space_in_terms)
+    grad_space_out = pooled(space_out_terms)
     gain_grad_zero = summed(gain_zero_terms)
     gain_grad_one = summed(gain_one_terms)
     gain_grad_two = summed(gain_two_terms)

time: 741 us -> 734 us (level)
  waiting for transfers between devices: 342 us -> 311 us
  local copies, waits for them, and re-layouts: 120 us -> 146 us
    all_to_all x8, waiting for transfers between devices: 99.4 us -> 75.5 us  [the longest x4 43.6 us: to_places(): lax.all_to_all(blocks, 'fsdp', split_axis=0, concat_axis=0, tiled=True)]
    convert_element_type x8 -> x12, local copies, waits for them, and re-layouts: 32.7 us -> 56.3 us  [attend_back(): stacked.reshape(back_context.shape[:-1] + (3 * D,)).astype(jnp.bfloat16)]
    convert_element_type x4 -> x8, local copies, waits for them, and re-layouts: 8.81 us -> 18.4 us  [attend_core(): context = context.reshape(normed.shape[:-1] + (D,)).astype(jnp.bfloat16)]
    dot_general x12 -> x6, matrix products: 33.5 us -> 24.2 us  [token_sum(): lax.dot_general(left_rows, right_rows, (((0,), (0,)), ((), ())), preferre...]
    unnamed x292 -> x282, local copies, waits for them, and re-layouts: 24.4 us -> 24.6 us
  transfers between devices with their start and end apart: 20 -> 20, of which waited for: 12 -> 13; matrix products, arithmetic and copies ran while one was open for 28% -> 33% of each run, Pallas kernels for 0% -> 0%
where the time goes in v3:
time: 734 us; the launch traced here: 728 us
  waiting for transfers between devices  311 us (42%)
  matrix products  154 us (21%)
  local copies, waits for them, and re-layouts  146 us (20%)
  other arithmetic  57.7 us (8%)
  starting transfers between devices  42 us (6%)
  between operations  16.5 us (2%)
    reduce_scatter x3, waiting for transfers between devices, reduce_group(): owned = lax.psum_scatter(packed, MEMBERS, scatter_dimension=0, tiled=True)  157 us
    convert_element_type x12, local copies, waits for them, and re-layouts, attend_back(): stacked.reshape(back_context.shape[:-1] + (3 * D,)).astype(jnp.bfloat16)  56.3 us
    all_gather x3, waiting for transfers between devices, gather_group(): gathered = lax.all_gather(block, MEMBERS, axis=0, tiled=True)  54.4 us
    dot_general x12, matrix products, flat_dot(): product = jnp.dot(flat, right, preferred_element_type=jnp.float32)  44.1 us
    all_to_all x4, waiting for transfers between devices, to_places(): lax.all_to_all(blocks, 'fsdp', split_axis=0, concat_axis=0, tiled=True)  43.6 us
    dot_general x12, matrix products, back_dot(): lax.dot_general(flat, right, (((1,), (1,)), ((), ())), preferred_element_...  40.3 us
    all_to_all x4, waiting for transfers between devices, to_frames(): lax.all_to_all(blocks, 'fsdp', split_axis=0, concat_axis=0, tiled=True)  31.9 us
    unnamed x282, local copies, waits for them, and re-layouts  24.6 us
  transfers between devices with their start and end apart: 20, of which 13 were waited for; matrix products, arithmetic and copies ran while one was open for 33% of the time, Pallas kernels for 0%

profile of v3, /device:TPU:0, one launch (start us, length us, event | category | flops | bytes accessed | tf_op | source)
XLA Modules:
  0.0 727.6 jit_solution(6623113123805611322)
XLA Ops:
  13.3 54.4 %all-gather.4.cloned.1.call-done = bf16[768,3200]{1,0:T(8,128)(2,1)} async-done(((bf16[48,3200]{1,0:T(8,128)(2,1)}), bf16[768,3200]{1,0:T(8,128)(2,1)}) %all-gather.4.cloned.1.call-update) | async-done | bytes 4915216 | tf_op jit(solution)/shard_map/all_gather | solution.py:204
  103.8 26.7 %all-to-all-done.2 = bf16[8,2,24,768]{3,2,1,0:T(8,128)(2,1)S(1)} async-done(((bf16[8,2,24,768]{3,2,1,0:T(8,128)(2,1)}), bf16[8,2,24,768]{3,2,1,0:T(8,128)(2,1)S(1)}, u32[]{:S(2)}, u32[]{:S(2)}) %all-to-all-start.2) | async-done | bytes 589856 | tf_op jit(solution)/shard_map/all_to_all | solution.py:141
  154.8 5.5 all-to-all-done
  170.3 6.4 reshape.596
  190.4 5.3 all-to-all-start.1
  199.2 29.0 %all-to-all-done.1 = bf16[8,2,24,768]{3,2,1,0:T(8,128)(2,1)} async-done(((bf16[8,2,24,768]{3,2,1,0:T(8,128)(2,1)}), bf16[8,2,24,768]{3,2,1,0:T(8,128)(2,1)}, u32[]{:S(2)}, u32[]{:S(2)}) %all-to-all-start.1) | async-done | bytes 589856 | tf_op jit(solution)/shard_map/all_to_all | solution.py:149
  273.2 5.2 fusion.49
  294.9 10.3 %all-to-all-done.6 = bf16[8,2,24,768]{3,2,1,0:T(8,128)(2,1)} async-done(((bf16[8,2,24,768]{3,2,1,0:T(8,128)(2,1)}), bf16[8,2,24,768]{3,2,1,0:T(8,128)(2,1)}, u32[]{:S(2)}, u32[]{:S(2)}) %all-to-all-start.6) | async-done | bytes 589856 | tf_op jit(solution)/shard_map/all_to_all | solution.py:141
  341.6 6.5 convert_element_type.466
  348.2 6.8 convert_element_type.441
  360.2 6.7 convert_element_type.473
  371.4 5.1 all-to-all-start.5
  376.5 7.0 convolution_convert_fusion.1
  383.5 6.6 convert_element_type.476
  390.0 5.1 pad_maximum_fusion.3
  395.2 5.0 convolution_convert_fusion.22
  401.0 6.0 all-to-all-start.7
  478.1 6.0 convert_element_type.496
  484.1 6.1 convert_element_type.497
  511.2 5.2 fusion.47
  524.1 5.8 collective-permute-done.2
  534.8 51.6 %reduce-scatter.4.cloned.1.call-done = bf16[48,3200]{1,0:T(8,128)(2,1)} async-done(((bf16[768,3200]{1,0:T(8,128)(2,1)}), bf16[48,3200]{1,0:T(8,128)(2,1)}) %reduce-scatter.4.cloned.1.call-update) | async-done | bytes 307216 | tf_op jit(solution)/shard_map/reduce_scatter | solution.py:232
  595.2 105.3 %reduce-scatter.8.cloned.1.call-done = bf16[48,6144]{1,0:T(8,128)(2,1)} async-done(((bf16[768,6144]{1,0:T(8,128)(2,1)}), bf16[48,6144]{1,0:T(8,128)(2,1)}) %reduce-scatter.8.cloned.1.call-update) | async-done | bytes 589840 | tf_op jit(solution)/shard_map/reduce_scatter | solution.py:232
  702.0 13.5 %collective-permute-done.4 = bf16[48,6144]{1,0:T(8,128)(2,1)S(1)} collective-permute-done((bf16[48,6144]{1,0:T(8,128)(2,1)}, bf16[48,6144]{1,0:T(8,128)(2,1)S(1)}, u32[]{:S(2)}, u32[]{:S(2)}) %collective-permute-start.4) | collective-permute-done | bytes 589856 | tf_op jit(solution)/shard_map/ppermute | solution.py:210
  (514 shorter events, 320.2 us)
Async XLA Ops:
  7.2 60.4 %all-gather.4.cloned.1.call-start = ((), (), s32[]{:S(2)}) async-start(), calls=%async_computation.11 | async-start | bytes 5222400 | tf_op jit(solution)/shard_map/all_gather | solution.py:204
  9.9 125.0 %all-gather.6.cloned.1.call-start = ((), (), s32[]{:S(2)}) async-start(), calls=%async_computation.12 | async-start | bytes 5013504 | tf_op jit(solution)/shard_map/all_gather | solution.py:204
  10.8 226.2 %all-gather.8.cloned.1.call-start = ((), (), s32[]{:S(2)}) async-start(), calls=%async_computation.13 | async-start | bytes 10027008 | tf_op jit(solution)/shard_map/all_gather | solution.py:204
  12.2 60.7 %copy-start.102 = (f32[2,192]{1,0:T(2,128)}, f32[2,192]{1,0:T(2,128)S(1)}, u32[]{:S(2)}) copy-start(f32[2,192]{1,0:T(2,128)S(1)} %get-tuple-element.151) | copy-start | bytes 4612
  12.2 63.3 %copy-start.104 = (f32[2,192]{1,0:T(2,128)}, f32[2,192]{1,0:T(2,128)S(1)}, u32[]{:S(2)}) copy-start(f32[2,192]{1,0:T(2,128)S(1)} %get-tuple-element.152) | copy-start | bytes 4612
  12.7 60.2 %copy-start.117 = (f32[2,192]{1,0:T(2,128)}, f32[2,192]{1,0:T(2,128)S(1)}, u32[]{:S(2)}) copy-start(f32[2,192]{1,0:T(2,128)S(1)} %get-tuple-element.70) | copy-start | bytes 4612
  13.3 62.2 %copy-start.113 = (f32[2,192]{1,0:T(2,128)}, f32[2,192]{1,0:T(2,128)S(1)}, u32[]{:S(2)}) copy-start(f32[2,192]{1,0:T(2,128)S(1)} %fusion.145) | copy-start | bytes 4612
  99.3 31.1 %all-to-all-start.2 = ((bf16[8,2,24,768]{3,2,1,0:T(8,128)(2,1)}), bf16[8,2,24,768]{3,2,1,0:T(8,128)(2,1)S(1)}, u32[]{:S(2)}, u32[]{:S(2)}) async-start(bf16[8,2,24,768]{3,2,1,0:T(8,128)(2,1)} %bitcast.416), calls=%async_computation.2 | async-start | bytes 1179648 | tf_op jit(solution)/shard_map/all_to_all | solution.py:141
  130.4 29.9 %all-to-all-start = ((bf16[8,2,24,768]{3,2,1,0:T(8,128)(2,1)}), bf16[8,2,24,768]{3,2,1,0:T(8,128)(2,1)S(1)}, u32[]{:S(2)}, u32[]{:S(2)}) async-start(bf16[8,2,24,768]{3,2,1,0:T(8,128)(2,1)} %bitcast.417), calls=%async_computation | async-start | bytes 1179648 | tf_op jit(solution)/shard_map/all_to_all | solution.py:141
  161.2 29.2 %all-to-all-start.3 = ((bf16[8,2,24,768]{3,2,1,0:T(8,128)(2,1)}), bf16[8,2,24,768]{3,2,1,0:T(8,128)(2,1)S(1)}, u32[]{:S(2)}, u32[]{:S(2)}) async-start(bf16[8,2,24,768]{3,2,1,0:T(8,128)(2,1)} %convert_element_type.423), calls=%async_computation.3 | async-start | bytes 1179648 | tf_op jit(solution)/shard_map/all_to_all | solution.py:149
  190.4 37.8 %all-to-all-start.1 = ((bf16[8,2,24,768]{3,2,1,0:T(8,128)(2,1)}), bf16[8,2,24,768]{3,2,1,0:T(8,128)(2,1)}, u32[]{:S(2)}, u32[]{:S(2)}) async-start(bf16[8,2,24,768]{3,2,1,0:T(8,128)(2,1)} %convert_element_type.407), calls=%async_computation.1 | async-start | bytes 1179648 | tf_op jit(solution)/shard_map/all_to_all | solution.py:149
  285.4 19.9 %all-to-all-start.6 = ((bf16[8,2,24,768]{3,2,1,0:T(8,128)(2,1)}), bf16[8,2,24,768]{3,2,1,0:T(8,128)(2,1)}, u32[]{:S(2)}, u32[]{:S(2)}) async-start(bf16[8,2,24,768]{3,2,1,0:T(8,128)(2,1)} %bitcast.457), calls=%async_computation.6 | async-start | bytes 1179648 | tf_op jit(solution)/shard_map/all_to_all | solution.py:141
  305.2 19.8 %all-to-all-start.4 = ((bf16[8,2,24,768]{3,2,1,0:T(8,128)(2,1)}), bf16[8,2,24,768]{3,2,1,0:T(8,128)(2,1)}, u32[]{:S(2)}, u32[]{:S(2)}) async-start(bf16[8,2,24,768]{3,2,1,0:T(8,128)(2,1)} %bitcast.456), calls=%async_computation.4 | async-start | bytes 1179648 | tf_op jit(solution)/shard_map/all_to_all | solution.py:141
  371.4 28.7 %all-to-all-start.5 = ((bf16[8,2,24,768]{3,2,1,0:T(8,128)(2,1)}), bf16[8,2,24,768]{3,2,1,0:T(8,128)(2,1)S(1)}, u32[]{:S(2)}, u32[]{:S(2)}) async-start(bf16[8,2,24,768]{3,2,1,0:T(8,128)(2,1)} %bitcast.469), calls=%async_computation.5 | async-start | bytes 1179648 | tf_op jit(solution)/shard_map/all_to_all | solution.py:149
  401.0 20.6 %all-to-all-start.7 = ((bf16[8,2,24,768]{3,2,1,0:T(8,128)(2,1)}), bf16[8,2,24,768]{3,2,1,0:T(8,128)(2,1)}, u32[]{:S(2)}, u32[]{:S(2)}) async-start(bf16[8,2,24,768]{3,2,1,0:T(8,128)(2,1)} %bitcast.99), calls=%async_computation.7 | async-start | bytes 1179648 | tf_op jit(solution)/shard_map/all_to_all | solution.py:149
  407.0 115.7 %reduce-scatter.6.cloned.1.call-start = ((), (), s32[]{:S(2)}) async-start(), calls=%async_computation.15 | async-start | bytes 5013504 | tf_op jit(solution)/shard_map/reduce_scatter | solution.py:232
  418.3 168.1 %reduce-scatter.4.cloned.1.call-start = ((), (), s32[]{:S(2)}) async-start(), calls=%async_computation.14 | async-start | bytes 5222400 | tf_op jit(solution)/shard_map/reduce_scatter | solution.py:232
  510.6 189.8 %reduce-scatter.8.cloned.1.call-start = ((), (), s32[]{:S(2)}) async-start(), calls=%async_computation.16 | async-start | bytes 10027008 | tf_op jit(solution)/shard_map/reduce_scatter | solution.py:232
  522.7 7.2 collective-permute-start.2
  531.0 56.9 %collective-permute-start.3 = (bf16[48,3072]{1,0:T(8,128)(2,1)S(1)}, bf16[48,3072]{1,0:T(8,128)(2,1)}, u32[]{:S(2)}, u32[]{:S(2)}) collective-permute-start(bf16[48,3072]{1,0:T(8,128)(2,1)S(1)} %add.248), channel_id=1, source_target_pairs={{0,8},{8,0},{1,9},{9,1},{2,10},{10,2},{3,11},{11,3},{4,12},{12,4},... | collective-permute-start | bytes 884744 | tf_op jit(solution)/shard_map/ppermute | solution.py:216
  586.4 7.6 %collective-permute-start = (bf16[48,3200]{1,0:T(8,128)(2,1)}, bf16[48,3200]{1,0:T(8,128)(2,1)S(1)}, u32[]{:S(2)}, u32[]{:S(2)}) collective-permute-start(bf16[48,3200]{1,0:T(8,128)(2,1)} %reduce-scatter.4.cloned.1.call-done), channel_id=1, source_target_pairs={{0,16},{16,0},{1,17},{17,1},{2,18},{18,2},{3,19},{19,3},{4,20},{20... | collective-permute-start | bytes 921608 | tf_op jit(solution)/shard_map/ppermute | solution.py:210
  594.1 107.8 %collective-permute-start.1 = (bf16[48,3200]{1,0:T(8,128)(2,1)S(1)}, bf16[48,3200]{1,0:T(8,128)(2,1)S(1)}, u32[]{:S(2)}, u32[]{:S(2)}) collective-permute-start(bf16[48,3200]{1,0:T(8,128)(2,1)S(1)} %add.247), channel_id=1, source_target_pairs={{0,8},{8,0},{1,9},{9,1},{2,10},{10,2},{3,11},{11,3},{4,12},{12,4},... | collective-permute-start | bytes 921608 | tf_op jit(solution)/shard_map/ppermute | solution.py:216
  700.4 15.0 %collective-permute-start.4 = (bf16[48,6144]{1,0:T(8,128)(2,1)}, bf16[48,6144]{1,0:T(8,128)(2,1)S(1)}, u32[]{:S(2)}, u32[]{:S(2)}) collective-permute-start(bf16[48,6144]{1,0:T(8,128)(2,1)} %reduce-scatter.8.cloned.1.call-done), channel_id=1, source_target_pairs={{0,16},{16,0},{1,17},{17,1},{2,18},{18,2},{3,19},{19,3},{4,20},{20... | collective-permute-start | bytes 1769480 | tf_op jit(solution)/shard_map/ppermute | solution.py:210
  715.6 2.5 collective-permute-start.5
  (135 other events, 667.0 us)
Sparse Core Ops, SparseCore 0:
  10.8 56.8 all-gather.3
  70.5 62.2 all-gather.5
  135.1 100.0 all-gather.7
  418.5 76.9 reduce-scatter.5
  510.7 75.6 reduce-scatter.3
  590.4 110.0 reduce-scatter.7

commit v4 on v3

--- a/solution.py
+++ b/solution.py
@@ -289,11 +289,6 @@
             )
         )
 
-    def pooled(pairs):
-        lefts = [left.reshape(-1, left.shape[-1]) for left, _ in pairs]
-        rights = [right.reshape(-1, right.shape[-1]) for _, right in pairs]
-        return token_sum(jnp.concatenate(lefts, axis=0), jnp.concatenate(rights, axis=0))
-
     def summed(terms):
         total = terms[0]
         for term in terms[1:]:
@@ -309,17 +304,17 @@
         s = saved[index]
         upstream = cotangent[index, 0].astype(jnp.float32)
         rounded = upstream.astype(jnp.bfloat16)
-        hidden_out_terms.append((s["activated"], rounded))
+        hidden_out_terms.append(token_sum(s["activated"], rounded))
         back_active = back_dot(rounded, h_out).astype(jnp.bfloat16)
         _, gelu_pull = jax.vjp(gelu, s["hidden"])
         back_hidden = gelu_pull(back_active.astype(jnp.float32))[0].astype(jnp.bfloat16)
-        hidden_in_terms.append((s["normed_three"], back_hidden))
+        hidden_in_terms.append(token_sum(s["normed_three"], back_hidden))
         back_threes.append(back_dot(back_hidden, h_in).astype(jnp.bfloat16))
         upstreams.append(upstream)
-    ffn_grads = (pooled(hidden_in_terms), pooled(hidden_out_terms))
+    ffn_grads = (summed(hidden_in_terms), summed(hidden_out_terms))
     ffn_kinds = ("plain", "grouped")
-    packed_ffn, back_threes[-1] = lax.optimization_barrier(
-        (pack_group(ffn_grads, ffn_kinds, members, half), back_threes[-1])
+    packed_ffn, back_threes[0] = lax.optimization_barrier(
+        (pack_group(ffn_grads, ffn_kinds, members, half), back_threes[0])
     )
     grad_ffn = reduce_group(packed_ffn, ffn_grads, ffn_kinds, half)
 
@@ -335,13 +330,13 @@
         upstream = upstreams[index] + back_mixed
         upstreams[index] = upstream
         rounded = upstream.astype(jnp.bfloat16)
-        time_out_terms.append((s["context_time"], rounded))
+        time_out_terms.append(token_sum(s["context_time"], rounded))
         back_context = back_dot(rounded, t_out).astype(jnp.bfloat16)
         back_placed = to_places(back_context)
         back_join = attend_back(s["join_time"], s["total_time"], back_placed, *temporal)
-        time_in_terms.append((s["placed"], back_join))
+        time_in_terms.append(token_sum(s["placed"], back_join))
         back_twos_placed.append(back_dot(back_join, t_in).astype(jnp.bfloat16))
-    time_grads = (pooled(time_in_terms), pooled(time_out_terms))
+    time_grads = (summed(time_in_terms), summed(time_out_terms))
     time_kinds = ("plain", "plain")
     packed_time, back_twos_placed[-1] = lax.optimization_barrier(
         (pack_group(time_grads, time_kinds, members, half), back_twos_placed[-1])
@@ -360,18 +355,18 @@
         gain_one_terms.append(gain_grad)
         upstream = upstreams[index] + back_mixed
         rounded = upstream.astype(jnp.bfloat16)
-        space_out_terms.append((s["context_space"], rounded))
+        space_out_terms.append(token_sum(s["context_space"], rounded))
         back_context = back_dot(rounded, s_out).astype(jnp.bfloat16)
         back_join = attend_back(s["join_space"], s["total_space"], back_context, *spatial)
-        space_in_terms.append((s["normed_one"], back_join))
+        space_in_terms.append(token_sum(s["normed_one"], back_join))
         back_one = back_dot(back_join, s_in).astype(jnp.bfloat16)
         back_mixed, gain_grad = norm_back(
             s["frames_in"], gain_rows[0], back_one.astype(jnp.float32)
         )
         gain_zero_terms.append(gain_grad)
         input_grads.append(upstream + back_mixed)
-    grad_space_in = pooled(space_in_terms)
-    grad_space_out = pooled(space_out_terms)
+    grad_space_in = summed(space_in_terms)
+    grad_space_out = summed(space_out_terms)
     gain_grad_zero = summed(gain_zero_terms)
     gain_grad_one = summed(gain_one_terms)
     gain_grad_two = summed(gain_two_terms)

time: 734 us -> 730 us (level)
  local copies, waits for them, and re-layouts: 146 us -> 114 us
  waiting for transfers between devices: 311 us -> 330 us
  matrix products: 154 us -> 165 us
    convert_element_type x12 -> x8, local copies, waits for them, and re-layouts: 56.3 us -> 32.5 us  [attend_back(): stacked.reshape(back_context.shape[:-1] + (3 * D,)).astype(jnp.bfloat16)]
    all_to_all x4, waiting for transfers between devices: 31.9 us -> 42.8 us  [to_frames(): lax.all_to_all(blocks, 'fsdp', split_axis=0, concat_axis=0, tiled=True)]
    convert_element_type x8 -> x4, local copies, waits for them, and re-layouts: 18.4 us -> 8.81 us  [attend_core(): context = context.reshape(normed.shape[:-1] + (D,)).astype(jnp.bfloat16)]
    dot_general x6 -> x12, matrix products: 24.2 us -> 33.4 us  [token_sum(): lax.dot_general(left_rows, right_rows, (((0,), (0,)), ((), ())), preferre...]
    unnamed x282 -> x294, local copies, waits for them, and re-layouts: 24.6 us -> 26.7 us
  transfers between devices with their start and end apart: 20 -> 20, of which waited for: 13 -> 13; matrix products, arithmetic and copies ran while one was open for 33% -> 28% of each run, Pallas kernels for 0% -> 0%
where the time goes in v4:
time: 730 us; the launch traced here: 724 us
  waiting for transfers between devices  330 us (45%)
  matrix products  165 us (23%)
  local copies, waits for them, and re-layouts  114 us (16%)
  other arithmetic  54.2 us (7%)
  starting transfers between devices  43.5 us (6%)
  between operations  16.6 us (2%)
    reduce_scatter x3, waiting for transfers between devices, reduce_group(): owned = lax.psum_scatter(packed, MEMBERS, scatter_dimension=0, tiled=True)  163 us
    all_gather x3, waiting for transfers between devices, gather_group(): gathered = lax.all_gather(block, MEMBERS, axis=0, tiled=True)  55.5 us
    dot_general x12, matrix products, flat_dot(): product = jnp.dot(flat, right, preferred_element_type=jnp.float32)  45.5 us
    all_to_all x4, waiting for transfers between devices, to_places(): lax.all_to_all(blocks, 'fsdp', split_axis=0, concat_axis=0, tiled=True)  44.6 us
    all_to_all x4, waiting for transfers between devices, to_frames(): lax.all_to_all(blocks, 'fsdp', split_axis=0, concat_axis=0, tiled=True)  42.8 us
    dot_general x12, matrix products, back_dot(): lax.dot_general(flat, right, (((1,), (1,)), ((), ())), preferred_element_...  40.7 us
    dot_general x12, matrix products, token_sum(): lax.dot_general(left_rows, right_rows, (((0,), (0,)), ((), ())), preferre...  33.4 us
    convert_element_type x8, local copies, waits for them, and re-layouts, attend_back(): stacked.reshape(back_context.shape[:-1] + (3 * D,)).astype(jnp.bfloat16)  32.5 us
  transfers between devices with their start and end apart: 20, of which 13 were waited for; matrix products, arithmetic and copies ran while one was open for 28% of the time, Pallas kernels for 0%

profile of v4, /device:TPU:0, one launch (start us, length us, event | category | flops | bytes accessed | tf_op | source)
XLA Modules:
  0.0 723.7 jit_solution(2841088269555736860)
XLA Ops:
  13.3 54.4 %all-gather.4.cloned.1.call-done = bf16[768,3200]{1,0:T(8,128)(2,1)} async-done(((bf16[48,3200]{1,0:T(8,128)(2,1)}), bf16[768,3200]{1,0:T(8,128)(2,1)}) %all-gather.4.cloned.1.call-update) | async-done | bytes 4915216 | tf_op jit(solution)/shard_map/all_gather | solution.py:204
  102.7 27.9 %all-to-all-done.2 = bf16[8,2,24,768]{3,2,1,0:T(8,128)(2,1)S(1)} async-done(((bf16[8,2,24,768]{3,2,1,0:T(8,128)(2,1)}), bf16[8,2,24,768]{3,2,1,0:T(8,128)(2,1)S(1)}, u32[]{:S(2)}, u32[]{:S(2)}) %all-to-all-start.2) | async-done | bytes 589856 | tf_op jit(solution)/shard_map/all_to_all | solution.py:141
  154.9 5.2 all-to-all-done
  169.5 6.5 reshape.586
  188.4 6.2 all-to-all-start.1
  198.1 28.6 %all-to-all-done.1 = bf16[8,2,24,768]{3,2,1,0:T(8,128)(2,1)} async-done(((bf16[8,2,24,768]{3,2,1,0:T(8,128)(2,1)}), bf16[8,2,24,768]{3,2,1,0:T(8,128)(2,1)}, u32[]{:S(2)}, u32[]{:S(2)}) %all-to-all-start.1) | async-done | bytes 589856 | tf_op jit(solution)/shard_map/all_to_all | solution.py:149
  247.4 5.4 add_convert_fusion.3
  256.3 6.7 add_convert_fusion.2
  268.0 5.4 fusion.126
  273.4 5.5 fusion.1
  283.7 5.2 fusion.51
  312.0 10.6 %all-to-all-done.4 = bf16[8,2,24,768]{3,2,1,0:T(8,128)(2,1)} async-done(((bf16[8,2,24,768]{3,2,1,0:T(8,128)(2,1)}), bf16[8,2,24,768]{3,2,1,0:T(8,128)(2,1)}, u32[]{:S(2)}, u32[]{:S(2)}) %all-to-all-start.4) | async-done | bytes 589856 | tf_op jit(solution)/shard_map/all_to_all | solution.py:141
  359.6 5.5 convert_element_type.476
  365.2 6.6 convert_element_type.458
  381.6 5.5 all-to-all-start.5
  387.2 6.6 convert_element_type.483
  399.8 6.7 convert_element_type.486
  416.2 6.0 all-to-all-start.7
  423.0 14.2 %all-to-all-done.7 = bf16[8,2,24,768]{3,2,1,0:T(8,128)(2,1)S(1)} async-done(((bf16[8,2,24,768]{3,2,1,0:T(8,128)(2,1)}), bf16[8,2,24,768]{3,2,1,0:T(8,128)(2,1)S(1)}, u32[]{:S(2)}, u32[]{:S(2)}) %all-to-all-start.7) | async-done | bytes 589856 | tf_op jit(solution)/shard_map/all_to_all | solution.py:149
  503.9 5.2 fusion.49
  514.4 5.6 collective-permute-done.2
  525.0 57.5 %reduce-scatter.4.cloned.1.call-done = bf16[48,3200]{1,0:T(8,128)(2,1)} async-done(((bf16[768,3200]{1,0:T(8,128)(2,1)}), bf16[48,3200]{1,0:T(8,128)(2,1)}) %reduce-scatter.4.cloned.1.call-update) | async-done | bytes 307216 | tf_op jit(solution)/shard_map/reduce_scatter | solution.py:232
  591.3 105.2 %reduce-scatter.8.cloned.1.call-done = bf16[48,6144]{1,0:T(8,128)(2,1)} async-done(((bf16[768,6144]{1,0:T(8,128)(2,1)}), bf16[48,6144]{1,0:T(8,128)(2,1)}) %reduce-scatter.8.cloned.1.call-update) | async-done | bytes 589840 | tf_op jit(solution)/shard_map/reduce_scatter | solution.py:232
  698.0 13.5 %collective-permute-done.4 = bf16[48,6144]{1,0:T(8,128)(2,1)S(1)} collective-permute-done((bf16[48,6144]{1,0:T(8,128)(2,1)}, bf16[48,6144]{1,0:T(8,128)(2,1)S(1)}, u32[]{:S(2)}, u32[]{:S(2)}) %collective-permute-start.4) | collective-permute-done | bytes 589856 | tf_op jit(solution)/shard_map/ppermute | solution.py:210
  (520 shorter events, 301.5 us)
Async XLA Ops:
  7.2 60.4 %all-gather.4.cloned.1.call-start = ((), (), s32[]{:S(2)}) async-start(), calls=%async_computation.11 | async-start | bytes 5222400 | tf_op jit(solution)/shard_map/all_gather | solution.py:204
  9.9 125.0 %all-gather.6.cloned.1.call-start = ((), (), s32[]{:S(2)}) async-start(), calls=%async_computation.12 | async-start | bytes 5013504 | tf_op jit(solution)/shard_map/all_gather | solution.py:204
  10.8 225.8 %all-gather.8.cloned.1.call-start = ((), (), s32[]{:S(2)}) async-start(), calls=%async_computation.13 | async-start | bytes 10027008 | tf_op jit(solution)/shard_map/all_gather | solution.py:204
  12.2 60.7 %copy-start.113 = (f32[2,192]{1,0:T(2,128)}, f32[2,192]{1,0:T(2,128)S(1)}, u32[]{:S(2)}) copy-start(f32[2,192]{1,0:T(2,128)S(1)} %get-tuple-element.143) | copy-start | bytes 4612
  12.2 63.3 %copy-start.115 = (f32[2,192]{1,0:T(2,128)}, f32[2,192]{1,0:T(2,128)S(1)}, u32[]{:S(2)}) copy-start(f32[2,192]{1,0:T(2,128)S(1)} %get-tuple-element.144) | copy-start | bytes 4612
  13.2 62.2 %copy-start.117 = (f32[2,192]{1,0:T(2,128)}, f32[2,192]{1,0:T(2,128)S(1)}, u32[]{:S(2)}) copy-start(f32[2,192]{1,0:T(2,128)S(1)} %fusion.135) | copy-start | bytes 4612
  98.3 32.3 %all-to-all-start.2 = ((bf16[8,2,24,768]{3,2,1,0:T(8,128)(2,1)}), bf16[8,2,24,768]{3,2,1,0:T(8,128)(2,1)S(1)}, u32[]{:S(2)}, u32[]{:S(2)}) async-start(bf16[8,2,24,768]{3,2,1,0:T(8,128)(2,1)} %bitcast.436), calls=%async_computation.2 | async-start | bytes 1179648 | tf_op jit(solution)/shard_map/all_to_all | solution.py:141
  130.6 29.6 %all-to-all-start = ((bf16[8,2,24,768]{3,2,1,0:T(8,128)(2,1)}), bf16[8,2,24,768]{3,2,1,0:T(8,128)(2,1)S(1)}, u32[]{:S(2)}, u32[]{:S(2)}) async-start(bf16[8,2,24,768]{3,2,1,0:T(8,128)(2,1)} %bitcast.437), calls=%async_computation | async-start | bytes 1179648 | tf_op jit(solution)/shard_map/all_to_all | solution.py:141
  160.1 28.2 %all-to-all-start.3 = ((bf16[8,2,24,768]{3,2,1,0:T(8,128)(2,1)}), bf16[8,2,24,768]{3,2,1,0:T(8,128)(2,1)}, u32[]{:S(2)}, u32[]{:S(2)}) async-start(bf16[8,2,24,768]{3,2,1,0:T(8,128)(2,1)} %convert_element_type.433), calls=%async_computation.3 | async-start | bytes 1179648 | tf_op jit(solution)/shard_map/all_to_all | solution.py:149
  188.4 38.3 %all-to-all-start.1 = ((bf16[8,2,24,768]{3,2,1,0:T(8,128)(2,1)}), bf16[8,2,24,768]{3,2,1,0:T(8,128)(2,1)}, u32[]{:S(2)}, u32[]{:S(2)}) async-start(bf16[8,2,24,768]{3,2,1,0:T(8,128)(2,1)} %convert_element_type.417), calls=%async_computation.1 | async-start | bytes 1179648 | tf_op jit(solution)/shard_map/all_to_all | solution.py:149
  301.4 21.2 %all-to-all-start.4 = ((bf16[8,2,24,768]{3,2,1,0:T(8,128)(2,1)}), bf16[8,2,24,768]{3,2,1,0:T(8,128)(2,1)}, u32[]{:S(2)}, u32[]{:S(2)}) async-start(bf16[8,2,24,768]{3,2,1,0:T(8,128)(2,1)} %bitcast.490), calls=%async_computation.4 | async-start | bytes 1179648 | tf_op jit(solution)/shard_map/all_to_all | solution.py:141
  322.6 19.7 %all-to-all-start.6 = ((bf16[8,2,24,768]{3,2,1,0:T(8,128)(2,1)}), bf16[8,2,24,768]{3,2,1,0:T(8,128)(2,1)S(1)}, u32[]{:S(2)}, u32[]{:S(2)}) async-start(bf16[8,2,24,768]{3,2,1,0:T(8,128)(2,1)} %bitcast.489), calls=%async_computation.6 | async-start | bytes 1179648 | tf_op jit(solution)/shard_map/all_to_all | solution.py:141
  381.6 34.5 %all-to-all-start.5 = ((bf16[8,2,24,768]{3,2,1,0:T(8,128)(2,1)}), bf16[8,2,24,768]{3,2,1,0:T(8,128)(2,1)S(1)}, u32[]{:S(2)}, u32[]{:S(2)}) async-start(bf16[8,2,24,768]{3,2,1,0:T(8,128)(2,1)} %bitcast.70), calls=%async_computation.5 | async-start | bytes 1179648 | tf_op jit(solution)/shard_map/all_to_all | solution.py:149
  416.2 21.0 %all-to-all-start.7 = ((bf16[8,2,24,768]{3,2,1,0:T(8,128)(2,1)}), bf16[8,2,24,768]{3,2,1,0:T(8,128)(2,1)S(1)}, u32[]{:S(2)}, u32[]{:S(2)}) async-start(bf16[8,2,24,768]{3,2,1,0:T(8,128)(2,1)} %bitcast.97), calls=%async_computation.7 | async-start | bytes 1179648 | tf_op jit(solution)/shard_map/all_to_all | solution.py:149
  422.2 90.6 %reduce-scatter.6.cloned.1.call-start = ((), (), s32[]{:S(2)}) async-start(), calls=%async_computation.15 | async-start | bytes 5013504 | tf_op jit(solution)/shard_map/reduce_scatter | solution.py:232
  422.7 159.7 %reduce-scatter.4.cloned.1.call-start = ((), (), s32[]{:S(2)}) async-start(), calls=%async_computation.14 | async-start | bytes 5222400 | tf_op jit(solution)/shard_map/reduce_scatter | solution.py:232
  503.3 193.1 %reduce-scatter.8.cloned.1.call-start = ((), (), s32[]{:S(2)}) async-start(), calls=%async_computation.16 | async-start | bytes 10027008 | tf_op jit(solution)/shard_map/reduce_scatter | solution.py:232
  512.8 7.2 collective-permute-start.2
  521.1 62.9 %collective-permute-start.3 = (bf16[48,3072]{1,0:T(8,128)(2,1)S(1)}, bf16[48,3072]{1,0:T(8,128)(2,1)}, u32[]{:S(2)}, u32[]{:S(2)}) collective-permute-start(bf16[48,3072]{1,0:T(8,128)(2,1)S(1)} %add.268), channel_id=1, source_target_pairs={{0,8},{8,0},{1,9},{9,1},{2,10},{10,2},{3,11},{11,3},{4,12},{12,4},... | collective-permute-start | bytes 884744 | tf_op jit(solution)/shard_map/ppermute | solution.py:216
  523.4 60.5 %copy-start.90 = (bf16[48,3072]{1,0:T(8,128)(2,1)S(1)}, bf16[48,3072]{1,0:T(8,128)(2,1)}, u32[]{:S(2)}) copy-start(bf16[48,3072]{1,0:T(8,128)(2,1)} %copy-done.89) | copy-start | bytes 884740
  582.5 7.7 %collective-permute-start = (bf16[48,3200]{1,0:T(8,128)(2,1)}, bf16[48,3200]{1,0:T(8,128)(2,1)S(1)}, u32[]{:S(2)}, u32[]{:S(2)}) collective-permute-start(bf16[48,3200]{1,0:T(8,128)(2,1)} %reduce-scatter.4.cloned.1.call-done), channel_id=1, source_target_pairs={{0,16},{16,0},{1,17},{17,1},{2,18},{18,2},{3,19},{19,3},{4,20},{20... | collective-permute-start | bytes 921608 | tf_op jit(solution)/shard_map/ppermute | solution.py:210
  590.2 107.7 %collective-permute-start.1 = (bf16[48,3200]{1,0:T(8,128)(2,1)S(1)}, bf16[48,3200]{1,0:T(8,128)(2,1)S(1)}, u32[]{:S(2)}, u32[]{:S(2)}) collective-permute-start(bf16[48,3200]{1,0:T(8,128)(2,1)S(1)} %add.267), channel_id=1, source_target_pairs={{0,8},{8,0},{1,9},{9,1},{2,10},{10,2},{3,11},{11,3},{4,12},{12,4},... | collective-permute-start | bytes 921608 | tf_op jit(solution)/shard_map/ppermute | solution.py:216
  696.5 15.0 %collective-permute-start.4 = (bf16[48,6144]{1,0:T(8,128)(2,1)}, bf16[48,6144]{1,0:T(8,128)(2,1)S(1)}, u32[]{:S(2)}, u32[]{:S(2)}) collective-permute-start(bf16[48,6144]{1,0:T(8,128)(2,1)} %reduce-scatter.8.cloned.1.call-done), channel_id=1, source_target_pairs={{0,16},{16,0},{1,17},{17,1},{2,18},{18,2},{3,19},{19,3},{4,20},{20... | collective-permute-start | bytes 1769480 | tf_op jit(solution)/shard_map/ppermute | solution.py:210
  711.6 2.5 collective-permute-start.5
  (141 other events, 616.2 us)
Sparse Core Ops, SparseCore 0:
  10.8 56.8 all-gather.3
  70.5 62.2 all-gather.5
  135.7 100.9 all-gather.7
  426.5 76.9 reduce-scatter.5
  507.3 75.0 reduce-scatter.3
  586.4 110.0 reduce-scatter.7

commit v5 on v4

--- a/solution.py
+++ b/solution.py
@@ -246,8 +246,12 @@
     s_in, s_out, gains = gather_group(
         (space_in, space_out, norm_gains), ("plain", "plain", "gains"), core, half
     )
-    t_in, t_out = gather_group((time_in, time_out), ("plain", "plain"), core, half)
-    h_in, h_out = gather_group((hidden_in, hidden_out), ("plain", "grouped"), core, half)
+    t_in, t_out, h_in, h_out = gather_group(
+        (time_in, time_out, hidden_in, hidden_out),
+        ("plain", "plain", "plain", "grouped"),
+        core,
+        half,
+    )
     gain_rows = gains.astype(jnp.float32)
 
     micro = inputs.shape[0]
@@ -313,8 +317,8 @@
         upstreams.append(upstream)
     ffn_grads = (summed(hidden_in_terms), summed(hidden_out_terms))
     ffn_kinds = ("plain", "grouped")
-    packed_ffn, back_threes[0] = lax.optimization_barrier(
-        (pack_group(ffn_grads, ffn_kinds, members, half), back_threes[0])
+    packed_ffn, back_threes[-1] = lax.optimization_barrier(
+        (pack_group(ffn_grads, ffn_kinds, members, half), back_threes[-1])
     )
     grad_ffn = reduce_group(packed_ffn, ffn_grads, ffn_kinds, half)
 

time: 730 us -> 768 us (1.052)
  waiting for transfers between devices: 330 us -> 359 us
    all_gather x3 -> x2, waiting for transfers between devices: 55.5 us -> 123 us  [gather_group(): gathered = lax.all_gather(block, MEMBERS, axis=0, tiled=True)]
    all_to_all x4, waiting for transfers between devices: 42.8 us -> 18.9 us  [to_frames(): lax.all_to_all(blocks, 'fsdp', split_axis=0, concat_axis=0, tiled=True)]
    all_to_all x4, waiting for transfers between devices: 44.6 us -> 29.2 us  [to_places(): lax.all_to_all(blocks, 'fsdp', split_axis=0, concat_axis=0, tiled=True)]
    unnamed x294 -> x300, local copies, waits for them, and re-layouts: 26.7 us -> 27.1 us
  transfers between devices with their start and end apart: 20 -> 19, of which waited for: 13 -> 12; matrix products, arithmetic and copies ran while one was open for 28% -> 29% of each run, Pallas kernels for 0% -> 0%
where the time goes in v5:
time: 768 us; the launch traced here: 762 us
  waiting for transfers between devices  359 us (47%)
  matrix products  170 us (22%)
  local copies, waits for them, and re-layouts  117 us (15%)
  other arithmetic  56.8 us (7%)
  starting transfers between devices  43 us (6%)
  between operations  16.3 us (2%)
    reduce_scatter x3, waiting for transfers between devices, reduce_group(): owned = lax.psum_scatter(packed, MEMBERS, scatter_dimension=0, tiled=True)  163 us
    all_gather x2, waiting for transfers between devices, gather_group(): gathered = lax.all_gather(block, MEMBERS, axis=0, tiled=True)  123 us
    dot_general x12, matrix products, flat_dot(): product = jnp.dot(flat, right, preferred_element_type=jnp.float32)  48.5 us
    dot_general x12, matrix products, back_dot(): lax.dot_general(flat, right, (((1,), (1,)), ((), ())), preferred_element_...  41.7 us
    dot_general x12, matrix products, token_sum(): lax.dot_general(left_rows, right_rows, (((0,), (0,)), ((), ())), preferre...  34.6 us
    convert_element_type x8, local copies, waits for them, and re-layouts, attend_back(): stacked.reshape(back_context.shape[:-1] + (3 * D,)).astype(jnp.bfloat16)  32.7 us
    all_to_all x4, waiting for transfers between devices, to_places(): lax.all_to_all(blocks, 'fsdp', split_axis=0, concat_axis=0, tiled=True)  29.2 us
    unnamed x300, local copies, waits for them, and re-layouts  27.1 us
  transfers between devices with their start and end apart: 19, of which 12 were waited for; matrix products, arithmetic and copies ran while one was open for 29% of the time, Pallas kernels for 0%

profile of v5, /device:TPU:0, one launch (start us, length us, event | category | flops | bytes accessed | tf_op | source)
XLA Modules:
  0.0 762.5 jit_solution(3420503999578518059)
XLA Ops:
  14.4 53.3 %all-gather.3.cloned.1.call-done = bf16[768,3200]{1,0:T(8,128)(2,1)} async-done(((bf16[48,3200]{1,0:T(8,128)(2,1)}), bf16[768,3200]{1,0:T(8,128)(2,1)}) %all-gather.3.cloned.1.call-update) | async-done | bytes 4915216 | tf_op jit(solution)/shard_map/all_gather | solution.py:204
  75.5 5.2 convolution_convert_fusion.5
  104.0 18.8 %all-to-all-done.2 = bf16[8,2,24,768]{3,2,1,0:T(8,128)(2,1)S(1)} async-done(((bf16[8,2,24,768]{3,2,1,0:T(8,128)(2,1)}), bf16[8,2,24,768]{3,2,1,0:T(8,128)(2,1)S(1)}, u32[]{:S(2)}, u32[]{:S(2)}) %all-to-all-start.2) | async-done | bytes 589856 | tf_op jit(solution)/shard_map/all_to_all | solution.py:141
  126.5 70.0 %all-gather.5.cloned.1.call-done = bf16[768,9216]{1,0:T(8,128)(2,1)} async-done(((bf16[48,9216]{1,0:T(8,128)(2,1)}), bf16[768,9216]{1,0:T(8,128)(2,1)}) %all-gather.5.cloned.1.call-update) | async-done | bytes 14155792 | tf_op jit(solution)/shard_map/all_gather | solution.py:204
  201.3 6.4 reshape.591
  233.4 6.4 reshape.586
  261.7 6.2 all-to-all-start.1
  267.9 6.5 fusion.11
  288.3 5.8 add_convert_fusion.3
  294.2 5.3 fusion.126
  305.3 7.9 %add_convert_fusion.2 = (bf16[2,192,3072]{2,1,0:T(8,128)(2,1)}, bf16[2,192,3072]{2,1,0:T(8,128)(2,1)}) fusion(f32[2,192,3072]{2,1,0:T(8,128)} %bitcast.504, bf16[768,9216]{1,0:T(8,128)(2,1)S(1)} %bitcast.454, f32[2,192,768]{2,1,0:T(8,128)S(1)} %copy-done.7, f32[2,192]{1,0:T(2,128)S(1)} %fusion.140, f32[2,192]{1,0:T(2,128)S(1)} %broadcast_multiply_fusion, ...), kind=kOutput, calls=%fused_computation.28 | convolution fusion | flops 1830813696 | bytes 15343616 | tf_op jit(solution)/shard_map/dot_general | solution.py:32
  319.4 5.5 fusion.1
  351.0 9.6 %all-to-all-done.4 = bf16[8,2,24,768]{3,2,1,0:T(8,128)(2,1)} async-done(((bf16[8,2,24,768]{3,2,1,0:T(8,128)(2,1)}), bf16[8,2,24,768]{3,2,1,0:T(8,128)(2,1)}, u32[]{:S(2)}, u32[]{:S(2)}) %all-to-all-start.4) | async-done | bytes 589856 | tf_op jit(solution)/shard_map/all_to_all | solution.py:141
  398.1 5.5 convert_element_type.476
  403.7 6.6 convert_element_type.451
  420.3 5.6 all-to-all-start.5
  425.9 6.6 convert_element_type.483
  438.6 6.7 convert_element_type.486
  455.0 6.0 all-to-all-start.7
  462.0 14.0 %all-to-all-done.7 = bf16[8,2,24,768]{3,2,1,0:T(8,128)(2,1)S(1)} async-done(((bf16[8,2,24,768]{3,2,1,0:T(8,128)(2,1)}), bf16[8,2,24,768]{3,2,1,0:T(8,128)(2,1)S(1)}, u32[]{:S(2)}, u32[]{:S(2)}) %all-to-all-start.7) | async-done | bytes 589856 | tf_op jit(solution)/shard_map/all_to_all | solution.py:149
  553.5 5.4 collective-permute-done.2
  563.9 57.8 %reduce-scatter.4.cloned.1.call-done = bf16[48,3200]{1,0:T(8,128)(2,1)} async-done(((bf16[768,3200]{1,0:T(8,128)(2,1)}), bf16[48,3200]{1,0:T(8,128)(2,1)}) %reduce-scatter.4.cloned.1.call-update) | async-done | bytes 307216 | tf_op jit(solution)/shard_map/reduce_scatter | solution.py:232
  630.5 105.2 %reduce-scatter.8.cloned.1.call-done = bf16[48,6144]{1,0:T(8,128)(2,1)} async-done(((bf16[768,6144]{1,0:T(8,128)(2,1)}), bf16[48,6144]{1,0:T(8,128)(2,1)}) %reduce-scatter.8.cloned.1.call-update) | async-done | bytes 589840 | tf_op jit(solution)/shard_map/reduce_scatter | solution.py:232
  737.2 13.4 %collective-permute-done.4 = bf16[48,6144]{1,0:T(8,128)(2,1)S(1)} collective-permute-done((bf16[48,6144]{1,0:T(8,128)(2,1)}, bf16[48,6144]{1,0:T(8,128)(2,1)S(1)}, u32[]{:S(2)}, u32[]{:S(2)}) %collective-permute-start.4) | collective-permute-done | bytes 589856 | tf_op jit(solution)/shard_map/ppermute | solution.py:210
  (521 shorter events, 306.4 us)
Async XLA Ops:
  7.2 60.4 %all-gather.3.cloned.1.call-start = ((), (), s32[]{:S(2)}) async-start(), calls=%async_computation.11 | async-start | bytes 5222400 | tf_op jit(solution)/shard_map/all_gather | solution.py:204
  9.9 186.6 %all-gather.5.cloned.1.call-start = ((), (), s32[]{:S(2)}) async-start(), calls=%async_computation.12 | async-start | bytes 15040512 | tf_op jit(solution)/shard_map/all_gather | solution.py:204
  13.3 59.6 %copy-start.112 = (f32[2,192]{1,0:T(2,128)}, f32[2,192]{1,0:T(2,128)S(1)}, u32[]{:S(2)}) copy-start(f32[2,192]{1,0:T(2,128)S(1)} %get-tuple-element.144) | copy-start | bytes 4612
  13.3 62.2 %copy-start.114 = (f32[2,192]{1,0:T(2,128)}, f32[2,192]{1,0:T(2,128)S(1)}, u32[]{:S(2)}) copy-start(f32[2,192]{1,0:T(2,128)S(1)} %get-tuple-element.145) | copy-start | bytes 4612
  14.4 61.1 %copy-start.116 = (f32[2,192]{1,0:T(2,128)}, f32[2,192]{1,0:T(2,128)S(1)}, u32[]{:S(2)}) copy-start(f32[2,192]{1,0:T(2,128)S(1)} %fusion.135) | copy-start | bytes 4612
  98.5 24.3 %all-to-all-start.2 = ((bf16[8,2,24,768]{3,2,1,0:T(8,128)(2,1)}), bf16[8,2,24,768]{3,2,1,0:T(8,128)(2,1)S(1)}, u32[]{:S(2)}, u32[]{:S(2)}) async-start(bf16[8,2,24,768]{3,2,1,0:T(8,128)(2,1)} %bitcast.436), calls=%async_computation.2 | async-start | bytes 1179648 | tf_op jit(solution)/shard_map/all_to_all | solution.py:141
  122.8 78.5 %copy-start.73 = (bf16[8,2,24,768]{3,2,1,0:T(8,128)(2,1)}, bf16[8,2,24,768]{3,2,1,0:T(8,128)(2,1)S(1)}, u32[]{:S(2)}) copy-start(bf16[8,2,24,768]{3,2,1,0:T(8,128)(2,1)S(1)} %all-to-all-done.2) | copy-start | bytes 1769476
  122.8 101.3 %all-to-all-start = ((bf16[8,2,24,768]{3,2,1,0:T(8,128)(2,1)}), bf16[8,2,24,768]{3,2,1,0:T(8,128)(2,1)S(1)}, u32[]{:S(2)}, u32[]{:S(2)}) async-start(bf16[8,2,24,768]{3,2,1,0:T(8,128)(2,1)} %bitcast.437), calls=%async_computation | async-start | bytes 1179648 | tf_op jit(solution)/shard_map/all_to_all | solution.py:141
  224.1 37.6 %all-to-all-start.3 = ((bf16[8,2,24,768]{3,2,1,0:T(8,128)(2,1)}), bf16[8,2,24,768]{3,2,1,0:T(8,128)(2,1)}, u32[]{:S(2)}, u32[]{:S(2)}) async-start(bf16[8,2,24,768]{3,2,1,0:T(8,128)(2,1)} %convert_element_type.433), calls=%async_computation.3 | async-start | bytes 1179648 | tf_op jit(solution)/shard_map/all_to_all | solution.py:149
  261.7 22.3 %all-to-all-start.1 = ((bf16[8,2,24,768]{3,2,1,0:T(8,128)(2,1)}), bf16[8,2,24,768]{3,2,1,0:T(8,128)(2,1)}, u32[]{:S(2)}, u32[]{:S(2)}) async-start(bf16[8,2,24,768]{3,2,1,0:T(8,128)(2,1)} %convert_element_type.417), calls=%async_computation.1 | async-start | bytes 1179648 | tf_op jit(solution)/shard_map/all_to_all | solution.py:149
  340.8 19.8 %all-to-all-start.4 = ((bf16[8,2,24,768]{3,2,1,0:T(8,128)(2,1)}), bf16[8,2,24,768]{3,2,1,0:T(8,128)(2,1)}, u32[]{:S(2)}, u32[]{:S(2)}) async-start(bf16[8,2,24,768]{3,2,1,0:T(8,128)(2,1)} %bitcast.492), calls=%async_computation.4 | async-start | bytes 1179648 | tf_op jit(solution)/shard_map/all_to_all | solution.py:141
  360.6 20.1 %all-to-all-start.6 = ((bf16[8,2,24,768]{3,2,1,0:T(8,128)(2,1)}), bf16[8,2,24,768]{3,2,1,0:T(8,128)(2,1)S(1)}, u32[]{:S(2)}, u32[]{:S(2)}) async-start(bf16[8,2,24,768]{3,2,1,0:T(8,128)(2,1)} %bitcast.491), calls=%async_computation.6 | async-start | bytes 1179648 | tf_op jit(solution)/shard_map/all_to_all | solution.py:141
  420.3 34.8 %all-to-all-start.5 = ((bf16[8,2,24,768]{3,2,1,0:T(8,128)(2,1)}), bf16[8,2,24,768]{3,2,1,0:T(8,128)(2,1)S(1)}, u32[]{:S(2)}, u32[]{:S(2)}) async-start(bf16[8,2,24,768]{3,2,1,0:T(8,128)(2,1)} %bitcast.60), calls=%async_computation.5 | async-start | bytes 1179648 | tf_op jit(solution)/shard_map/all_to_all | solution.py:149
  455.0 21.0 %all-to-all-start.7 = ((bf16[8,2,24,768]{3,2,1,0:T(8,128)(2,1)}), bf16[8,2,24,768]{3,2,1,0:T(8,128)(2,1)S(1)}, u32[]{:S(2)}, u32[]{:S(2)}) async-start(bf16[8,2,24,768]{3,2,1,0:T(8,128)(2,1)} %bitcast.97), calls=%async_computation.7 | async-start | bytes 1179648 | tf_op jit(solution)/shard_map/all_to_all | solution.py:149
  461.0 90.8 %reduce-scatter.6.cloned.1.call-start = ((), (), s32[]{:S(2)}) async-start(), calls=%async_computation.14 | async-start | bytes 5013504 | tf_op jit(solution)/shard_map/reduce_scatter | solution.py:232
  461.8 159.9 %reduce-scatter.4.cloned.1.call-start = ((), (), s32[]{:S(2)}) async-start(), calls=%async_computation.13 | async-start | bytes 5222400 | tf_op jit(solution)/shard_map/reduce_scatter | solution.py:232
  542.3 193.3 %reduce-scatter.8.cloned.1.call-start = ((), (), s32[]{:S(2)}) async-start(), calls=%async_computation.15 | async-start | bytes 10027008 | tf_op jit(solution)/shard_map/reduce_scatter | solution.py:232
  551.8 7.1 collective-permute-start.2
  560.0 63.2 %collective-permute-start.3 = (bf16[48,3072]{1,0:T(8,128)(2,1)S(1)}, bf16[48,3072]{1,0:T(8,128)(2,1)}, u32[]{:S(2)}, u32[]{:S(2)}) collective-permute-start(bf16[48,3072]{1,0:T(8,128)(2,1)S(1)} %add.268), channel_id=1, source_target_pairs={{0,8},{8,0},{1,9},{9,1},{2,10},{10,2},{3,11},{11,3},{4,12},{12,4},... | collective-permute-start | bytes 884744 | tf_op jit(solution)/shard_map/ppermute | solution.py:216
  562.3 60.8 %copy-start.91 = (bf16[48,3072]{1,0:T(8,128)(2,1)S(1)}, bf16[48,3072]{1,0:T(8,128)(2,1)}, u32[]{:S(2)}) copy-start(bf16[48,3072]{1,0:T(8,128)(2,1)} %copy-done.90) | copy-start | bytes 884740
  621.7 7.7 %collective-permute-start = (bf16[48,3200]{1,0:T(8,128)(2,1)}, bf16[48,3200]{1,0:T(8,128)(2,1)S(1)}, u32[]{:S(2)}, u32[]{:S(2)}) collective-permute-start(bf16[48,3200]{1,0:T(8,128)(2,1)} %reduce-scatter.4.cloned.1.call-done), channel_id=1, source_target_pairs={{0,16},{16,0},{1,17},{17,1},{2,18},{18,2},{3,19},{19,3},{4,20},{20... | collective-permute-start | bytes 921608 | tf_op jit(solution)/shard_map/ppermute | solution.py:210
  629.4 107.7 %collective-permute-start.1 = (bf16[48,3200]{1,0:T(8,128)(2,1)S(1)}, bf16[48,3200]{1,0:T(8,128)(2,1)S(1)}, u32[]{:S(2)}, u32[]{:S(2)}) collective-permute-start(bf16[48,3200]{1,0:T(8,128)(2,1)S(1)} %add.267), channel_id=1, source_target_pairs={{0,8},{8,0},{1,9},{9,1},{2,10},{10,2},{3,11},{11,3},{4,12},{12,4},... | collective-permute-start | bytes 921608 | tf_op jit(solution)/shard_map/ppermute | solution.py:216
  735.7 15.0 %collective-permute-start.4 = (bf16[48,6144]{1,0:T(8,128)(2,1)}, bf16[48,6144]{1,0:T(8,128)(2,1)S(1)}, u32[]{:S(2)}, u32[]{:S(2)}) collective-permute-start(bf16[48,6144]{1,0:T(8,128)(2,1)} %reduce-scatter.8.cloned.1.call-done), channel_id=1, source_target_pairs={{0,16},{16,0},{1,17},{17,1},{2,18},{18,2},{3,19},{19,3},{4,20},{20... | collective-permute-start | bytes 1769480 | tf_op jit(solution)/shard_map/ppermute | solution.py:210
  750.8 2.5 collective-permute-start.5
  (142 other events, 678.6 us)
Sparse Core Ops, SparseCore 0:
  10.8 56.8 all-gather.2
  70.5 126.0 all-gather.4
  465.7 76.9 reduce-scatter.5
  546.6 75.0 reduce-scatter.3
  625.6 109.9 reduce-scatter.7

commit v6 on v4

--- a/solution.py
+++ b/solution.py
@@ -255,7 +255,7 @@
     temporal = ("lg", "mg", "ghlm")
 
     saved = []
-    results = []
+    mixed_twos = []
     for index in range(micro):
         frames_in = inputs[index, 0].astype(jnp.float32)
         normed_one = layer_norm(frames_in, gain_rows[0]).astype(jnp.bfloat16)
@@ -266,10 +266,6 @@
         join_time, total_time, context_placed = attend_core(placed, t_in, *temporal)
         context_time = to_frames(context_placed)
         mixed_two = mixed_one + flat_dot(context_time, t_out)
-        normed_three = layer_norm(mixed_two, gain_rows[2]).astype(jnp.bfloat16)
-        hidden = flat_dot(normed_three, h_in)
-        activated = gelu(hidden).astype(jnp.bfloat16)
-        results.append(mixed_two + flat_dot(activated, h_out))
         saved.append(
             dict(
                 frames_in=frames_in,
@@ -282,12 +278,15 @@
                 join_time=join_time,
                 total_time=total_time,
                 context_time=context_time,
-                mixed_two=mixed_two,
-                normed_three=normed_three,
-                hidden=hidden,
-                activated=activated,
             )
         )
+        mixed_twos.append(mixed_two)
+
+    mixed_two = jnp.stack(mixed_twos)
+    normed_three = layer_norm(mixed_two, gain_rows[2]).astype(jnp.bfloat16)
+    hidden = flat_dot(normed_three, h_in)
+    activated = gelu(hidden).astype(jnp.bfloat16)
+    result = mixed_two + flat_dot(activated, h_out)
 
     def summed(terms):
         total = terms[0]
@@ -295,28 +294,23 @@
             total = total + term
         return total
 
-    upstreams = []
-    back_threes = []
     gain_two_terms = []
-    hidden_out_terms = []
-    hidden_in_terms = []
-    for index in range(micro):
-        s = saved[index]
-        upstream = cotangent[index, 0].astype(jnp.float32)
-        rounded = upstream.astype(jnp.bfloat16)
-        hidden_out_terms.append(token_sum(s["activated"], rounded))
-        back_active = back_dot(rounded, h_out).astype(jnp.bfloat16)
-        _, gelu_pull = jax.vjp(gelu, s["hidden"])
-        back_hidden = gelu_pull(back_active.astype(jnp.float32))[0].astype(jnp.bfloat16)
-        hidden_in_terms.append(token_sum(s["normed_three"], back_hidden))
-        back_threes.append(back_dot(back_hidden, h_in).astype(jnp.bfloat16))
-        upstreams.append(upstream)
-    ffn_grads = (summed(hidden_in_terms), summed(hidden_out_terms))
+    upstream_all = cotangent[:, 0].astype(jnp.float32)
+    rounded = upstream_all.astype(jnp.bfloat16)
+    grad_hidden_out = token_sum(activated, rounded)
+    back_active = back_dot(rounded, h_out).astype(jnp.bfloat16)
+    _, gelu_pull = jax.vjp(gelu, hidden)
+    back_hidden = gelu_pull(back_active.astype(jnp.float32))[0].astype(jnp.bfloat16)
+    grad_hidden_in = token_sum(normed_three, back_hidden)
+    back_three_all = back_dot(back_hidden, h_in).astype(jnp.bfloat16)
+    ffn_grads = (grad_hidden_in, grad_hidden_out)
     ffn_kinds = ("plain", "grouped")
-    packed_ffn, back_threes[0] = lax.optimization_barrier(
-        (pack_group(ffn_grads, ffn_kinds, members, half), back_threes[0])
+    packed_ffn, back_three_all = lax.optimization_barrier(
+        (pack_group(ffn_grads, ffn_kinds, members, half), back_three_all)
     )
     grad_ffn = reduce_group(packed_ffn, ffn_grads, ffn_kinds, half)
+    back_threes = [back_three_all[index] for index in range(micro)]
+    upstreams = [upstream_all[index] for index in range(micro)]
 
     back_twos_placed = []
     time_out_terms = []
@@ -324,7 +318,7 @@
     for index in range(micro):
         s = saved[index]
         back_mixed, gain_grad = norm_back(
-            s["mixed_two"], gain_rows[2], back_threes[index].astype(jnp.float32)
+            mixed_twos[index], gain_rows[2], back_threes[index].astype(jnp.float32)
         )
         gain_two_terms.append(gain_grad)
         upstream = upstreams[index] + back_mixed
@@ -370,7 +364,6 @@
     gain_grad_zero = summed(gain_zero_terms)
     gain_grad_one = summed(gain_one_terms)
     gain_grad_two = summed(gain_two_terms)
-    result = jnp.stack(results)
     input_grad = jnp.stack(input_grads)
 
     gain_grads = jnp.stack((gain_grad_zero, gain_grad_one, gain_grad_two))

time: 730 us -> 717 us (0.982)
  matrix products: 165 us -> 150 us
    dot_general x12 -> x10, matrix products: 33.4 us -> 28 us  [token_sum(): lax.dot_general(left_rows, right_rows, (((0,), (0,)), ((), ())), preferre...]
    dot_general x12 -> x10, matrix products: 40.7 us -> 35.6 us  [back_dot(): lax.dot_general(flat, right, (((1,), (1,)), ((), ())), preferred_element_...]
    unnamed x294 -> x250, local copies, waits for them, and re-layouts: 26.7 us -> 24.1 us
    dot_general x12 -> x10, matrix products: 45.5 us -> 45.8 us  [flat_dot(): product = jnp.dot(flat, right, preferred_element_type=jnp.float32)]
  transfers between devices with their start and end apart: 20 -> 20, of which waited for: 13 -> 12; matrix products, arithmetic and copies ran while one was open for 28% -> 31% of each run, Pallas kernels for 0% -> 0%
where the time goes in v6:
time: 717 us; the launch traced here: 712 us
  waiting for transfers between devices  335 us (47%)
  matrix products  150 us (21%)
  local copies, waits for them, and re-layouts  112 us (16%)
  other arithmetic  53.7 us (7%)
  starting transfers between devices  44.1 us (6%)
  between operations  16.4 us (2%)
    reduce_scatter x3, waiting for transfers between devices, reduce_group(): owned = lax.psum_scatter(packed, MEMBERS, scatter_dimension=0, tiled=True)  164 us
    all_gather x3, waiting for transfers between devices, gather_group(): gathered = lax.all_gather(block, MEMBERS, axis=0, tiled=True)  58.6 us
    dot_general x10, matrix products, flat_dot(): product = jnp.dot(flat, right, preferred_element_type=jnp.float32)  45.8 us
    all_to_all x4, waiting for transfers between devices, to_places(): lax.all_to_all(blocks, 'fsdp', split_axis=0, concat_axis=0, tiled=True)  43.1 us
    all_to_all x4, waiting for transfers between devices, to_frames(): lax.all_to_all(blocks, 'fsdp', split_axis=0, concat_axis=0, tiled=True)  42.9 us
    dot_general x10, matrix products, back_dot(): lax.dot_general(flat, right, (((1,), (1,)), ((), ())), preferred_element_...  35.6 us
    convert_element_type x8, local copies, waits for them, and re-layouts, attend_back(): stacked.reshape(back_context.shape[:-1] + (3 * D,)).astype(jnp.bfloat16)  35.1 us
    dot_general x10, matrix products, token_sum(): lax.dot_general(left_rows, right_rows, (((0,), (0,)), ((), ())), preferre...  28 us
  transfers between devices with their start and end apart: 20, of which 12 were waited for; matrix products, arithmetic and copies ran while one was open for 31% of the time, Pallas kernels for 0%

profile of v6, /device:TPU:0, one launch (start us, length us, event | category | flops | bytes accessed | tf_op | source)
XLA Modules:
  0.0 711.6 jit_solution(17139472385724659410)
XLA Ops:
  12.7 54.9 %all-gather.4.cloned.1.call-done = bf16[768,3200]{1,0:T(8,128)(2,1)} async-done(((bf16[48,3200]{1,0:T(8,128)(2,1)}), bf16[768,3200]{1,0:T(8,128)(2,1)}) %all-gather.4.cloned.1.call-update) | async-done | bytes 4915216 | tf_op jit(solution)/shard_map/all_gather | solution.py:204
  103.0 27.5 %all-to-all-done.2 = bf16[8,2,24,768]{3,2,1,0:T(8,128)(2,1)S(1)} async-done(((bf16[8,2,24,768]{3,2,1,0:T(8,128)(2,1)}), bf16[8,2,24,768]{3,2,1,0:T(8,128)(2,1)S(1)}, u32[]{:S(2)}, u32[]{:S(2)}) %all-to-all-start.2) | async-done | bytes 589856 | tf_op jit(solution)/shard_map/all_to_all | solution.py:141
  154.9 5.1 all-to-all-done
  169.2 6.5 reshape.597
  187.8 6.2 all-to-all-start.1
  198.0 28.8 %all-to-all-done.1 = bf16[8,2,24,768]{3,2,1,0:T(8,128)(2,1)} async-done(((bf16[8,2,24,768]{3,2,1,0:T(8,128)(2,1)}), bf16[8,2,24,768]{3,2,1,0:T(8,128)(2,1)}, u32[]{:S(2)}, u32[]{:S(2)}) %all-to-all-start.1) | async-done | bytes 589856 | tf_op jit(solution)/shard_map/all_to_all | solution.py:149
  246.9 10.2 %add_convert_fusion = (bf16[2,2,192,3072]{3,2,1,0:T(8,128)(2,1)}, bf16[2,2,192,3072]{3,2,1,0:T(8,128)(2,1)}) fusion(f32[2,2,192,3072]{3,2,1,0:T(8,128)S(1)} %bitcast.510, bf16[768,6144]{1,0:T(8,128)(2,1)S(1)} %bitcast.468, f32[768]{0:T(1024)S(1)} %get-tuple-element.80, f32[2,2,192]{2,1,0:T(2,128)S(1)} %add_rsqrt_fusion, ...), kind=kOutput, calls=%fused_computation.4 | convolution fusion | flops 3662217216 | bytes 25964544 | tf_op jit(solution)/shard_map/dot_general | solution.py:32
  257.1 6.7 convolution_convert_fusion
  266.2 5.2 bitcast_convert_fusion
  276.2 7.8 %fusion.21 = bf16[2,2,192,768]{3,2,1,0:T(8,128)(2,1)S(1)} fusion(bf16[2,2,192,3072]{3,2,1,0:T(8,128)(2,1)} %get-tuple-element.90, bf16[768,6144]{1,0:T(8,128)(2,1)} %all-gather.8.cloned.1.call-done), kind=kOutput, calls=%fused_computation.96 | convolution fusion | flops 3624468480 | bytes 10616832 | tf_op jit(solution)/shard_map/dot_general | solution.py:38
  301.8 10.6 %all-to-all-done.4 = bf16[8,2,24,768]{3,2,1,0:T(8,128)(2,1)} async-done(((bf16[8,2,24,768]{3,2,1,0:T(8,128)(2,1)}), bf16[8,2,24,768]{3,2,1,0:T(8,128)(2,1)}, u32[]{:S(2)}, u32[]{:S(2)}) %all-to-all-start.4) | async-done | bytes 589856 | tf_op jit(solution)/shard_map/all_to_all | solution.py:141
  333.5 6.6 convert_element_type.424
  340.0 6.6 convert_element_type.440
  363.1 6.4 all-to-all-start.5
  374.9 6.7 convert_element_type.447
  387.7 6.7 convert_element_type.450
  404.0 6.0 all-to-all-start.7
  411.0 14.0 %all-to-all-done.7 = bf16[8,2,24,768]{3,2,1,0:T(8,128)(2,1)S(1)} async-done(((bf16[8,2,24,768]{3,2,1,0:T(8,128)(2,1)}), bf16[8,2,24,768]{3,2,1,0:T(8,128)(2,1)S(1)}, u32[]{:S(2)}, u32[]{:S(2)}) %all-to-all-start.7) | async-done | bytes 589856 | tf_op jit(solution)/shard_map/all_to_all | solution.py:149
  488.2 9.1 %add_bitcast_fusion = f32[2,1,2,192,768]{4,3,2,1,0:T(8,128)} fusion(bf16[2,2,192,3072]{3,2,1,0:T(8,128)(2,1)} %get-tuple-element.91, bf16[3072,768,1,1]{1,0,3,2:T(8,128)(2,1)} %bitcast.480, f32[1,2,192,768]{3,2,1,0:T(8,128)S(1)} %bitcast.451, f32[1,2,192,768]{3,2,1,0:T(8,128)S(1)} %bitcast.456), kind=kOutput, calls=%fused_computation.67 | convolution fusion | flops 3625058304 | bytes 14155776 | tf_op jit(solution)/shard_map/dot_general | solution.py:32
  498.8 6.0 collective-permute-done.2
  511.4 58.9 %reduce-scatter.4.cloned.1.call-done = bf16[48,3200]{1,0:T(8,128)(2,1)} async-done(((bf16[768,3200]{1,0:T(8,128)(2,1)}), bf16[48,3200]{1,0:T(8,128)(2,1)}) %reduce-scatter.4.cloned.1.call-update) | async-done | bytes 307216 | tf_op jit(solution)/shard_map/reduce_scatter | solution.py:232
  572.6 5.3 collective-permute-done
  579.0 105.4 %reduce-scatter.8.cloned.1.call-done = bf16[48,6144]{1,0:T(8,128)(2,1)} async-done(((bf16[768,6144]{1,0:T(8,128)(2,1)}), bf16[48,6144]{1,0:T(8,128)(2,1)}) %reduce-scatter.8.cloned.1.call-update) | async-done | bytes 589840 | tf_op jit(solution)/shard_map/reduce_scatter | solution.py:232
  686.0 13.4 %collective-permute-done.4 = bf16[48,6144]{1,0:T(8,128)(2,1)S(1)} collective-permute-done((bf16[48,6144]{1,0:T(8,128)(2,1)}, bf16[48,6144]{1,0:T(8,128)(2,1)S(1)}, u32[]{:S(2)}, u32[]{:S(2)}) %collective-permute-start.4) | collective-permute-done | bytes 589856 | tf_op jit(solution)/shard_map/ppermute | solution.py:210
  (468 shorter events, 274.5 us)
Async XLA Ops:
  7.2 60.4 %all-gather.4.cloned.1.call-start = ((), (), s32[]{:S(2)}) async-start(), calls=%async_computation.11 | async-start | bytes 5222400 | tf_op jit(solution)/shard_map/all_gather | solution.py:204
  9.9 125.0 %all-gather.6.cloned.1.call-start = ((), (), s32[]{:S(2)}) async-start(), calls=%async_computation.12 | async-start | bytes 5013504 | tf_op jit(solution)/shard_map/all_gather | solution.py:204
  10.8 226.9 %all-gather.8.cloned.1.call-start = ((), (), s32[]{:S(2)}) async-start(), calls=%async_computation.13 | async-start | bytes 10027008 | tf_op jit(solution)/shard_map/all_gather | solution.py:204
  12.2 63.6 %copy-start.96 = (f32[2,192]{1,0:T(2,128)}, f32[2,192]{1,0:T(2,128)S(1)}, u32[]{:S(2)}) copy-start(f32[2,192]{1,0:T(2,128)S(1)} %broadcast_multiply_fusion.6) | copy-start | bytes 4612
  12.2 60.7 %copy-start.98 = (f32[2,192]{1,0:T(2,128)}, f32[2,192]{1,0:T(2,128)S(1)}, u32[]{:S(2)}) copy-start(f32[2,192]{1,0:T(2,128)S(1)} %broadcast_multiply_fusion.4) | copy-start | bytes 4612
  12.7 60.2 %copy-start.102 = (f32[2,192]{1,0:T(2,128)}, f32[2,192]{1,0:T(2,128)S(1)}, u32[]{:S(2)}) copy-start(f32[2,192]{1,0:T(2,128)S(1)} %get-tuple-element.75) | copy-start | bytes 4612
  12.7 63.1 %copy-start.110 = (f32[2,192]{1,0:T(2,128)}, f32[2,192]{1,0:T(2,128)S(1)}, u32[]{:S(2)}) copy-start(f32[2,192]{1,0:T(2,128)S(1)} %fusion.125) | copy-start | bytes 4612
  98.6 31.9 %all-to-all-start.2 = ((bf16[8,2,24,768]{3,2,1,0:T(8,128)(2,1)}), bf16[8,2,24,768]{3,2,1,0:T(8,128)(2,1)S(1)}, u32[]{:S(2)}, u32[]{:S(2)}) async-start(bf16[8,2,24,768]{3,2,1,0:T(8,128)(2,1)} %bitcast.441), calls=%async_computation.2 | async-start | bytes 1179648 | tf_op jit(solution)/shard_map/all_to_all | solution.py:141
  130.5 29.5 %all-to-all-start = ((bf16[8,2,24,768]{3,2,1,0:T(8,128)(2,1)}), bf16[8,2,24,768]{3,2,1,0:T(8,128)(2,1)S(1)}, u32[]{:S(2)}, u32[]{:S(2)}) async-start(bf16[8,2,24,768]{3,2,1,0:T(8,128)(2,1)} %bitcast.442), calls=%async_computation | async-start | bytes 1179648 | tf_op jit(solution)/shard_map/all_to_all | solution.py:141
  160.0 27.8 %all-to-all-start.3 = ((bf16[8,2,24,768]{3,2,1,0:T(8,128)(2,1)}), bf16[8,2,24,768]{3,2,1,0:T(8,128)(2,1)}, u32[]{:S(2)}, u32[]{:S(2)}) async-start(bf16[8,2,24,768]{3,2,1,0:T(8,128)(2,1)} %convert_element_type.404), calls=%async_computation.3 | async-start | bytes 1179648 | tf_op jit(solution)/shard_map/all_to_all | solution.py:149
  187.8 39.1 %all-to-all-start.1 = ((bf16[8,2,24,768]{3,2,1,0:T(8,128)(2,1)}), bf16[8,2,24,768]{3,2,1,0:T(8,128)(2,1)}, u32[]{:S(2)}, u32[]{:S(2)}) async-start(bf16[8,2,24,768]{3,2,1,0:T(8,128)(2,1)} %convert_element_type.390), calls=%async_computation.1 | async-start | bytes 1179648 | tf_op jit(solution)/shard_map/all_to_all | solution.py:149
  291.5 20.8 %all-to-all-start.4 = ((bf16[8,2,24,768]{3,2,1,0:T(8,128)(2,1)}), bf16[8,2,24,768]{3,2,1,0:T(8,128)(2,1)}, u32[]{:S(2)}, u32[]{:S(2)}) async-start(bf16[8,2,24,768]{3,2,1,0:T(8,128)(2,1)} %bitcast.497), calls=%async_computation.4 | async-start | bytes 1179648 | tf_op jit(solution)/shard_map/all_to_all | solution.py:141
  312.3 34.3 %all-to-all-start.6 = ((bf16[8,2,24,768]{3,2,1,0:T(8,128)(2,1)}), bf16[8,2,24,768]{3,2,1,0:T(8,128)(2,1)S(1)}, u32[]{:S(2)}, u32[]{:S(2)}) async-start(bf16[8,2,24,768]{3,2,1,0:T(8,128)(2,1)} %bitcast.496), calls=%async_computation.6 | async-start | bytes 1179648 | tf_op jit(solution)/shard_map/all_to_all | solution.py:141
  363.1 41.0 %all-to-all-start.5 = ((bf16[8,2,24,768]{3,2,1,0:T(8,128)(2,1)}), bf16[8,2,24,768]{3,2,1,0:T(8,128)(2,1)S(1)}, u32[]{:S(2)}, u32[]{:S(2)}) async-start(bf16[8,2,24,768]{3,2,1,0:T(8,128)(2,1)} %bitcast.504), calls=%async_computation.5 | async-start | bytes 1179648 | tf_op jit(solution)/shard_map/all_to_all | solution.py:149
  404.0 21.0 %all-to-all-start.7 = ((bf16[8,2,24,768]{3,2,1,0:T(8,128)(2,1)}), bf16[8,2,24,768]{3,2,1,0:T(8,128)(2,1)S(1)}, u32[]{:S(2)}, u32[]{:S(2)}) async-start(bf16[8,2,24,768]{3,2,1,0:T(8,128)(2,1)} %bitcast.96), calls=%async_computation.7 | async-start | bytes 1179648 | tf_op jit(solution)/shard_map/all_to_all | solution.py:149
  410.0 87.2 %reduce-scatter.6.cloned.1.call-start = ((), (), s32[]{:S(2)}) async-start(), calls=%async_computation.15 | async-start | bytes 5013504 | tf_op jit(solution)/shard_map/reduce_scatter | solution.py:232
  410.6 159.8 %reduce-scatter.4.cloned.1.call-start = ((), (), s32[]{:S(2)}) async-start(), calls=%async_computation.14 | async-start | bytes 5222400 | tf_op jit(solution)/shard_map/reduce_scatter | solution.py:232
  486.5 197.9 %reduce-scatter.8.cloned.1.call-start = ((), (), s32[]{:S(2)}) async-start(), calls=%async_computation.16 | async-start | bytes 10027008 | tf_op jit(solution)/shard_map/reduce_scatter | solution.py:232
  497.3 7.5 %collective-permute-start.2 = (bf16[48,3072]{1,0:T(8,128)(2,1)}, bf16[48,3072]{1,0:T(8,128)(2,1)S(1)}, u32[]{:S(2)}, u32[]{:S(2)}) collective-permute-start(bf16[48,3072]{1,0:T(8,128)(2,1)} %reduce-scatter.6.cloned.1.call-done), channel_id=1, source_target_pairs={{0,16},{16,0},{1,17},{17,1},{2,18},{18,2},{3,19},{19,3},{4,20},{20... | collective-permute-start | bytes 884744 | tf_op jit(solution)/shard_map/ppermute | solution.py:210
  505.9 66.0 %collective-permute-start.3 = (bf16[48,3072]{1,0:T(8,128)(2,1)S(1)}, bf16[48,3072]{1,0:T(8,128)(2,1)S(1)}, u32[]{:S(2)}, u32[]{:S(2)}) collective-permute-start(bf16[48,3072]{1,0:T(8,128)(2,1)S(1)} %add.262), channel_id=1, source_target_pairs={{0,8},{8,0},{1,9},{9,1},{2,10},{10,2},{3,11},{11,3},{4,12},{12,4},... | collective-permute-start | bytes 884744 | tf_op jit(solution)/shard_map/ppermute | solution.py:216
  570.4 7.5 %collective-permute-start = (bf16[48,3200]{1,0:T(8,128)(2,1)}, bf16[48,3200]{1,0:T(8,128)(2,1)S(1)}, u32[]{:S(2)}, u32[]{:S(2)}) collective-permute-start(bf16[48,3200]{1,0:T(8,128)(2,1)} %reduce-scatter.4.cloned.1.call-done), channel_id=1, source_target_pairs={{0,16},{16,0},{1,17},{17,1},{2,18},{18,2},{3,19},{19,3},{4,20},{20... | collective-permute-start | bytes 921608 | tf_op jit(solution)/shard_map/ppermute | solution.py:210
  578.0 108.0 %collective-permute-start.1 = (bf16[48,3200]{1,0:T(8,128)(2,1)S(1)}, bf16[48,3200]{1,0:T(8,128)(2,1)S(1)}, u32[]{:S(2)}, u32[]{:S(2)}) collective-permute-start(bf16[48,3200]{1,0:T(8,128)(2,1)S(1)} %add.261), channel_id=1, source_target_pairs={{0,8},{8,0},{1,9},{9,1},{2,10},{10,2},{3,11},{11,3},{4,12},{12,4},... | collective-permute-start | bytes 921608 | tf_op jit(solution)/shard_map/ppermute | solution.py:216
  684.5 15.0 %collective-permute-start.4 = (bf16[48,6144]{1,0:T(8,128)(2,1)}, bf16[48,6144]{1,0:T(8,128)(2,1)S(1)}, u32[]{:S(2)}, u32[]{:S(2)}) collective-permute-start(bf16[48,6144]{1,0:T(8,128)(2,1)} %reduce-scatter.8.cloned.1.call-done), channel_id=1, source_target_pairs={{0,16},{16,0},{1,17},{17,1},{2,18},{18,2},{3,19},{19,3},{4,20},{20... | collective-permute-start | bytes 1769480 | tf_op jit(solution)/shard_map/ppermute | solution.py:210
  699.6 2.5 collective-permute-start.5
  (119 other events, 506.1 us)
Sparse Core Ops, SparseCore 0:
  10.8 56.8 all-gather.3
  70.5 62.2 all-gather.5
  135.6 102.0 all-gather.7
  414.4 76.9 reduce-scatter.5
  495.2 75.1 reduce-scatter.3
  574.3 110.0 reduce-scatter.7

commit v7 on v6

--- a/solution.py
+++ b/solution.py
@@ -305,8 +305,8 @@
     back_three_all = back_dot(back_hidden, h_in).astype(jnp.bfloat16)
     ffn_grads = (grad_hidden_in, grad_hidden_out)
     ffn_kinds = ("plain", "grouped")
-    packed_ffn, back_three_all = lax.optimization_barrier(
-        (pack_group(ffn_grads, ffn_kinds, members, half), back_three_all)
+    packed_ffn, t_in, t_out = lax.optimization_barrier(
+        (pack_group(ffn_grads, ffn_kinds, members, half), t_in, t_out)
     )
     grad_ffn = reduce_group(packed_ffn, ffn_grads, ffn_kinds, half)
     back_threes = [back_three_all[index] for index in range(micro)]
@@ -332,8 +332,8 @@
         back_twos_placed.append(back_dot(back_join, t_in).astype(jnp.bfloat16))
     time_grads = (summed(time_in_terms), summed(time_out_terms))
     time_kinds = ("plain", "plain")
-    packed_time, back_twos_placed[-1] = lax.optimization_barrier(
-        (pack_group(time_grads, time_kinds, members, half), back_twos_placed[-1])
+    packed_time, s_in, s_out = lax.optimization_barrier(
+        (pack_group(time_grads, time_kinds, members, half), s_in, s_out)
     )
     grad_time = reduce_group(packed_time, time_grads, time_kinds, half)
 

time: 717 us -> 723 us (level)
  waiting for transfers between devices: 335 us -> 322 us
  local copies, waits for them, and re-layouts: 112 us -> 122 us
    all_to_all x4, waiting for transfers between devices: 42.9 us -> 25.8 us  [to_frames(): lax.all_to_all(blocks, 'fsdp', split_axis=0, concat_axis=0, tiled=True)]
    slice x2 -> x6, local copies, waits for them, and re-layouts: 2.34 us -> 11.9 us  [from_members(): part = block[:, offset:offset + width]]
    unnamed x250 -> x258, local copies, waits for them, and re-layouts: 24.1 us -> 23.5 us
  transfers between devices with their start and end apart: 20 -> 20, of which waited for: 12 -> 13; matrix products, arithmetic and copies ran while one was open for 31% -> 32% of each run, Pallas kernels for 0% -> 0%
where the time goes in v7:
time: 723 us; the launch traced here: 717 us
  waiting for transfers between devices  322 us (45%)
  matrix products  157 us (22%)
  local copies, waits for them, and re-layouts  122 us (17%)
  other arithmetic  56.3 us (8%)
  starting transfers between devices  43.2 us (6%)
  between operations  16.4 us (2%)
    reduce_scatter x3, waiting for transfers between devices, reduce_group(): owned = lax.psum_scatter(packed, MEMBERS, scatter_dimension=0, tiled=True)  169 us
    all_gather x3, waiting for transfers between devices, gather_group(): gathered = lax.all_gather(block, MEMBERS, axis=0, tiled=True)  58.7 us
    dot_general x10, matrix products, flat_dot(): product = jnp.dot(flat, right, preferred_element_type=jnp.float32)  47 us
    all_to_all x4, waiting for transfers between devices, to_places(): lax.all_to_all(blocks, 'fsdp', split_axis=0, concat_axis=0, tiled=True)  43.9 us
    convert_element_type x8, local copies, waits for them, and re-layouts, attend_back(): stacked.reshape(back_context.shape[:-1] + (3 * D,)).astype(jnp.bfloat16)  35.8 us
    dot_general x10, matrix products, token_sum(): lax.dot_general(left_rows, right_rows, (((0,), (0,)), ((), ())), preferre...  34.9 us
    dot_general x10, matrix products, back_dot(): lax.dot_general(flat, right, (((1,), (1,)), ((), ())), preferred_element_...  30.6 us
    all_to_all x4, waiting for transfers between devices, to_frames(): lax.all_to_all(blocks, 'fsdp', split_axis=0, concat_axis=0, tiled=True)  25.8 us
  transfers between devices with their start and end apart: 20, of which 13 were waited for; matrix products, arithmetic and copies ran while one was open for 32% of the time, Pallas kernels for 0%

profile of v7, /device:TPU:0, one launch (start us, length us, event | category | flops | bytes accessed | tf_op | source)
XLA Modules:
  0.0 716.9 jit_solution(3832585629895410899)
XLA Ops:
  12.7 54.9 %all-gather.4.cloned.1.call-done = bf16[768,3200]{1,0:T(8,128)(2,1)} async-done(((bf16[48,3200]{1,0:T(8,128)(2,1)}), bf16[768,3200]{1,0:T(8,128)(2,1)}) %all-gather.4.cloned.1.call-update) | async-done | bytes 4915216 | tf_op jit(solution)/shard_map/all_gather | solution.py:204
  103.0 27.5 %all-to-all-done.2 = bf16[8,2,24,768]{3,2,1,0:T(8,128)(2,1)S(1)} async-done(((bf16[8,2,24,768]{3,2,1,0:T(8,128)(2,1)}), bf16[8,2,24,768]{3,2,1,0:T(8,128)(2,1)S(1)}, u32[]{:S(2)}, u32[]{:S(2)}) %all-to-all-start.2) | async-done | bytes 589856 | tf_op jit(solution)/shard_map/all_to_all | solution.py:141
  169.2 6.4 reshape.597
  187.7 6.2 all-to-all-start.1
  207.7 19.1 %all-to-all-done.1 = bf16[8,2,24,768]{3,2,1,0:T(8,128)(2,1)} async-done(((bf16[8,2,24,768]{3,2,1,0:T(8,128)(2,1)}), bf16[8,2,24,768]{3,2,1,0:T(8,128)(2,1)}, u32[]{:S(2)}, u32[]{:S(2)}) %all-to-all-start.1) | async-done | bytes 589856 | tf_op jit(solution)/shard_map/all_to_all | solution.py:149
  241.8 6.7 fusion.2
  250.2 11.4 %add_convert_fusion = (bf16[2,2,192,3072]{3,2,1,0:T(8,128)(2,1)}, bf16[2,2,192,3072]{3,2,1,0:T(8,128)(2,1)S(1)}) fusion(f32[2,2,192,3072]{3,2,1,0:T(8,128)} %bitcast.539, bf16[768,6144]{1,0:T(8,128)(2,1)S(1)} %bitcast.496, f32[768]{0:T(1024)S(1)} %get-tuple-element.84, f32[2,2,192]{2,1,0:T(2,128)S(1)} %add_rsqrt_fusion, ...), kind=kOutput, calls=%fused_computation.4 | convolution fusion | flops 3662217216 | bytes 25964544 | tf_op jit(solution)/shard_map/dot_general | solution.py:32
  261.5 8.9 %bitcast_convert_fusion = bf16[768,3072]{1,0:T(8,128)(2,1)S(1)} fusion(bf16[2,2,192,3072]{3,2,1,0:T(8,128)(2,1)} %get-tuple-element.94, f32[768]{0:T(1024)S(1)} %get-tuple-element.84, f32[2,2,192]{2,1,0:T(2,128)S(1)} %add_rsqrt_fusion, f32[2,2,192]{2,1,0:T(2,128)S(1)} %broadcast_multiply_fusion, f32[1,2,192,768]{3,2,1,0:T(8,128)S(1)} %bitcast.478, ...), kind=kOutput, calls=%fused_computation.3 | convolution fusion | flops 3629187072 | bytes 11805696 | tf_op jit(solution)/shard_map/dot_general | solution.py:47
  270.5 6.3 fusion.33
  304.8 10.5 %all-to-all-done.4 = bf16[8,2,24,768]{3,2,1,0:T(8,128)(2,1)} async-done(((bf16[8,2,24,768]{3,2,1,0:T(8,128)(2,1)}), bf16[8,2,24,768]{3,2,1,0:T(8,128)(2,1)}, u32[]{:S(2)}, u32[]{:S(2)}) %all-to-all-start.4) | async-done | bytes 589856 | tf_op jit(solution)/shard_map/all_to_all | solution.py:141
  352.0 6.6 convert_element_type.424
  363.5 5.7 all-to-all-start.5
  372.4 6.6 convert_element_type.430
  379.0 5.4 copy.236
  384.4 6.6 convert_element_type.450
  390.9 5.6 convert_element_type.439
  396.6 6.5 fusion.194
  405.5 6.1 all-to-all-start.7
  420.1 6.7 all-to-all-done.7
  489.6 9.1 %add_bitcast_fusion = f32[2,1,2,192,768]{4,3,2,1,0:T(8,128)} fusion(bf16[2,2,192,3072]{3,2,1,0:T(8,128)(2,1)} %copy-done.116, bf16[3072,768,1,1]{1,0,3,2:T(8,128)(2,1)} %bitcast.510, f32[1,2,192,768]{3,2,1,0:T(8,128)S(1)} %bitcast.479, f32[1,2,192,768]{3,2,1,0:T(8,128)S(1)} %bitcast.484), kind=kOutput, calls=%fused_computation.77 | convolution fusion | flops 3625058304 | bytes 14155776 | tf_op jit(solution)/shard_map/dot_general | solution.py:32
  500.1 5.7 collective-permute-done.2
  512.3 63.4 %reduce-scatter.4.cloned.1.call-done = bf16[48,3200]{1,0:T(8,128)(2,1)} async-done(((bf16[768,3200]{1,0:T(8,128)(2,1)}), bf16[48,3200]{1,0:T(8,128)(2,1)}) %reduce-scatter.4.cloned.1.call-update) | async-done | bytes 307216 | tf_op jit(solution)/shard_map/reduce_scatter | solution.py:232
  584.3 105.4 %reduce-scatter.8.cloned.1.call-done = bf16[48,6144]{1,0:T(8,128)(2,1)} async-done(((bf16[768,6144]{1,0:T(8,128)(2,1)}), bf16[48,6144]{1,0:T(8,128)(2,1)}) %reduce-scatter.8.cloned.1.call-update) | async-done | bytes 589840 | tf_op jit(solution)/shard_map/reduce_scatter | solution.py:232
  691.3 13.5 %collective-permute-done.4 = bf16[48,6144]{1,0:T(8,128)(2,1)S(1)} collective-permute-done((bf16[48,6144]{1,0:T(8,128)(2,1)}, bf16[48,6144]{1,0:T(8,128)(2,1)S(1)}, u32[]{:S(2)}, u32[]{:S(2)}) %collective-permute-start.4) | collective-permute-done | bytes 589856 | tf_op jit(solution)/shard_map/ppermute | solution.py:210
  (480 shorter events, 289.8 us)
Async XLA Ops:
  7.2 60.4 %all-gather.4.cloned.1.call-start = ((), (), s32[]{:S(2)}) async-start(), calls=%async_computation.11 | async-start | bytes 5222400 | tf_op jit(solution)/shard_map/all_gather | solution.py:204
  9.9 124.9 %all-gather.6.cloned.1.call-start = ((), (), s32[]{:S(2)}) async-start(), calls=%async_computation.12 | async-start | bytes 5013504 | tf_op jit(solution)/shard_map/all_gather | solution.py:204
  10.8 226.9 %all-gather.8.cloned.1.call-start = ((), (), s32[]{:S(2)}) async-start(), calls=%async_computation.13 | async-start | bytes 10027008 | tf_op jit(solution)/shard_map/all_gather | solution.py:204
  12.2 63.6 %copy-start.100 = (f32[2,192]{1,0:T(2,128)}, f32[2,192]{1,0:T(2,128)S(1)}, u32[]{:S(2)}) copy-start(f32[2,192]{1,0:T(2,128)S(1)} %broadcast_multiply_fusion.6) | copy-start | bytes 4612
  12.2 60.7 %copy-start.102 = (f32[2,192]{1,0:T(2,128)}, f32[2,192]{1,0:T(2,128)S(1)}, u32[]{:S(2)}) copy-start(f32[2,192]{1,0:T(2,128)S(1)} %broadcast_multiply_fusion.4) | copy-start | bytes 4612
  12.7 60.2 %copy-start.106 = (f32[2,192]{1,0:T(2,128)}, f32[2,192]{1,0:T(2,128)S(1)}, u32[]{:S(2)}) copy-start(f32[2,192]{1,0:T(2,128)S(1)} %get-tuple-element.79) | copy-start | bytes 4612
  12.7 63.1 %copy-start.114 = (f32[2,192]{1,0:T(2,128)}, f32[2,192]{1,0:T(2,128)S(1)}, u32[]{:S(2)}) copy-start(f32[2,192]{1,0:T(2,128)S(1)} %fusion.157) | copy-start | bytes 4612
  98.5 32.0 %all-to-all-start.2 = ((bf16[8,2,24,768]{3,2,1,0:T(8,128)(2,1)}), bf16[8,2,24,768]{3,2,1,0:T(8,128)(2,1)S(1)}, u32[]{:S(2)}, u32[]{:S(2)}) async-start(bf16[8,2,24,768]{3,2,1,0:T(8,128)(2,1)} %bitcast.469), calls=%async_computation.2 | async-start | bytes 1179648 | tf_op jit(solution)/shard_map/all_to_all | solution.py:141
  130.5 29.5 %all-to-all-start = ((bf16[8,2,24,768]{3,2,1,0:T(8,128)(2,1)}), bf16[8,2,24,768]{3,2,1,0:T(8,128)(2,1)S(1)}, u32[]{:S(2)}, u32[]{:S(2)}) async-start(bf16[8,2,24,768]{3,2,1,0:T(8,128)(2,1)} %bitcast.470), calls=%async_computation | async-start | bytes 1179648 | tf_op jit(solution)/shard_map/all_to_all | solution.py:141
  160.0 27.8 %all-to-all-start.3 = ((bf16[8,2,24,768]{3,2,1,0:T(8,128)(2,1)}), bf16[8,2,24,768]{3,2,1,0:T(8,128)(2,1)}, u32[]{:S(2)}, u32[]{:S(2)}) async-start(bf16[8,2,24,768]{3,2,1,0:T(8,128)(2,1)} %convert_element_type.404), calls=%async_computation.3 | async-start | bytes 1179648 | tf_op jit(solution)/shard_map/all_to_all | solution.py:149
  187.7 39.1 %all-to-all-start.1 = ((bf16[8,2,24,768]{3,2,1,0:T(8,128)(2,1)}), bf16[8,2,24,768]{3,2,1,0:T(8,128)(2,1)}, u32[]{:S(2)}, u32[]{:S(2)}) async-start(bf16[8,2,24,768]{3,2,1,0:T(8,128)(2,1)} %convert_element_type.390), calls=%async_computation.1 | async-start | bytes 1179648 | tf_op jit(solution)/shard_map/all_to_all | solution.py:149
  294.5 20.8 %all-to-all-start.4 = ((bf16[8,2,24,768]{3,2,1,0:T(8,128)(2,1)}), bf16[8,2,24,768]{3,2,1,0:T(8,128)(2,1)}, u32[]{:S(2)}, u32[]{:S(2)}) async-start(bf16[8,2,24,768]{3,2,1,0:T(8,128)(2,1)} %bitcast.527), calls=%async_computation.4 | async-start | bytes 1179648 | tf_op jit(solution)/shard_map/all_to_all | solution.py:141
  315.3 19.9 %all-to-all-start.6 = ((bf16[8,2,24,768]{3,2,1,0:T(8,128)(2,1)}), bf16[8,2,24,768]{3,2,1,0:T(8,128)(2,1)S(1)}, u32[]{:S(2)}, u32[]{:S(2)}) async-start(bf16[8,2,24,768]{3,2,1,0:T(8,128)(2,1)} %bitcast.526), calls=%async_computation.6 | async-start | bytes 1179648 | tf_op jit(solution)/shard_map/all_to_all | solution.py:141
  363.5 42.0 %all-to-all-start.5 = ((bf16[8,2,24,768]{3,2,1,0:T(8,128)(2,1)}), bf16[8,2,24,768]{3,2,1,0:T(8,128)(2,1)S(1)}, u32[]{:S(2)}, u32[]{:S(2)}) async-start(bf16[8,2,24,768]{3,2,1,0:T(8,128)(2,1)} %bitcast.535), calls=%async_computation.5 | async-start | bytes 1179648 | tf_op jit(solution)/shard_map/all_to_all | solution.py:149
  405.5 21.3 %all-to-all-start.7 = ((bf16[8,2,24,768]{3,2,1,0:T(8,128)(2,1)}), bf16[8,2,24,768]{3,2,1,0:T(8,128)(2,1)}, u32[]{:S(2)}, u32[]{:S(2)}) async-start(bf16[8,2,24,768]{3,2,1,0:T(8,128)(2,1)} %bitcast.534), calls=%async_computation.7 | async-start | bytes 1179648 | tf_op jit(solution)/shard_map/all_to_all | solution.py:149
  411.7 87.1 %reduce-scatter.6.cloned.1.call-start = ((), (), s32[]{:S(2)}) async-start(), calls=%async_computation.15 | async-start | bytes 5013504 | tf_op jit(solution)/shard_map/reduce_scatter | solution.py:232
  419.7 156.0 %reduce-scatter.4.cloned.1.call-start = ((), (), s32[]{:S(2)}) async-start(), calls=%async_computation.14 | async-start | bytes 5222400 | tf_op jit(solution)/shard_map/reduce_scatter | solution.py:232
  488.0 201.7 %reduce-scatter.8.cloned.1.call-start = ((), (), s32[]{:S(2)}) async-start(), calls=%async_computation.16 | async-start | bytes 10027008 | tf_op jit(solution)/shard_map/reduce_scatter | solution.py:232
  498.8 7.1 collective-permute-start.2
  506.9 70.3 %collective-permute-start.3 = (bf16[48,3072]{1,0:T(8,128)(2,1)S(1)}, bf16[48,3072]{1,0:T(8,128)(2,1)S(1)}, u32[]{:S(2)}, u32[]{:S(2)}) collective-permute-start(bf16[48,3072]{1,0:T(8,128)(2,1)S(1)} %add.262), channel_id=1, source_target_pairs={{0,8},{8,0},{1,9},{9,1},{2,10},{10,2},{3,11},{11,3},{4,12},{12,4},... | collective-permute-start | bytes 884744 | tf_op jit(solution)/shard_map/ppermute | solution.py:216
  575.7 7.5 %collective-permute-start = (bf16[48,3200]{1,0:T(8,128)(2,1)}, bf16[48,3200]{1,0:T(8,128)(2,1)S(1)}, u32[]{:S(2)}, u32[]{:S(2)}) collective-permute-start(bf16[48,3200]{1,0:T(8,128)(2,1)} %reduce-scatter.4.cloned.1.call-done), channel_id=1, source_target_pairs={{0,16},{16,0},{1,17},{17,1},{2,18},{18,2},{3,19},{19,3},{4,20},{20... | collective-permute-start | bytes 921608 | tf_op jit(solution)/shard_map/ppermute | solution.py:210
  583.3 107.9 %collective-permute-start.1 = (bf16[48,3200]{1,0:T(8,128)(2,1)S(1)}, bf16[48,3200]{1,0:T(8,128)(2,1)S(1)}, u32[]{:S(2)}, u32[]{:S(2)}) collective-permute-start(bf16[48,3200]{1,0:T(8,128)(2,1)S(1)} %add.261), channel_id=1, source_target_pairs={{0,8},{8,0},{1,9},{9,1},{2,10},{10,2},{3,11},{11,3},{4,12},{12,4},... | collective-permute-start | bytes 921608 | tf_op jit(solution)/shard_map/ppermute | solution.py:216
  689.7 15.0 %collective-permute-start.4 = (bf16[48,6144]{1,0:T(8,128)(2,1)}, bf16[48,6144]{1,0:T(8,128)(2,1)S(1)}, u32[]{:S(2)}, u32[]{:S(2)}) collective-permute-start(bf16[48,6144]{1,0:T(8,128)(2,1)} %reduce-scatter.8.cloned.1.call-done), channel_id=1, source_target_pairs={{0,16},{16,0},{1,17},{17,1},{2,18},{18,2},{3,19},{19,3},{4,20},{20... | collective-permute-start | bytes 1769480 | tf_op jit(solution)/shard_map/ppermute | solution.py:210
  704.9 2.5 collective-permute-start.5
  (123 other events, 549.7 us)
Sparse Core Ops, SparseCore 0:
  10.8 56.8 all-gather.3
  70.5 62.2 all-gather.5
  135.6 102.0 all-gather.7
  419.8 76.9 reduce-scatter.5
  500.6 75.0 reduce-scatter.3
  579.7 110.0 reduce-scatter.7

commit v8 on v7

--- a/solution.py
+++ b/solution.py
@@ -309,7 +309,11 @@
         (pack_group(ffn_grads, ffn_kinds, members, half), t_in, t_out)
     )
     grad_ffn = reduce_group(packed_ffn, ffn_grads, ffn_kinds, half)
-    back_threes = [back_three_all[index] for index in range(micro)]
+    back_mixed, gain_grad = norm_back(mixed_two, gain_rows[2], back_three_all.astype(jnp.float32))
+    gain_two_terms.append(gain_grad)
+    upstream_all = upstream_all + back_mixed
+    rounded_all = upstream_all.astype(jnp.bfloat16)
+    back_context_all = back_dot(rounded_all, t_out).astype(jnp.bfloat16)
     upstreams = [upstream_all[index] for index in range(micro)]
 
     back_twos_placed = []
@@ -317,23 +321,15 @@
     time_in_terms = []
     for index in range(micro):
         s = saved[index]
-        back_mixed, gain_grad = norm_back(
-            mixed_twos[index], gain_rows[2], back_threes[index].astype(jnp.float32)
-        )
-        gain_two_terms.append(gain_grad)
-        upstream = upstreams[index] + back_mixed
-        upstreams[index] = upstream
-        rounded = upstream.astype(jnp.bfloat16)
-        time_out_terms.append(token_sum(s["context_time"], rounded))
-        back_context = back_dot(rounded, t_out).astype(jnp.bfloat16)
-        back_placed = to_places(back_context)
+        time_out_terms.append(token_sum(s["context_time"], rounded_all[index]))
+        back_placed = to_places(back_context_all[index])
         back_join = attend_back(s["join_time"], s["total_time"], back_placed, *temporal)
         time_in_terms.append(token_sum(s["placed"], back_join))
         back_twos_placed.append(back_dot(back_join, t_in).astype(jnp.bfloat16))
     time_grads = (summed(time_in_terms), summed(time_out_terms))
     time_kinds = ("plain", "plain")
-    packed_time, s_in, s_out = lax.optimization_barrier(
-        (pack_group(time_grads, time_kinds, members, half), s_in, s_out)
+    packed_time, back_twos_placed[-1] = lax.optimization_barrier(
+        (pack_group(time_grads, time_kinds, members, half), back_twos_placed[-1])
     )
     grad_time = reduce_group(packed_time, time_grads, time_kinds, half)
 

time: 723 us -> 721 us (level)
  local copies, waits for them, and re-layouts: 122 us -> 111 us
  waiting for transfers between devices: 322 us -> 332 us
    all_to_all x4, waiting for transfers between devices: 25.8 us -> 43.3 us  [to_frames(): lax.all_to_all(blocks, 'fsdp', split_axis=0, concat_axis=0, tiled=True)]
    unnamed x258 -> x230, local copies, waits for them, and re-layouts: 23.5 us -> 17.1 us
    dot_general x10 -> x9, matrix products: 30.6 us -> 34.7 us  [back_dot(): lax.dot_general(flat, right, (((1,), (1,)), ((), ())), preferred_element_...]
  transfers between devices with their start and end apart: 20 -> 20, of which waited for: 13 -> 13; matrix products, arithmetic and copies ran while one was open for 32% -> 29% of each run, Pallas kernels for 0% -> 0%
where the time goes in v8:
time: 721 us; the launch traced here: 715 us
  waiting for transfers between devices  332 us (46%)
  matrix products  159 us (22%)
  local copies, waits for them, and re-layouts  111 us (15%)
  other arithmetic  56.4 us (8%)
  starting transfers between devices  40 us (6%)
  between operations  16.4 us (2%)
    reduce_scatter x3, waiting for transfers between devices, reduce_group(): owned = lax.psum_scatter(packed, MEMBERS, scatter_dimension=0, tiled=True)  168 us
    all_gather x3, waiting for transfers between devices, gather_group(): gathered = lax.all_gather(block, MEMBERS, axis=0, tiled=True)  53.2 us
    dot_general x10, matrix products, flat_dot(): product = jnp.dot(flat, right, preferred_element_type=jnp.float32)  49.1 us
    all_to_all x4, waiting for transfers between devices, to_frames(): lax.all_to_all(blocks, 'fsdp', split_axis=0, concat_axis=0, tiled=True)  43.3 us
    all_to_all x4, waiting for transfers between devices, to_places(): lax.all_to_all(blocks, 'fsdp', split_axis=0, concat_axis=0, tiled=True)  42 us
    dot_general x9, matrix products, back_dot(): lax.dot_general(flat, right, (((1,), (1,)), ((), ())), preferred_element_...  34.7 us
    convert_element_type x8, local copies, waits for them, and re-layouts, attend_back(): stacked.reshape(back_context.shape[:-1] + (3 * D,)).astype(jnp.bfloat16)  32.9 us
    dot_general x10, matrix products, token_sum(): lax.dot_general(left_rows, right_rows, (((0,), (0,)), ((), ())), preferre...  30.1 us
  transfers between devices with their start and end apart: 20, of which 13 were waited for; matrix products, arithmetic and copies ran while one was open for 29% of the time, Pallas kernels for 0%

profile of v8, /device:TPU:0, one launch (start us, length us, event | category | flops | bytes accessed | tf_op | source)
XLA Modules:
  0.0 715.5 jit_solution(9836637147424221001)
XLA Ops:
  14.5 53.1 %all-gather.4.cloned.1.call-done = bf16[768,3200]{1,0:T(8,128)(2,1)} async-done(((bf16[48,3200]{1,0:T(8,128)(2,1)}), bf16[768,3200]{1,0:T(8,128)(2,1)}) %all-gather.4.cloned.1.call-update) | async-done | bytes 4915216 | tf_op jit(solution)/shard_map/all_gather | solution.py:204
  77.4 5.9 convolution_convert_fusion.5
  109.2 23.1 %all-to-all-done.2 = bf16[8,2,24,768]{3,2,1,0:T(8,128)(2,1)S(1)} async-done(((bf16[8,2,24,768]{3,2,1,0:T(8,128)(2,1)}), bf16[8,2,24,768]{3,2,1,0:T(8,128)(2,1)S(1)}, u32[]{:S(2)}, u32[]{:S(2)}) %all-to-all-start.2) | async-done | bytes 589856 | tf_op jit(solution)/shard_map/all_to_all | solution.py:141
  155.9 7.0 all-to-all-done
  172.5 6.5 reshape.522
  203.9 25.7 %all-to-all-done.1 = bf16[8,2,24,768]{3,2,1,0:T(8,128)(2,1)} async-done(((bf16[8,2,24,768]{3,2,1,0:T(8,128)(2,1)}), bf16[8,2,24,768]{3,2,1,0:T(8,128)(2,1)}, u32[]{:S(2)}, u32[]{:S(2)}) %all-to-all-start.1) | async-done | bytes 589856 | tf_op jit(solution)/shard_map/all_to_all | solution.py:149
  240.8 6.7 fusion.2
  249.2 11.4 %add_convert_fusion = (bf16[2,2,192,3072]{3,2,1,0:T(8,128)(2,1)}, bf16[2,2,192,3072]{3,2,1,0:T(8,128)(2,1)S(1)}) fusion(f32[2,2,192,3072]{3,2,1,0:T(8,128)} %bitcast.503, bf16[768,6144]{1,0:T(8,128)(2,1)S(1)} %bitcast.461, f32[768]{0:T(1024)S(1)} %get-tuple-element.74, f32[2,2,192]{2,1,0:T(2,128)S(1)} %fusion.136, ...), kind=kOutput, calls=%fused_computation.4 | convolution fusion | flops 3662217216 | bytes 25964544 | tf_op jit(solution)/shard_map/dot_general | solution.py:32
  260.6 8.4 %bitcast_convert_fusion = bf16[768,3072]{1,0:T(8,128)(2,1)S(1)} fusion(bf16[2,2,192,3072]{3,2,1,0:T(8,128)(2,1)} %get-tuple-element.82, f32[768]{0:T(1024)S(1)} %get-tuple-element.74, f32[2,2,192]{2,1,0:T(2,128)S(1)} %fusion.136, f32[2,2,192]{2,1,0:T(2,128)S(1)} %broadcast_multiply_fusion, f32[1,2,192,768]{3,2,1,0:T(8,128)S(1)} %copy-done.7, ...), kind=kOutput, calls=%fused_computation.3 | convolution fusion | flops 3629187072 | bytes 11805696 | tf_op jit(solution)/shard_map/dot_general | solution.py:47
  269.0 7.4 %fusion.22 = (f32[2,2,192]{2,1,0:T(2,128)S(1)}, bf16[2,2,192,768]{3,2,1,0:T(8,128)(2,1)}) fusion(f32[768]{0:T(1024)S(1)} %get-tuple-element.74, f32[2,2,192]{2,1,0:T(2,128)S(1)} %broadcast_multiply_fusion, f32[1,2,192,768]{3,2,1,0:T(8,128)S(1)} %copy-done.7, f32[1,2,192,768]{3,2,1,0:T(8,128)S(1)} %copy-done.10, ...), kind=kOutput, calls=%fused_computation.62 | convolution fusion | flops 3628006656 | bytes 12987392 | tf_op jit(solution)/shard_map/dot_general | solution.py:38
  305.4 10.3 %all-to-all-done.6 = bf16[8,2,24,768]{3,2,1,0:T(8,128)(2,1)} async-done(((bf16[8,2,24,768]{3,2,1,0:T(8,128)(2,1)}), bf16[8,2,24,768]{3,2,1,0:T(8,128)(2,1)}, u32[]{:S(2)}, u32[]{:S(2)}) %all-to-all-start.6) | async-done | bytes 589856 | tf_op jit(solution)/shard_map/all_to_all | solution.py:141
  350.5 5.5 convert_element_type.425
  356.1 6.7 convert_element_type.411
  368.3 6.6 convert_element_type.430
  374.9 5.0 fusion.54
  390.4 6.7 convert_element_type.433
  406.9 6.0 all-to-all-start.7
  413.8 14.2 %all-to-all-done.7 = bf16[8,2,24,768]{3,2,1,0:T(8,128)(2,1)S(1)} async-done(((bf16[8,2,24,768]{3,2,1,0:T(8,128)(2,1)}), bf16[8,2,24,768]{3,2,1,0:T(8,128)(2,1)S(1)}, u32[]{:S(2)}, u32[]{:S(2)}) %all-to-all-start.7) | async-done | bytes 589856 | tf_op jit(solution)/shard_map/all_to_all | solution.py:149
  486.9 9.1 %add_bitcast_fusion = f32[2,1,2,192,768]{4,3,2,1,0:T(8,128)} fusion(bf16[2,2,192,3072]{3,2,1,0:T(8,128)(2,1)} %copy-done.102, bf16[3072,768,1,1]{1,0,3,2:T(8,128)(2,1)} %bitcast.473, f32[1,2,192,768]{3,2,1,0:T(8,128)S(1)} %copy-done.8, f32[1,2,192,768]{3,2,1,0:T(8,128)S(1)} %copy-done.11), kind=kOutput, calls=%fused_computation.80 | convolution fusion | flops 3625058304 | bytes 14155776 | tf_op jit(solution)/shard_map/dot_general | solution.py:32
  497.6 5.8 collective-permute-done.2
  510.0 63.2 %reduce-scatter.4.cloned.1.call-done = bf16[48,3200]{1,0:T(8,128)(2,1)} async-done(((bf16[768,3200]{1,0:T(8,128)(2,1)}), bf16[48,3200]{1,0:T(8,128)(2,1)}) %reduce-scatter.4.cloned.1.call-update) | async-done | bytes 307216 | tf_op jit(solution)/shard_map/reduce_scatter | solution.py:232
  575.5 5.3 collective-permute-done
  583.0 104.3 %reduce-scatter.8.cloned.1.call-done = bf16[48,6144]{1,0:T(8,128)(2,1)} async-done(((bf16[768,6144]{1,0:T(8,128)(2,1)}), bf16[48,6144]{1,0:T(8,128)(2,1)}) %reduce-scatter.8.cloned.1.call-update) | async-done | bytes 589840 | tf_op jit(solution)/shard_map/reduce_scatter | solution.py:232
  688.9 13.4 %collective-permute-done.4 = bf16[48,6144]{1,0:T(8,128)(2,1)S(1)} collective-permute-done((bf16[48,6144]{1,0:T(8,128)(2,1)}, bf16[48,6144]{1,0:T(8,128)(2,1)S(1)}, u32[]{:S(2)}, u32[]{:S(2)}) %collective-permute-start.4) | collective-permute-done | bytes 589856 | tf_op jit(solution)/shard_map/ppermute | solution.py:210
  (444 shorter events, 281.8 us)
Async XLA Ops:
  7.2 60.4 %all-gather.4.cloned.1.call-start = ((), (), s32[]{:S(2)}) async-start(), calls=%async_computation.11 | async-start | bytes 5222400 | tf_op jit(solution)/shard_map/all_gather | solution.py:204
  9.9 126.1 %all-gather.6.cloned.1.call-start = ((), (), s32[]{:S(2)}) async-start(), calls=%async_computation.12 | async-start | bytes 5013504 | tf_op jit(solution)/shard_map/all_gather | solution.py:204
  12.6 224.1 %all-gather.8.cloned.1.call-start = ((), (), s32[]{:S(2)}) async-start(), calls=%async_computation.13 | async-start | bytes 10027008 | tf_op jit(solution)/shard_map/all_gather | solution.py:204
  13.9 63.4 %copy-start.86 = (f32[2,192]{1,0:T(2,128)}, f32[2,192]{1,0:T(2,128)S(1)}, u32[]{:S(2)}) copy-start(f32[2,192]{1,0:T(2,128)S(1)} %broadcast_multiply_fusion.4) | copy-start | bytes 4612
  13.9 60.1 %copy-start.88 = (f32[2,192]{1,0:T(2,128)}, f32[2,192]{1,0:T(2,128)S(1)}, u32[]{:S(2)}) copy-start(f32[2,192]{1,0:T(2,128)S(1)} %broadcast_multiply_fusion.2) | copy-start | bytes 4612
  14.4 59.6 %copy-start.90 = (f32[2,192]{1,0:T(2,128)}, f32[2,192]{1,0:T(2,128)S(1)}, u32[]{:S(2)}) copy-start(f32[2,192]{1,0:T(2,128)S(1)} %get-tuple-element.70) | copy-start | bytes 4612
  14.5 62.9 %copy-start.98 = (f32[2,192]{1,0:T(2,128)}, f32[2,192]{1,0:T(2,128)S(1)}, u32[]{:S(2)}) copy-start(f32[2,192]{1,0:T(2,128)S(1)} %fusion.137) | copy-start | bytes 4612
  104.8 27.5 %all-to-all-start.2 = ((bf16[8,2,24,768]{3,2,1,0:T(8,128)(2,1)}), bf16[8,2,24,768]{3,2,1,0:T(8,128)(2,1)S(1)}, u32[]{:S(2)}, u32[]{:S(2)}) async-start(bf16[8,2,24,768]{3,2,1,0:T(8,128)(2,1)} %bitcast.444), calls=%async_computation.2 | async-start | bytes 1179648 | tf_op jit(solution)/shard_map/all_to_all | solution.py:141
  132.3 30.6 %all-to-all-start = ((bf16[8,2,24,768]{3,2,1,0:T(8,128)(2,1)}), bf16[8,2,24,768]{3,2,1,0:T(8,128)(2,1)S(1)}, u32[]{:S(2)}, u32[]{:S(2)}) async-start(bf16[8,2,24,768]{3,2,1,0:T(8,128)(2,1)} %bitcast.445), calls=%async_computation | async-start | bytes 1179648 | tf_op jit(solution)/shard_map/all_to_all | solution.py:141
  162.9 31.3 %all-to-all-start.3 = ((bf16[8,2,24,768]{3,2,1,0:T(8,128)(2,1)}), bf16[8,2,24,768]{3,2,1,0:T(8,128)(2,1)}, u32[]{:S(2)}, u32[]{:S(2)}) async-start(bf16[8,2,24,768]{3,2,1,0:T(8,128)(2,1)} %convert_element_type.391), calls=%async_computation.3 | async-start | bytes 1179648 | tf_op jit(solution)/shard_map/all_to_all | solution.py:149
  194.2 35.4 %all-to-all-start.1 = ((bf16[8,2,24,768]{3,2,1,0:T(8,128)(2,1)}), bf16[8,2,24,768]{3,2,1,0:T(8,128)(2,1)}, u32[]{:S(2)}, u32[]{:S(2)}) async-start(bf16[8,2,24,768]{3,2,1,0:T(8,128)(2,1)} %convert_element_type.377), calls=%async_computation.1 | async-start | bytes 1179648 | tf_op jit(solution)/shard_map/all_to_all | solution.py:149
  295.2 20.5 %all-to-all-start.6 = ((bf16[8,2,24,768]{3,2,1,0:T(8,128)(2,1)}), bf16[8,2,24,768]{3,2,1,0:T(8,128)(2,1)}, u32[]{:S(2)}, u32[]{:S(2)}) async-start(bf16[8,2,24,768]{3,2,1,0:T(8,128)(2,1)} %bitcast.489), calls=%async_computation.6 | async-start | bytes 1179648 | tf_op jit(solution)/shard_map/all_to_all | solution.py:141
  315.7 19.7 %all-to-all-start.4 = ((bf16[8,2,24,768]{3,2,1,0:T(8,128)(2,1)}), bf16[8,2,24,768]{3,2,1,0:T(8,128)(2,1)S(1)}, u32[]{:S(2)}, u32[]{:S(2)}) async-start(bf16[8,2,24,768]{3,2,1,0:T(8,128)(2,1)} %bitcast.488), calls=%async_computation.4 | async-start | bytes 1179648 | tf_op jit(solution)/shard_map/all_to_all | solution.py:141
  379.9 27.1 %all-to-all-start.5 = ((bf16[8,2,24,768]{3,2,1,0:T(8,128)(2,1)}), bf16[8,2,24,768]{3,2,1,0:T(8,128)(2,1)S(1)}, u32[]{:S(2)}, u32[]{:S(2)}) async-start(bf16[8,2,24,768]{3,2,1,0:T(8,128)(2,1)} %bitcast.499), calls=%async_computation.5 | async-start | bytes 1179648 | tf_op jit(solution)/shard_map/all_to_all | solution.py:149
  406.9 21.0 %all-to-all-start.7 = ((bf16[8,2,24,768]{3,2,1,0:T(8,128)(2,1)}), bf16[8,2,24,768]{3,2,1,0:T(8,128)(2,1)S(1)}, u32[]{:S(2)}, u32[]{:S(2)}) async-start(bf16[8,2,24,768]{3,2,1,0:T(8,128)(2,1)} %bitcast.99), calls=%async_computation.7 | async-start | bytes 1179648 | tf_op jit(solution)/shard_map/all_to_all | solution.py:149
  412.9 83.1 %reduce-scatter.6.cloned.1.call-start = ((), (), s32[]{:S(2)}) async-start(), calls=%async_computation.15 | async-start | bytes 5013504 | tf_op jit(solution)/shard_map/reduce_scatter | solution.py:232
  413.5 159.7 %reduce-scatter.4.cloned.1.call-start = ((), (), s32[]{:S(2)}) async-start(), calls=%async_computation.14 | async-start | bytes 5222400 | tf_op jit(solution)/shard_map/reduce_scatter | solution.py:232
  485.3 202.0 %reduce-scatter.8.cloned.1.call-start = ((), (), s32[]{:S(2)}) async-start(), calls=%async_computation.16 | async-start | bytes 10027008 | tf_op jit(solution)/shard_map/reduce_scatter | solution.py:232
  496.1 7.4 %collective-permute-start.2 = (bf16[48,3072]{1,0:T(8,128)(2,1)}, bf16[48,3072]{1,0:T(8,128)(2,1)S(1)}, u32[]{:S(2)}, u32[]{:S(2)}) collective-permute-start(bf16[48,3072]{1,0:T(8,128)(2,1)} %reduce-scatter.6.cloned.1.call-done), channel_id=1, source_target_pairs={{0,16},{16,0},{1,17},{17,1},{2,18},{18,2},{3,19},{19,3},{4,20},{20... | collective-permute-start | bytes 884744 | tf_op jit(solution)/shard_map/ppermute | solution.py:210
  504.5 70.2 %collective-permute-start.3 = (bf16[48,3072]{1,0:T(8,128)(2,1)S(1)}, bf16[48,3072]{1,0:T(8,128)(2,1)S(1)}, u32[]{:S(2)}, u32[]{:S(2)}) collective-permute-start(bf16[48,3072]{1,0:T(8,128)(2,1)S(1)} %add.220), channel_id=1, source_target_pairs={{0,8},{8,0},{1,9},{9,1},{2,10},{10,2},{3,11},{11,3},{4,12},{12,4},... | collective-permute-start | bytes 884744 | tf_op jit(solution)/shard_map/ppermute | solution.py:216
  573.2 7.6 %collective-permute-start = (bf16[48,3200]{1,0:T(8,128)(2,1)}, bf16[48,3200]{1,0:T(8,128)(2,1)S(1)}, u32[]{:S(2)}, u32[]{:S(2)}) collective-permute-start(bf16[48,3200]{1,0:T(8,128)(2,1)} %reduce-scatter.4.cloned.1.call-done), channel_id=1, source_target_pairs={{0,16},{16,0},{1,17},{17,1},{2,18},{18,2},{3,19},{19,3},{4,20},{20... | collective-permute-start | bytes 921608 | tf_op jit(solution)/shard_map/ppermute | solution.py:210
  581.9 106.9 %collective-permute-start.1 = (bf16[48,3200]{1,0:T(8,128)(2,1)S(1)}, bf16[48,3200]{1,0:T(8,128)(2,1)S(1)}, u32[]{:S(2)}, u32[]{:S(2)}) collective-permute-start(bf16[48,3200]{1,0:T(8,128)(2,1)S(1)} %add.219), channel_id=1, source_target_pairs={{0,8},{8,0},{1,9},{9,1},{2,10},{10,2},{3,11},{11,3},{4,12},{12,4},... | collective-permute-start | bytes 921608 | tf_op jit(solution)/shard_map/ppermute | solution.py:216
  687.3 15.0 %collective-permute-start.4 = (bf16[48,6144]{1,0:T(8,128)(2,1)}, bf16[48,6144]{1,0:T(8,128)(2,1)S(1)}, u32[]{:S(2)}, u32[]{:S(2)}) collective-permute-start(bf16[48,6144]{1,0:T(8,128)(2,1)} %reduce-scatter.8.cloned.1.call-done), channel_id=1, source_target_pairs={{0,16},{16,0},{1,17},{17,1},{2,18},{18,2},{3,19},{19,3},{4,20},{20... | collective-permute-start | bytes 1769480 | tf_op jit(solution)/shard_map/ppermute | solution.py:210
  703.5 2.5 collective-permute-start.5
  (110 other events, 560.7 us)
Sparse Core Ops, SparseCore 0:
  10.8 56.8 all-gather.3
  70.5 61.9 all-gather.5
  135.3 101.1 all-gather.7
  417.3 77.0 reduce-scatter.5
  498.2 75.0 reduce-scatter.3
  577.2 110.0 reduce-scatter.7

commit v9 on v7

--- a/solution.py
+++ b/solution.py
@@ -332,14 +332,14 @@
         back_twos_placed.append(back_dot(back_join, t_in).astype(jnp.bfloat16))
     time_grads = (summed(time_in_terms), summed(time_out_terms))
     time_kinds = ("plain", "plain")
-    packed_time, s_in, s_out = lax.optimization_barrier(
-        (pack_group(time_grads, time_kinds, members, half), s_in, s_out)
+    packed_time, back_twos_placed[-1] = lax.optimization_barrier(
+        (pack_group(time_grads, time_kinds, members, half), back_twos_placed[-1])
     )
     grad_time = reduce_group(packed_time, time_grads, time_kinds, half)
 
     input_grads = []
     gain_one_terms = []
-    gain_zero_terms = []
+    back_ones = []
     space_out_terms = []
     space_in_terms = []
     for index in range(micro):
@@ -353,18 +353,16 @@
         back_context = back_dot(rounded, s_out).astype(jnp.bfloat16)
         back_join = attend_back(s["join_space"], s["total_space"], back_context, *spatial)
         space_in_terms.append(token_sum(s["normed_one"], back_join))
-        back_one = back_dot(back_join, s_in).astype(jnp.bfloat16)
-        back_mixed, gain_grad = norm_back(
-            s["frames_in"], gain_rows[0], back_one.astype(jnp.float32)
-        )
-        gain_zero_terms.append(gain_grad)
-        input_grads.append(upstream + back_mixed)
+        back_ones.append(back_dot(back_join, s_in).astype(jnp.bfloat16))
+        input_grads.append(upstream)
     grad_space_in = summed(space_in_terms)
     grad_space_out = summed(space_out_terms)
-    gain_grad_zero = summed(gain_zero_terms)
+    back_mixed, gain_grad_zero = norm_back(
+        inputs[:, 0].astype(jnp.float32), gain_rows[0], jnp.stack(back_ones).astype(jnp.float32)
+    )
     gain_grad_one = summed(gain_one_terms)
     gain_grad_two = summed(gain_two_terms)
-    input_grad = jnp.stack(input_grads)
+    input_grad = jnp.stack(input_grads) + back_mixed
 
     gain_grads = jnp.stack((gain_grad_zero, gain_grad_one, gain_grad_two))
     space_grads = (grad_space_in, grad_space_out, gain_grads)

time: 723 us -> 719 us (level)
  local copies, waits for them, and re-layouts: 122 us -> 111 us
  waiting for transfers between devices: 322 us -> 331 us
    all_to_all x4, waiting for transfers between devices: 25.8 us -> 36.7 us  [to_frames(): lax.all_to_all(blocks, 'fsdp', split_axis=0, concat_axis=0, tiled=True)]
    reduce_scatter x3, waiting for transfers between devices: 169 us -> 178 us  [reduce_group(): owned = lax.psum_scatter(packed, MEMBERS, scatter_dimension=0, tiled=True)]
    unnamed x258 -> x226, local copies, waits for them, and re-layouts: 23.5 us -> 18.5 us
  transfers between devices with their start and end apart: 20 -> 20, of which waited for: 13 -> 12; matrix products, arithmetic and copies ran while one was open for 32% -> 32% of each run, Pallas kernels for 0% -> 0%
where the time goes in v9:
time: 719 us; the launch traced here: 713 us
  waiting for transfers between devices  331 us (46%)
  matrix products  152 us (21%)
  local copies, waits for them, and re-layouts  111 us (15%)
  other arithmetic  58.3 us (8%)
  starting transfers between devices  44.6 us (6%)
  between operations  16.3 us (2%)
    reduce_scatter x3, waiting for transfers between devices, reduce_group(): owned = lax.psum_scatter(packed, MEMBERS, scatter_dimension=0, tiled=True)  178 us
    all_gather x3, waiting for transfers between devices, gather_group(): gathered = lax.all_gather(block, MEMBERS, axis=0, tiled=True)  54.5 us
    dot_general x10, matrix products, flat_dot(): product = jnp.dot(flat, right, preferred_element_type=jnp.float32)  46.3 us
    all_to_all x4, waiting for transfers between devices, to_places(): lax.all_to_all(blocks, 'fsdp', split_axis=0, concat_axis=0, tiled=True)  42.7 us
    all_to_all x4, waiting for transfers between devices, to_frames(): lax.all_to_all(blocks, 'fsdp', split_axis=0, concat_axis=0, tiled=True)  36.7 us
    convert_element_type x8, local copies, waits for them, and re-layouts, attend_back(): stacked.reshape(back_context.shape[:-1] + (3 * D,)).astype(jnp.bfloat16)  35.3 us
    dot_general x10, matrix products, back_dot(): lax.dot_general(flat, right, (((1,), (1,)), ((), ())), preferred_element_...  31.4 us
    dot_general x10, matrix products, token_sum(): lax.dot_general(left_rows, right_rows, (((0,), (0,)), ((), ())), preferre...  30.3 us
  transfers between devices with their start and end apart: 20, of which 12 were waited for; matrix products, arithmetic and copies ran while one was open for 32% of the time, Pallas kernels for 0%

profile of v9, /device:TPU:0, one launch (start us, length us, event | category | flops | bytes accessed | tf_op | source)
XLA Modules:
  0.0 712.9 jit_solution(17175316205239760921)
XLA Ops:
  14.5 53.1 %all-gather.4.cloned.1.call-done = bf16[768,3200]{1,0:T(8,128)(2,1)} async-done(((bf16[48,3200]{1,0:T(8,128)(2,1)}), bf16[768,3200]{1,0:T(8,128)(2,1)}) %all-gather.4.cloned.1.call-update) | async-done | bytes 4915216 | tf_op jit(solution)/shard_map/all_gather | solution.py:204
  103.7 26.7 %all-to-all-done.2 = bf16[8,2,24,768]{3,2,1,0:T(8,128)(2,1)S(1)} async-done(((bf16[8,2,24,768]{3,2,1,0:T(8,128)(2,1)}), bf16[8,2,24,768]{3,2,1,0:T(8,128)(2,1)S(1)}, u32[]{:S(2)}, u32[]{:S(2)}) %all-to-all-start.2) | async-done | bytes 589856 | tf_op jit(solution)/shard_map/all_to_all | solution.py:141
  155.1 5.2 all-to-all-done
  169.5 6.4 reshape.625
  187.7 6.2 all-to-all-start.1
  204.3 22.6 %all-to-all-done.1 = bf16[8,2,24,768]{3,2,1,0:T(8,128)(2,1)} async-done(((bf16[8,2,24,768]{3,2,1,0:T(8,128)(2,1)}), bf16[8,2,24,768]{3,2,1,0:T(8,128)(2,1)}, u32[]{:S(2)}, u32[]{:S(2)}) %all-to-all-start.1) | async-done | bytes 589856 | tf_op jit(solution)/shard_map/all_to_all | solution.py:149
  239.5 6.7 fusion.2
  247.9 11.4 %add_convert_fusion = (bf16[2,2,192,3072]{3,2,1,0:T(8,128)(2,1)}, bf16[2,2,192,3072]{3,2,1,0:T(8,128)(2,1)S(1)}) fusion(f32[2,2,192,3072]{3,2,1,0:T(8,128)} %bitcast.535, bf16[768,6144]{1,0:T(8,128)(2,1)S(1)} %bitcast.487, f32[768]{0:T(1024)S(1)} %get-tuple-element.78, f32[2,2,192]{2,1,0:T(2,128)S(1)} %add_rsqrt_fusion, ...), kind=kOutput, calls=%fused_computation.4 | convolution fusion | flops 3662217216 | bytes 25964544 | tf_op jit(solution)/shard_map/dot_general | solution.py:32
  259.3 8.5 %bitcast_convert_fusion = bf16[768,3072]{1,0:T(8,128)(2,1)S(1)} fusion(bf16[2,2,192,3072]{3,2,1,0:T(8,128)(2,1)} %get-tuple-element.88, f32[768]{0:T(1024)S(1)} %get-tuple-element.78, f32[2,2,192]{2,1,0:T(2,128)S(1)} %add_rsqrt_fusion, f32[2,2,192]{2,1,0:T(2,128)S(1)} %broadcast_multiply_fusion.1, f32[1,2,192,768]{3,2,1,0:T(8,128)S(1)} %bitcast.469, ...), kind=kOutput, calls=%fused_computation.3 | convolution fusion | flops 3629187072 | bytes 11805696 | tf_op jit(solution)/shard_map/dot_general | solution.py:47
  267.7 6.3 fusion.41
  302.8 10.8 %all-to-all-done.4 = bf16[8,2,24,768]{3,2,1,0:T(8,128)(2,1)} async-done(((bf16[8,2,24,768]{3,2,1,0:T(8,128)(2,1)}), bf16[8,2,24,768]{3,2,1,0:T(8,128)(2,1)}, u32[]{:S(2)}, u32[]{:S(2)}) %all-to-all-start.4) | async-done | bytes 589856 | tf_op jit(solution)/shard_map/all_to_all | solution.py:141
  335.0 6.6 convert_element_type.437
  341.5 6.6 convert_element_type.444
  363.3 6.2 all-to-all-start.5
  375.0 6.7 convert_element_type.451
  387.7 6.7 convert_element_type.454
  404.3 6.0 all-to-all-start.7
  411.4 14.0 %all-to-all-done.7 = bf16[8,2,24,768]{3,2,1,0:T(8,128)(2,1)} async-done(((bf16[8,2,24,768]{3,2,1,0:T(8,128)(2,1)}), bf16[8,2,24,768]{3,2,1,0:T(8,128)(2,1)}, u32[]{:S(2)}, u32[]{:S(2)}) %all-to-all-start.7) | async-done | bytes 589856 | tf_op jit(solution)/shard_map/all_to_all | solution.py:149
  484.1 7.5 %reduce-scatter.6.cloned.1.call-done = bf16[48,3072]{1,0:T(8,128)(2,1)} async-done(((bf16[768,3072]{1,0:T(8,128)(2,1)}), bf16[48,3072]{1,0:T(8,128)(2,1)}) %reduce-scatter.6.cloned.1.call-update) | async-done | bytes 294928 | tf_op jit(solution)/shard_map/reduce_scatter | solution.py:232
  493.2 9.4 %add_bitcast_fusion = f32[2,1,2,192,768]{4,3,2,1,0:T(8,128)} fusion(bf16[2,2,192,3072]{3,2,1,0:T(8,128)(2,1)} %copy-done.100, bf16[3072,768,1,1]{1,0,3,2:T(8,128)(2,1)} %bitcast.505, f32[1,2,192,768]{3,2,1,0:T(8,128)S(1)} %bitcast.470, f32[1,2,192,768]{3,2,1,0:T(8,128)} %bitcast.473), kind=kOutput, calls=%fused_computation.92 | convolution fusion | flops 3625058304 | bytes 14155776 | tf_op jit(solution)/shard_map/dot_general | solution.py:32
  504.7 66.0 %reduce-scatter.4.cloned.1.call-done = bf16[48,3200]{1,0:T(8,128)(2,1)} async-done(((bf16[768,3200]{1,0:T(8,128)(2,1)}), bf16[48,3200]{1,0:T(8,128)(2,1)}) %reduce-scatter.4.cloned.1.call-update) | async-done | bytes 307216 | tf_op jit(solution)/shard_map/reduce_scatter | solution.py:232
  573.0 5.6 collective-permute-done
  580.8 104.0 %reduce-scatter.8.cloned.1.call-done = bf16[48,6144]{1,0:T(8,128)(2,1)} async-done(((bf16[768,6144]{1,0:T(8,128)(2,1)}), bf16[48,6144]{1,0:T(8,128)(2,1)}) %reduce-scatter.8.cloned.1.call-update) | async-done | bytes 589840 | tf_op jit(solution)/shard_map/reduce_scatter | solution.py:232
  686.3 13.4 %collective-permute-done.4 = bf16[48,6144]{1,0:T(8,128)(2,1)S(1)} collective-permute-done((bf16[48,6144]{1,0:T(8,128)(2,1)}, bf16[48,6144]{1,0:T(8,128)(2,1)S(1)}, u32[]{:S(2)}, u32[]{:S(2)}) %collective-permute-start.4) | collective-permute-done | bytes 589856 | tf_op jit(solution)/shard_map/ppermute | solution.py:210
  (445 shorter events, 273.8 us)
Async XLA Ops:
  7.2 60.4 %all-gather.4.cloned.1.call-start = ((), (), s32[]{:S(2)}) async-start(), calls=%async_computation.11 | async-start | bytes 5222400 | tf_op jit(solution)/shard_map/all_gather | solution.py:204
  9.9 125.3 %all-gather.6.cloned.1.call-start = ((), (), s32[]{:S(2)}) async-start(), calls=%async_computation.12 | async-start | bytes 5013504 | tf_op jit(solution)/shard_map/all_gather | solution.py:204
  12.6 222.8 %all-gather.8.cloned.1.call-start = ((), (), s32[]{:S(2)}) async-start(), calls=%async_computation.13 | async-start | bytes 10027008 | tf_op jit(solution)/shard_map/all_gather | solution.py:204
  13.9 61.7 %copy-start.94 = (f32[2,192]{1,0:T(2,128)}, f32[2,192]{1,0:T(2,128)S(1)}, u32[]{:S(2)}) copy-start(f32[2,192]{1,0:T(2,128)S(1)} %broadcast_multiply_fusion.7) | copy-start | bytes 4612
  14.0 58.9 %copy-start.92 = (f32[2,192]{1,0:T(2,128)}, f32[2,192]{1,0:T(2,128)S(1)}, u32[]{:S(2)}) copy-start(f32[2,192]{1,0:T(2,128)S(1)} %broadcast_multiply_fusion.5) | copy-start | bytes 4612
  14.5 58.4 %copy-start.96 = (f32[2,192]{1,0:T(2,128)}, f32[2,192]{1,0:T(2,128)S(1)}, u32[]{:S(2)}) copy-start(f32[2,192]{1,0:T(2,128)S(1)} %add_rsqrt_fusion.1) | copy-start | bytes 4612
  14.5 61.1 %copy-start.98 = (f32[2,192]{1,0:T(2,128)}, f32[2,192]{1,0:T(2,128)S(1)}, u32[]{:S(2)}) copy-start(f32[2,192]{1,0:T(2,128)S(1)} %add_rsqrt_fusion.2) | copy-start | bytes 4612
  99.2 31.1 %all-to-all-start.2 = ((bf16[8,2,24,768]{3,2,1,0:T(8,128)(2,1)}), bf16[8,2,24,768]{3,2,1,0:T(8,128)(2,1)S(1)}, u32[]{:S(2)}, u32[]{:S(2)}) async-start(bf16[8,2,24,768]{3,2,1,0:T(8,128)(2,1)} %bitcast.460), calls=%async_computation.2 | async-start | bytes 1179648 | tf_op jit(solution)/shard_map/all_to_all | solution.py:141
  130.4 30.0 %all-to-all-start = ((bf16[8,2,24,768]{3,2,1,0:T(8,128)(2,1)}), bf16[8,2,24,768]{3,2,1,0:T(8,128)(2,1)S(1)}, u32[]{:S(2)}, u32[]{:S(2)}) async-start(bf16[8,2,24,768]{3,2,1,0:T(8,128)(2,1)} %bitcast.461), calls=%async_computation | async-start | bytes 1179648 | tf_op jit(solution)/shard_map/all_to_all | solution.py:141
  160.3 27.3 %all-to-all-start.3 = ((bf16[8,2,24,768]{3,2,1,0:T(8,128)(2,1)}), bf16[8,2,24,768]{3,2,1,0:T(8,128)(2,1)}, u32[]{:S(2)}, u32[]{:S(2)}) async-start(bf16[8,2,24,768]{3,2,1,0:T(8,128)(2,1)} %convert_element_type.417), calls=%async_computation.3 | async-start | bytes 1179648 | tf_op jit(solution)/shard_map/all_to_all | solution.py:149
  187.7 39.2 %all-to-all-start.1 = ((bf16[8,2,24,768]{3,2,1,0:T(8,128)(2,1)}), bf16[8,2,24,768]{3,2,1,0:T(8,128)(2,1)}, u32[]{:S(2)}, u32[]{:S(2)}) async-start(bf16[8,2,24,768]{3,2,1,0:T(8,128)(2,1)} %convert_element_type.403), calls=%async_computation.1 | async-start | bytes 1179648 | tf_op jit(solution)/shard_map/all_to_all | solution.py:149
  292.7 20.8 %all-to-all-start.4 = ((bf16[8,2,24,768]{3,2,1,0:T(8,128)(2,1)}), bf16[8,2,24,768]{3,2,1,0:T(8,128)(2,1)}, u32[]{:S(2)}, u32[]{:S(2)}) async-start(bf16[8,2,24,768]{3,2,1,0:T(8,128)(2,1)} %bitcast.522), calls=%async_computation.4 | async-start | bytes 1179648 | tf_op jit(solution)/shard_map/all_to_all | solution.py:141
  313.5 34.6 %all-to-all-start.6 = ((bf16[8,2,24,768]{3,2,1,0:T(8,128)(2,1)}), bf16[8,2,24,768]{3,2,1,0:T(8,128)(2,1)S(1)}, u32[]{:S(2)}, u32[]{:S(2)}) async-start(bf16[8,2,24,768]{3,2,1,0:T(8,128)(2,1)} %bitcast.521), calls=%async_computation.6 | async-start | bytes 1179648 | tf_op jit(solution)/shard_map/all_to_all | solution.py:141
  363.3 41.0 %all-to-all-start.5 = ((bf16[8,2,24,768]{3,2,1,0:T(8,128)(2,1)}), bf16[8,2,24,768]{3,2,1,0:T(8,128)(2,1)S(1)}, u32[]{:S(2)}, u32[]{:S(2)}) async-start(bf16[8,2,24,768]{3,2,1,0:T(8,128)(2,1)} %bitcast.529), calls=%async_computation.5 | async-start | bytes 1179648 | tf_op jit(solution)/shard_map/all_to_all | solution.py:149
  404.3 21.1 %all-to-all-start.7 = ((bf16[8,2,24,768]{3,2,1,0:T(8,128)(2,1)}), bf16[8,2,24,768]{3,2,1,0:T(8,128)(2,1)}, u32[]{:S(2)}, u32[]{:S(2)}) async-start(bf16[8,2,24,768]{3,2,1,0:T(8,128)(2,1)} %bitcast.90), calls=%async_computation.7 | async-start | bytes 1179648 | tf_op jit(solution)/shard_map/all_to_all | solution.py:149
  410.3 81.4 %reduce-scatter.6.cloned.1.call-start = ((), (), s32[]{:S(2)}) async-start(), calls=%async_computation.15 | async-start | bytes 5013504 | tf_op jit(solution)/shard_map/reduce_scatter | solution.py:232
  410.9 159.9 %reduce-scatter.4.cloned.1.call-start = ((), (), s32[]{:S(2)}) async-start(), calls=%async_computation.14 | async-start | bytes 5222400 | tf_op jit(solution)/shard_map/reduce_scatter | solution.py:232
  483.5 201.2 %reduce-scatter.8.cloned.1.call-start = ((), (), s32[]{:S(2)}) async-start(), calls=%async_computation.16 | async-start | bytes 10027008 | tf_op jit(solution)/shard_map/reduce_scatter | solution.py:232
  491.7 10.9 %collective-permute-start.2 = (bf16[48,3072]{1,0:T(8,128)(2,1)}, bf16[48,3072]{1,0:T(8,128)(2,1)S(1)}, u32[]{:S(2)}, u32[]{:S(2)}) collective-permute-start(bf16[48,3072]{1,0:T(8,128)(2,1)} %reduce-scatter.6.cloned.1.call-done), channel_id=1, source_target_pairs={{0,16},{16,0},{1,17},{17,1},{2,18},{18,2},{3,19},{19,3},{4,20},{20... | collective-permute-start | bytes 884744 | tf_op jit(solution)/shard_map/ppermute | solution.py:210
  502.7 69.6 %collective-permute-start.3 = (bf16[48,3072]{1,0:T(8,128)(2,1)S(1)}, bf16[48,3072]{1,0:T(8,128)(2,1)S(1)}, u32[]{:S(2)}, u32[]{:S(2)}) collective-permute-start(bf16[48,3072]{1,0:T(8,128)(2,1)S(1)} %add.245), channel_id=1, source_target_pairs={{0,8},{8,0},{1,9},{9,1},{2,10},{10,2},{3,11},{11,3},{4,12},{12,4},... | collective-permute-start | bytes 884744 | tf_op jit(solution)/shard_map/ppermute | solution.py:216
  570.8 7.9 %collective-permute-start = (bf16[48,3200]{1,0:T(8,128)(2,1)}, bf16[48,3200]{1,0:T(8,128)(2,1)S(1)}, u32[]{:S(2)}, u32[]{:S(2)}) collective-permute-start(bf16[48,3200]{1,0:T(8,128)(2,1)} %reduce-scatter.4.cloned.1.call-done), channel_id=1, source_target_pairs={{0,16},{16,0},{1,17},{17,1},{2,18},{18,2},{3,19},{19,3},{4,20},{20... | collective-permute-start | bytes 921608 | tf_op jit(solution)/shard_map/ppermute | solution.py:210
  579.7 106.5 %collective-permute-start.1 = (bf16[48,3200]{1,0:T(8,128)(2,1)S(1)}, bf16[48,3200]{1,0:T(8,128)(2,1)S(1)}, u32[]{:S(2)}, u32[]{:S(2)}) collective-permute-start(bf16[48,3200]{1,0:T(8,128)(2,1)S(1)} %add.244), channel_id=1, source_target_pairs={{0,8},{8,0},{1,9},{9,1},{2,10},{10,2},{3,11},{11,3},{4,12},{12,4},... | collective-permute-start | bytes 921608 | tf_op jit(solution)/shard_map/ppermute | solution.py:216
  684.8 15.0 %collective-permute-start.4 = (bf16[48,6144]{1,0:T(8,128)(2,1)}, bf16[48,6144]{1,0:T(8,128)(2,1)S(1)}, u32[]{:S(2)}, u32[]{:S(2)}) collective-permute-start(bf16[48,6144]{1,0:T(8,128)(2,1)} %reduce-scatter.8.cloned.1.call-done), channel_id=1, source_target_pairs={{0,16},{16,0},{1,17},{17,1},{2,18},{18,2},{3,19},{19,3},{4,20},{20... | collective-permute-start | bytes 1769480 | tf_op jit(solution)/shard_map/ppermute | solution.py:210
  700.9 2.5 collective-permute-start.5
  (107 other events, 429.9 us)
Sparse Core Ops, SparseCore 0:
  10.8 56.8 all-gather.3
  70.5 62.2 all-gather.5
  135.1 100.3 all-gather.7
  414.7 76.9 reduce-scatter.5
  495.5 75.2 reduce-scatter.3
  574.7 110.0 reduce-scatter.7

commit v10 on v7

--- a/solution.py
+++ b/solution.py
@@ -288,6 +288,11 @@
     activated = gelu(hidden).astype(jnp.bfloat16)
     result = mixed_two + flat_dot(activated, h_out)
 
+    def pooled(pairs):
+        lefts = [left.reshape(-1, left.shape[-1]) for left, _ in pairs]
+        rights = [right.reshape(-1, right.shape[-1]) for _, right in pairs]
+        return token_sum(jnp.concatenate(lefts, axis=0), jnp.concatenate(rights, axis=0))
+
     def summed(terms):
         total = terms[0]
         for term in terms[1:]:
@@ -324,16 +329,16 @@
         upstream = upstreams[index] + back_mixed
         upstreams[index] = upstream
         rounded = upstream.astype(jnp.bfloat16)
-        time_out_terms.append(token_sum(s["context_time"], rounded))
+        time_out_terms.append((s["context_time"], rounded))
         back_context = back_dot(rounded, t_out).astype(jnp.bfloat16)
         back_placed = to_places(back_context)
         back_join = attend_back(s["join_time"], s["total_time"], back_placed, *temporal)
-        time_in_terms.append(token_sum(s["placed"], back_join))
+        time_in_terms.append((s["placed"], back_join))
         back_twos_placed.append(back_dot(back_join, t_in).astype(jnp.bfloat16))
-    time_grads = (summed(time_in_terms), summed(time_out_terms))
+    time_grads = (pooled(time_in_terms), pooled(time_out_terms))
     time_kinds = ("plain", "plain")
-    packed_time, s_in, s_out = lax.optimization_barrier(
-        (pack_group(time_grads, time_kinds, members, half), s_in, s_out)
+    packed_time, back_twos_placed[-1] = lax.optimization_barrier(
+        (pack_group(time_grads, time_kinds, members, half), back_twos_placed[-1])
     )
     grad_time = reduce_group(packed_time, time_grads, time_kinds, half)
 

time: 723 us -> 720 us (level)
    all_to_all x4, waiting for transfers between devices: 25.8 us -> 37.5 us  [to_frames(): lax.all_to_all(blocks, 'fsdp', split_axis=0, concat_axis=0, tiled=True)]
    dot_general x10 -> x8, matrix products: 34.9 us -> 28.7 us  [token_sum(): lax.dot_general(left_rows, right_rows, (((0,), (0,)), ((), ())), preferre...]
    unnamed x258 -> x246, local copies, waits for them, and re-layouts: 23.5 us -> 22 us
  transfers between devices with their start and end apart: 20 -> 20, of which waited for: 13 -> 13; matrix products, arithmetic and copies ran while one was open for 32% -> 30% of each run, Pallas kernels for 0% -> 0%
where the time goes in v10:
time: 720 us; the launch traced here: 714 us
  waiting for transfers between devices  329 us (46%)
  matrix products  155 us (22%)
  local copies, waits for them, and re-layouts  115 us (16%)
  other arithmetic  56.5 us (8%)
  starting transfers between devices  42.8 us (6%)
  between operations  16.3 us (2%)
    reduce_scatter x3, waiting for transfers between devices, reduce_group(): owned = lax.psum_scatter(packed, MEMBERS, scatter_dimension=0, tiled=True)  164 us
    all_gather x3, waiting for transfers between devices, gather_group(): gathered = lax.all_gather(block, MEMBERS, axis=0, tiled=True)  55.6 us
    dot_general x10, matrix products, flat_dot(): product = jnp.dot(flat, right, preferred_element_type=jnp.float32)  47.1 us
    all_to_all x4, waiting for transfers between devices, to_places(): lax.all_to_all(blocks, 'fsdp', split_axis=0, concat_axis=0, tiled=True)  44.9 us
    all_to_all x4, waiting for transfers between devices, to_frames(): lax.all_to_all(blocks, 'fsdp', split_axis=0, concat_axis=0, tiled=True)  37.5 us
    dot_general x10, matrix products, back_dot(): lax.dot_general(flat, right, (((1,), (1,)), ((), ())), preferred_element_...  35.4 us
    convert_element_type x8, local copies, waits for them, and re-layouts, attend_back(): stacked.reshape(back_context.shape[:-1] + (3 * D,)).astype(jnp.bfloat16)  34 us
    dot_general x8, matrix products, token_sum(): lax.dot_general(left_rows, right_rows, (((0,), (0,)), ((), ())), preferre...  28.7 us
  transfers between devices with their start and end apart: 20, of which 13 were waited for; matrix products, arithmetic and copies ran while one was open for 30% of the time, Pallas kernels for 0%

profile of v10, /device:TPU:0, one launch (start us, length us, event | category | flops | bytes accessed | tf_op | source)
XLA Modules:
  0.0 714.0 jit_solution(2732250735877437045)
XLA Ops:
  12.7 54.9 %all-gather.4.cloned.1.call-done = bf16[768,3200]{1,0:T(8,128)(2,1)} async-done(((bf16[48,3200]{1,0:T(8,128)(2,1)}), bf16[768,3200]{1,0:T(8,128)(2,1)}) %all-gather.4.cloned.1.call-update) | async-done | bytes 4915216 | tf_op jit(solution)/shard_map/all_gather | solution.py:204
  102.9 27.5 %all-to-all-done.2 = bf16[8,2,24,768]{3,2,1,0:T(8,128)(2,1)S(1)} async-done(((bf16[8,2,24,768]{3,2,1,0:T(8,128)(2,1)}), bf16[8,2,24,768]{3,2,1,0:T(8,128)(2,1)S(1)}, u32[]{:S(2)}, u32[]{:S(2)}) %all-to-all-start.2) | async-done | bytes 589856 | tf_op jit(solution)/shard_map/all_to_all | solution.py:141
  169.8 6.4 reshape.585
  188.4 6.4 all-to-all-start.1
  204.2 23.4 %all-to-all-done.1 = bf16[8,2,24,768]{3,2,1,0:T(8,128)(2,1)} async-done(((bf16[8,2,24,768]{3,2,1,0:T(8,128)(2,1)}), bf16[8,2,24,768]{3,2,1,0:T(8,128)(2,1)}, u32[]{:S(2)}, u32[]{:S(2)}) %all-to-all-start.1) | async-done | bytes 589856 | tf_op jit(solution)/shard_map/all_to_all | solution.py:149
  239.6 6.7 fusion.2
  248.0 11.3 %add_convert_fusion = (bf16[2,2,192,3072]{3,2,1,0:T(8,128)(2,1)}, bf16[2,2,192,3072]{3,2,1,0:T(8,128)(2,1)S(1)}) fusion(f32[2,2,192,3072]{3,2,1,0:T(8,128)} %bitcast.519, bf16[768,6144]{1,0:T(8,128)(2,1)S(1)} %bitcast.476, f32[768]{0:T(1024)S(1)} %get-tuple-element.82, f32[2,2,192]{2,1,0:T(2,128)S(1)} %add_rsqrt_fusion, ...), kind=kOutput, calls=%fused_computation.4 | convolution fusion | flops 3662217216 | bytes 25964544 | tf_op jit(solution)/shard_map/dot_general | solution.py:32
  259.3 8.4 %bitcast_convert_fusion = bf16[768,3072]{1,0:T(8,128)(2,1)S(1)} fusion(bf16[2,2,192,3072]{3,2,1,0:T(8,128)(2,1)} %get-tuple-element.92, f32[768]{0:T(1024)S(1)} %get-tuple-element.82, f32[2,2,192]{2,1,0:T(2,128)S(1)} %add_rsqrt_fusion, f32[2,2,192]{2,1,0:T(2,128)S(1)} %broadcast_multiply_fusion, f32[1,2,192,768]{3,2,1,0:T(8,128)S(1)} %bitcast.458, ...), kind=kOutput, calls=%fused_computation.3 | convolution fusion | flops 3629187072 | bytes 11805696 | tf_op jit(solution)/shard_map/dot_general | solution.py:47
  267.8 6.3 fusion.30
  301.5 11.3 %all-to-all-done.4 = bf16[8,2,24,768]{3,2,1,0:T(8,128)(2,1)} async-done(((bf16[8,2,24,768]{3,2,1,0:T(8,128)(2,1)}), bf16[8,2,24,768]{3,2,1,0:T(8,128)(2,1)}, u32[]{:S(2)}, u32[]{:S(2)}) %all-to-all-start.4) | async-done | bytes 589856 | tf_op jit(solution)/shard_map/all_to_all | solution.py:141
  349.4 6.6 convert_element_type.412
  355.9 6.6 convert_element_type.428
  367.4 5.5 all-to-all-start.5
  378.4 6.7 convert_element_type.435
  385.1 6.4 convolution_convert_fusion
  391.5 5.5 convert_element_type.438
  406.6 6.0 all-to-all-start.7
  413.6 14.1 %all-to-all-done.7 = bf16[8,2,24,768]{3,2,1,0:T(8,128)(2,1)S(1)} async-done(((bf16[8,2,24,768]{3,2,1,0:T(8,128)(2,1)}), bf16[8,2,24,768]{3,2,1,0:T(8,128)(2,1)S(1)}, u32[]{:S(2)}, u32[]{:S(2)}) %all-to-all-start.7) | async-done | bytes 589856 | tf_op jit(solution)/shard_map/all_to_all | solution.py:149
  490.2 9.1 %add_bitcast_fusion = f32[2,1,2,192,768]{4,3,2,1,0:T(8,128)} fusion(bf16[2,2,192,3072]{3,2,1,0:T(8,128)(2,1)} %copy-done.110, bf16[3072,768,1,1]{1,0,3,2:T(8,128)(2,1)} %bitcast.484, f32[1,2,192,768]{3,2,1,0:T(8,128)S(1)} %bitcast.459, f32[1,2,192,768]{3,2,1,0:T(8,128)S(1)} %bitcast.464), kind=kOutput, calls=%fused_computation.74 | convolution fusion | flops 3625058304 | bytes 14155776 | tf_op jit(solution)/shard_map/dot_general | solution.py:32
  500.8 6.6 collective-permute-done.2
  513.9 59.0 %reduce-scatter.4.cloned.1.call-done = bf16[48,3200]{1,0:T(8,128)(2,1)} async-done(((bf16[768,3200]{1,0:T(8,128)(2,1)}), bf16[48,3200]{1,0:T(8,128)(2,1)}) %reduce-scatter.4.cloned.1.call-update) | async-done | bytes 307216 | tf_op jit(solution)/shard_map/reduce_scatter | solution.py:232
  575.2 5.6 collective-permute-done
  581.9 105.0 %reduce-scatter.8.cloned.1.call-done = bf16[48,6144]{1,0:T(8,128)(2,1)} async-done(((bf16[768,6144]{1,0:T(8,128)(2,1)}), bf16[48,6144]{1,0:T(8,128)(2,1)}) %reduce-scatter.8.cloned.1.call-update) | async-done | bytes 589840 | tf_op jit(solution)/shard_map/reduce_scatter | solution.py:232
  688.5 13.4 %collective-permute-done.4 = bf16[48,6144]{1,0:T(8,128)(2,1)S(1)} collective-permute-done((bf16[48,6144]{1,0:T(8,128)(2,1)}, bf16[48,6144]{1,0:T(8,128)(2,1)S(1)}, u32[]{:S(2)}, u32[]{:S(2)}) %collective-permute-start.4) | collective-permute-done | bytes 589856 | tf_op jit(solution)/shard_map/ppermute | solution.py:210
  (464 shorter events, 278.9 us)
Async XLA Ops:
  7.2 60.4 %all-gather.4.cloned.1.call-start = ((), (), s32[]{:S(2)}) async-start(), calls=%async_computation.11 | async-start | bytes 5222400 | tf_op jit(solution)/shard_map/all_gather | solution.py:204
  9.9 124.9 %all-gather.6.cloned.1.call-start = ((), (), s32[]{:S(2)}) async-start(), calls=%async_computation.12 | async-start | bytes 5013504 | tf_op jit(solution)/shard_map/all_gather | solution.py:204
  10.8 224.7 %all-gather.8.cloned.1.call-start = ((), (), s32[]{:S(2)}) async-start(), calls=%async_computation.13 | async-start | bytes 10027008 | tf_op jit(solution)/shard_map/all_gather | solution.py:204
  12.2 63.6 %copy-start.94 = (f32[2,192]{1,0:T(2,128)}, f32[2,192]{1,0:T(2,128)S(1)}, u32[]{:S(2)}) copy-start(f32[2,192]{1,0:T(2,128)S(1)} %broadcast_multiply_fusion.6) | copy-start | bytes 4612
  12.2 60.7 %copy-start.96 = (f32[2,192]{1,0:T(2,128)}, f32[2,192]{1,0:T(2,128)S(1)}, u32[]{:S(2)}) copy-start(f32[2,192]{1,0:T(2,128)S(1)} %broadcast_multiply_fusion.4) | copy-start | bytes 4612
  12.7 60.2 %copy-start.100 = (f32[2,192]{1,0:T(2,128)}, f32[2,192]{1,0:T(2,128)S(1)}, u32[]{:S(2)}) copy-start(f32[2,192]{1,0:T(2,128)S(1)} %get-tuple-element.77) | copy-start | bytes 4612
  12.7 63.1 %copy-start.108 = (f32[2,192]{1,0:T(2,128)}, f32[2,192]{1,0:T(2,128)S(1)}, u32[]{:S(2)}) copy-start(f32[2,192]{1,0:T(2,128)S(1)} %fusion.153) | copy-start | bytes 4612
  98.5 32.0 %all-to-all-start.2 = ((bf16[8,2,24,768]{3,2,1,0:T(8,128)(2,1)}), bf16[8,2,24,768]{3,2,1,0:T(8,128)(2,1)S(1)}, u32[]{:S(2)}, u32[]{:S(2)}) async-start(bf16[8,2,24,768]{3,2,1,0:T(8,128)(2,1)} %bitcast.449), calls=%async_computation.2 | async-start | bytes 1179648 | tf_op jit(solution)/shard_map/all_to_all | solution.py:141
  130.5 29.5 %all-to-all-start = ((bf16[8,2,24,768]{3,2,1,0:T(8,128)(2,1)}), bf16[8,2,24,768]{3,2,1,0:T(8,128)(2,1)S(1)}, u32[]{:S(2)}, u32[]{:S(2)}) async-start(bf16[8,2,24,768]{3,2,1,0:T(8,128)(2,1)} %bitcast.450), calls=%async_computation | async-start | bytes 1179648 | tf_op jit(solution)/shard_map/all_to_all | solution.py:141
  160.8 27.6 %all-to-all-start.3 = ((bf16[8,2,24,768]{3,2,1,0:T(8,128)(2,1)}), bf16[8,2,24,768]{3,2,1,0:T(8,128)(2,1)S(1)}, u32[]{:S(2)}, u32[]{:S(2)}) async-start(bf16[8,2,24,768]{3,2,1,0:T(8,128)(2,1)} %convert_element_type.392), calls=%async_computation.3 | async-start | bytes 1179648 | tf_op jit(solution)/shard_map/all_to_all | solution.py:149
  188.4 39.2 %all-to-all-start.1 = ((bf16[8,2,24,768]{3,2,1,0:T(8,128)(2,1)}), bf16[8,2,24,768]{3,2,1,0:T(8,128)(2,1)}, u32[]{:S(2)}, u32[]{:S(2)}) async-start(bf16[8,2,24,768]{3,2,1,0:T(8,128)(2,1)} %convert_element_type.378), calls=%async_computation.1 | async-start | bytes 1179648 | tf_op jit(solution)/shard_map/all_to_all | solution.py:149
  291.9 20.8 %all-to-all-start.4 = ((bf16[8,2,24,768]{3,2,1,0:T(8,128)(2,1)}), bf16[8,2,24,768]{3,2,1,0:T(8,128)(2,1)}, u32[]{:S(2)}, u32[]{:S(2)}) async-start(bf16[8,2,24,768]{3,2,1,0:T(8,128)(2,1)} %bitcast.500), calls=%async_computation.4 | async-start | bytes 1179648 | tf_op jit(solution)/shard_map/all_to_all | solution.py:141
  312.8 19.7 %all-to-all-start.6 = ((bf16[8,2,24,768]{3,2,1,0:T(8,128)(2,1)}), bf16[8,2,24,768]{3,2,1,0:T(8,128)(2,1)S(1)}, u32[]{:S(2)}, u32[]{:S(2)}) async-start(bf16[8,2,24,768]{3,2,1,0:T(8,128)(2,1)} %bitcast.499), calls=%async_computation.6 | async-start | bytes 1179648 | tf_op jit(solution)/shard_map/all_to_all | solution.py:141
  367.4 39.2 %all-to-all-start.5 = ((bf16[8,2,24,768]{3,2,1,0:T(8,128)(2,1)}), bf16[8,2,24,768]{3,2,1,0:T(8,128)(2,1)S(1)}, u32[]{:S(2)}, u32[]{:S(2)}) async-start(bf16[8,2,24,768]{3,2,1,0:T(8,128)(2,1)} %bitcast.513), calls=%async_computation.5 | async-start | bytes 1179648 | tf_op jit(solution)/shard_map/all_to_all | solution.py:149
  406.6 21.0 %all-to-all-start.7 = ((bf16[8,2,24,768]{3,2,1,0:T(8,128)(2,1)}), bf16[8,2,24,768]{3,2,1,0:T(8,128)(2,1)S(1)}, u32[]{:S(2)}, u32[]{:S(2)}) async-start(bf16[8,2,24,768]{3,2,1,0:T(8,128)(2,1)} %bitcast.98), calls=%async_computation.7 | async-start | bytes 1179648 | tf_op jit(solution)/shard_map/all_to_all | solution.py:149
  412.6 86.7 %reduce-scatter.6.cloned.1.call-start = ((), (), s32[]{:S(2)}) async-start(), calls=%async_computation.15 | async-start | bytes 5013504 | tf_op jit(solution)/shard_map/reduce_scatter | solution.py:232
  413.2 159.7 %reduce-scatter.4.cloned.1.call-start = ((), (), s32[]{:S(2)}) async-start(), calls=%async_computation.14 | async-start | bytes 5222400 | tf_op jit(solution)/shard_map/reduce_scatter | solution.py:232
  488.6 198.3 %reduce-scatter.8.cloned.1.call-start = ((), (), s32[]{:S(2)}) async-start(), calls=%async_computation.16 | async-start | bytes 10027008 | tf_op jit(solution)/shard_map/reduce_scatter | solution.py:232
  499.3 8.1 %collective-permute-start.2 = (bf16[48,3072]{1,0:T(8,128)(2,1)}, bf16[48,3072]{1,0:T(8,128)(2,1)S(1)}, u32[]{:S(2)}, u32[]{:S(2)}) collective-permute-start(bf16[48,3072]{1,0:T(8,128)(2,1)} %reduce-scatter.6.cloned.1.call-done), channel_id=1, source_target_pairs={{0,16},{16,0},{1,17},{17,1},{2,18},{18,2},{3,19},{19,3},{4,20},{20... | collective-permute-start | bytes 884744 | tf_op jit(solution)/shard_map/ppermute | solution.py:210
  508.4 66.0 %collective-permute-start.3 = (bf16[48,3072]{1,0:T(8,128)(2,1)S(1)}, bf16[48,3072]{1,0:T(8,128)(2,1)S(1)}, u32[]{:S(2)}, u32[]{:S(2)}) collective-permute-start(bf16[48,3072]{1,0:T(8,128)(2,1)S(1)} %add.254), channel_id=1, source_target_pairs={{0,8},{8,0},{1,9},{9,1},{2,10},{10,2},{3,11},{11,3},{4,12},{12,4},... | collective-permute-start | bytes 884744 | tf_op jit(solution)/shard_map/ppermute | solution.py:216
  572.9 7.9 %collective-permute-start = (bf16[48,3200]{1,0:T(8,128)(2,1)}, bf16[48,3200]{1,0:T(8,128)(2,1)S(1)}, u32[]{:S(2)}, u32[]{:S(2)}) collective-permute-start(bf16[48,3200]{1,0:T(8,128)(2,1)} %reduce-scatter.4.cloned.1.call-done), channel_id=1, source_target_pairs={{0,16},{16,0},{1,17},{17,1},{2,18},{18,2},{3,19},{19,3},{4,20},{20... | collective-permute-start | bytes 921608 | tf_op jit(solution)/shard_map/ppermute | solution.py:210
  580.9 107.5 %collective-permute-start.1 = (bf16[48,3200]{1,0:T(8,128)(2,1)S(1)}, bf16[48,3200]{1,0:T(8,128)(2,1)S(1)}, u32[]{:S(2)}, u32[]{:S(2)}) collective-permute-start(bf16[48,3200]{1,0:T(8,128)(2,1)S(1)} %add.253), channel_id=1, source_target_pairs={{0,8},{8,0},{1,9},{9,1},{2,10},{10,2},{3,11},{11,3},{4,12},{12,4},... | collective-permute-start | bytes 921608 | tf_op jit(solution)/shard_map/ppermute | solution.py:216
  686.9 15.0 %collective-permute-start.4 = (bf16[48,6144]{1,0:T(8,128)(2,1)}, bf16[48,6144]{1,0:T(8,128)(2,1)S(1)}, u32[]{:S(2)}, u32[]{:S(2)}) collective-permute-start(bf16[48,6144]{1,0:T(8,128)(2,1)} %reduce-scatter.8.cloned.1.call-done), channel_id=1, source_target_pairs={{0,16},{16,0},{1,17},{17,1},{2,18},{18,2},{3,19},{19,3},{4,20},{20... | collective-permute-start | bytes 1769480 | tf_op jit(solution)/shard_map/ppermute | solution.py:210
  702.0 2.5 collective-permute-start.5
  (117 other events, 496.9 us)
Sparse Core Ops, SparseCore 0:
  10.8 56.8 all-gather.3
  70.5 62.2 all-gather.5
  135.6 99.8 all-gather.7
  417.0 76.9 reduce-scatter.5
  497.8 75.0 reduce-scatter.3
  576.9 110.0 reduce-scatter.7
